TPU v7x, 256 devices: a whole 4x4x8 slice. The times are simulated.
256 devices in a mesh: trial: 4 (over z_lo), south: 4 (over y_lo, core), east: 4 (over x), down: 4 (over z_hi, y_hi).
Axes of the slice: x: 4, y: 4 (y_hi: 2, y_lo: 2; y = y_hi * 2 + y_lo), z: 8 (z_hi: 2, z_lo: 4; z = z_hi * 4 + z_lo), core: 2. Of those that a mesh axis runs over, the one named last changes fastest.
Arguments:
- tracer: float32 [64, 64, 512, 128], P(('trial', 'south'), 'east', 'down'), parts along dimension 0, may hold values from 0.5 to 2
- mobility: float32 [64, 64, 512, 128], P(('trial', 'south'), 'east', 'down'), parts along dimension 0, may hold values from 0.03 to 0.15
- source: float32 [64, 64, 512, 128], P(('trial', 'south'), 'east', 'down'), parts along dimension 0, may hold values from -0.2 to 0.2
Outputs:
- standardized: float32 [64, 64, 512, 128], P(('trial', 'south'), 'east', 'down'), parts along dimension 0
- tracer_end: float32 [64, 64, 512, 128], P(('trial', 'south'), 'east', 'down'), parts along dimension 0
There are 4 independent parts, one for each index of `trial`. A program takes and returns all parts, laid end to end along the dimension named above; each array names one. Nothing has to cross between parts.
All inputs are finite; a program needn't handle non-finite values.
Results may differ from a plain program's by a relative error of at most 0.00002.
Values sent between devices are 32-bit elements; how exact they have to be, the bound alone decides.
No kernel may reach another device: no remote copies, remote signals or barrier semaphores. Data moves between devices by JAX's collectives and lax.ppermute only.
A program may use at most 128 MiB of HBM per device.

v0:
```python
import jax
import jax.numpy as jnp
from jax import lax
from jax.sharding import PartitionSpec as P

STEPS = 3


def with_halo(value, sides, width):
    edges = {}
    for axis, dim in sides:
        peers, length = (lax.axis_size(axis), value.shape[dim])
        up = [(i, (i + 1) % peers) for i in range(peers)]
        last = lax.slice_in_dim(value, length - width, length, axis=dim)
        leading = lax.slice_in_dim(value, 0, width, axis=dim)
        edges[dim] = (
            lax.ppermute(last, axis, up),
            lax.ppermute(leading, axis, [(b, a) for a, b in up]),
        )
    done = []
    for _, dim in sides:
        low, high = edges[dim]
        around = [(width, width) if d in done else (0, 0) for d in range(value.ndim)]
        value = jnp.concatenate([jnp.pad(low, around), value, jnp.pad(high, around)], axis=dim)
        done.append(dim)
    return value


def copy_for_each(value, axis):
    copies = jnp.broadcast_to(value, (lax.axis_size(axis), *value.shape))
    return lax.all_to_all(copies, axis, split_axis=0, concat_axis=0, tiled=True)


def taken_together(value, axis):
    everything = copy_for_each(value, axis)
    return jnp.sum(everything, axis=0)


def packed_total(arrays, axis):
    ends = [0]
    for a in arrays:
        ends.append(ends[-1] + a.size)
    total = taken_together(jnp.concatenate([a.ravel() for a in arrays]), axis)
    return tuple((total[b:e].reshape(a.shape) for a, b, e in zip(arrays, ends, ends[1:])))


def strip_edges(values, dims):
    for dim in dims:
        values = lax.slice_in_dim(values, 1, values.shape[dim] - 1, axis=dim)
    return values


def neighbour(values, dim, start, dims):
    others = [other for other in dims if other != dim]
    values = strip_edges(values, others)
    return lax.slice_in_dim(values, start, start + values.shape[dim] - 2, axis=dim)


def one_step(padded, mobility, source):
    middle = strip_edges(padded, (0, 1, 2))
    lower = [neighbour(padded, dim, 0, (0, 1, 2)) for dim in (0, 1, 2)]
    upper = [neighbour(padded, dim, 2, (0, 1, 2)) for dim in (0, 1, 2)]
    spread = lower[0] + upper[0] + lower[1] + upper[1] + lower[2] + upper[2] - 6.0 * middle
    return middle + mobility * spread + source


def body(tracer, mobility, source):
    for step in range(STEPS):
        padded = with_halo(tracer, (("south", 0), ("east", 1), ("down", 2)), 1)
        tracer = one_step(padded, mobility, source)
    count = tracer.shape[2] * lax.axis_size("down")
    guess = 1.0
    moved = tracer - guess
    totals, squares = packed_total(
        (jnp.sum(moved, axis=2, keepdims=True), jnp.sum(moved * moved, axis=2, keepdims=True)),
        "down",
    )
    line_mean = guess + totals / count
    centred = tracer - line_mean
    line_variance = squares / count - totals / count * (totals / count)
    standardized = centred * lax.rsqrt(line_variance + 0.0001)
    return (standardized, tracer)


def solution(mesh):
    in_specs = (
        P(("trial", "south"), "east", "down", None),
        P(("trial", "south"), "east", "down", None),
        P(("trial", "south"), "east", "down", None),
    )
    out_specs = (
        P(("trial", "south"), "east", "down", None),
        P(("trial", "south"), "east", "down", None),
    )
    return jax.shard_map(body, mesh=mesh, in_specs=in_specs, out_specs=out_specs, check_vma=False)
```

profile of v0, /device:TPU:44, one launch (start us, length us, event | category | flops | bytes accessed | tf_op | source)
XLA Modules:
  0.0 152.9 jit_solution(15135447036923437315)
XLA Ops:
  0.6 0.0 copy-start.3
  0.6 1.8 %fusion.46 = (f32[1,16,128,128]{3,2,1,0:T(8,128)S(1)}, f32[1,16,128,128]{3,2,1,0:T(8,128)S(1)}) fusion(f32[4,16,128,128]{3,2,1,0:T(8,128)} %param.3), kind=kLoop, calls=%fused_computation.102 | loop fusion | bytes 4194304 | tf_op jit(solution)/shard_map/slice | solution.py:15
  2.5 0.1 collective-permute-start
  2.6 1.7 %collective-permute-start.1 = (f32[1,16,128,128]{3,2,1,0:T(8,128)S(1)}, f32[1,16,128,128]{3,2,1,0:T(8,128)S(1)}, u32[]{:S(2)}, u32[]{:S(2)}) collective-permute-start(f32[1,16,128,128]{3,2,1,0:T(8,128)S(1)} %get-tuple-element.21), channel_id=1, source_target_pairs={{16,0},{32,16},{48,32},{0,48},{17,1},{33,17},{49,33},{1,49},{18,2}... | collective-permute-start | bytes 3145736 | tf_op jit(solution)/shard_map/ppermute | solution.py:18
  4.3 0.0 copy-done.3
  4.4 1.3 collective-permute-start.2
  5.6 0.8 collective-permute-start.3
  6.5 2.4 %collective-permute-start.4 = (f32[4,16,1,128]{3,2,1,0:T(1,128)S(1)}, f32[4,16,1,128]{3,2,1,0:T(1,128)S(1)}, u32[]{:S(2)}, u32[]{:S(2)}) collective-permute-start(f32[4,16,1,128]{3,2,1,0:T(1,128)S(1)} %get-tuple-element.17), channel_id=1, source_target_pairs={{0,1},{1,2},{2,3},{3,0},{4,5},{5,6},{6,7},{7,4},{8,9},{9,10},{10,1... | collective-permute-start | bytes 98312 | tf_op jit(solution)/shard_map/ppermute | solution.py:17
  8.9 2.7 %collective-permute-done.2 = f32[4,1,128,128]{3,2,1,0:T(8,128)S(1)} collective-permute-done((f32[4,1,128,128]{3,2,1,0:T(8,128)S(1)}, f32[4,1,128,128]{3,2,1,0:T(8,128)S(1)}, u32[]{:S(2)}, u32[]{:S(2)}) %collective-permute-start.2) | collective-permute-done | bytes 262176 | tf_op jit(solution)/shard_map/ppermute | solution.py:17
  11.6 8.2 %collective-permute-start.5 = (f32[4,16,1,128]{3,2,1,0:T(1,128)S(1)}, f32[4,16,1,128]{3,2,1,0:T(1,128)S(1)}, u32[]{:S(2)}, u32[]{:S(2)}) collective-permute-start(f32[4,16,1,128]{3,2,1,0:T(1,128)S(1)} %get-tuple-element.18), channel_id=1, source_target_pairs={{1,0},{2,1},{3,2},{0,3},{5,4},{6,5},{7,6},{4,7},{9,8},{10,9},{11,1... | collective-permute-start | bytes 98312 | tf_op jit(solution)/shard_map/ppermute | solution.py:18
  19.8 0.0 collective-permute-done.3
  19.9 8.1 %collective-permute-done = f32[1,16,128,128]{3,2,1,0:T(8,128)S(1)} collective-permute-done((f32[1,16,128,128]{3,2,1,0:T(8,128)S(1)}, f32[1,16,128,128]{3,2,1,0:T(8,128)S(1)}, u32[]{:S(2)}, u32[]{:S(2)}) %collective-permute-start) | collective-permute-done | bytes 1048608 | tf_op jit(solution)/shard_map/ppermute | solution.py:17
  28.0 1.1 constant_dynamic-update-slice_fusion.2
  29.0 0.0 copy-start
  29.0 0.0 copy-start.1
  29.0 2.4 %constant_dynamic-update-slice_fusion.1 = f32[6,16,128,128]{3,2,1,0:T(8,128)} fusion(f32[6,16,128,128]{3,2,1,0:T(8,128)} %constant_dynamic-update-slice_fusion.2, f32[4,16,128,128]{3,2,1,0:T(8,128)S(1)} %copy-done.3), kind=kLoop, calls=%fused_computation.92 | loop fusion | bytes 8388608
  31.5 0.0 collective-permute-done.1
  31.5 1.1 constant_dynamic-update-slice_fusion
  32.5 0.0 collective-permute-done.4
  32.5 0.0 collective-permute-done.5
  32.5 0.6 copy-done
  33.1 1.3 copy-done.1
  34.4 13.9 %fusion.27 = f32[4,16,128,128]{3,2,1,0:T(8,128)} fusion(f32[4,16,128,128]{3,2,1,0:T(8,128)S(1)} %copy-done, f32[4,16,128,128]{3,2,1,0:T(8,128)} %param.3, f32[4,16,128,128]{3,2,1,0:T(8,128)S(1)} %copy-done.1, f32[4,16,1,128]{3,2,1,0:T(1,128)S(1)} %collective-permute-done.5, f32[6,1,128,128]{3,2,1,0:T(8,128)S(1)} %pad.39, ...), kind=kLoop, calls=%fused_computation.64 | loop fusion | flops 27262976 | bytes 26017792 | tf_op jit(solution)/shard_map/add | solution.py:64
  48.3 0.0 copy-start.2
  48.3 1.8 %fusion.42 = (f32[1,16,128,128]{3,2,1,0:T(8,128)S(1)}, f32[1,16,128,128]{3,2,1,0:T(8,128)S(1)}) fusion(f32[4,16,128,128]{3,2,1,0:T(8,128)} %fusion.27), kind=kLoop, calls=%fused_computation.98 | loop fusion | bytes 4194304 | tf_op jit(solution)/shard_map/slice | solution.py:14
  50.2 0.1 collective-permute-start.6
  50.3 1.7 %collective-permute-start.7 = (f32[1,16,128,128]{3,2,1,0:T(8,128)S(1)}, f32[1,16,128,128]{3,2,1,0:T(8,128)S(1)}, u32[]{:S(2)}, u32[]{:S(2)}) collective-permute-start(f32[1,16,128,128]{3,2,1,0:T(8,128)S(1)} %get-tuple-element.14), channel_id=1, source_target_pairs={{16,0},{32,16},{48,32},{0,48},{17,1},{33,17},{49,33},{1,49},{18,2}... | collective-permute-start | bytes 3145736 | tf_op jit(solution)/shard_map/ppermute | solution.py:18
  52.0 0.0 copy-done.2
  52.0 1.3 collective-permute-start.8
  53.3 0.8 collective-permute-start.9
  54.2 2.3 %collective-permute-start.10 = (f32[4,16,1,128]{3,2,1,0:T(1,128)S(1)}, f32[4,16,1,128]{3,2,1,0:T(1,128)S(1)}, u32[]{:S(2)}, u32[]{:S(2)}) collective-permute-start(f32[4,16,1,128]{3,2,1,0:T(1,128)S(1)} %get-tuple-element.11), channel_id=1, source_target_pairs={{0,1},{1,2},{2,3},{3,0},{4,5},{5,6},{6,7},{7,4},{8,9},{9,10},{10,1... | collective-permute-start | bytes 98312 | tf_op jit(solution)/shard_map/ppermute | solution.py:17
  56.5 2.7 %collective-permute-done.8 = f32[4,1,128,128]{3,2,1,0:T(8,128)S(1)} collective-permute-done((f32[4,1,128,128]{3,2,1,0:T(8,128)S(1)}, f32[4,1,128,128]{3,2,1,0:T(8,128)S(1)}, u32[]{:S(2)}, u32[]{:S(2)}) %collective-permute-start.8) | collective-permute-done | bytes 262176 | tf_op jit(solution)/shard_map/ppermute | solution.py:17
  59.2 7.7 %collective-permute-start.11 = (f32[4,16,1,128]{3,2,1,0:T(1,128)S(1)}, f32[4,16,1,128]{3,2,1,0:T(1,128)S(1)}, u32[]{:S(2)}, u32[]{:S(2)}) collective-permute-start(f32[4,16,1,128]{3,2,1,0:T(1,128)S(1)} %get-tuple-element.12), channel_id=1, source_target_pairs={{1,0},{2,1},{3,2},{0,3},{5,4},{6,5},{7,6},{4,7},{9,8},{10,9},{11,1... | collective-permute-start | bytes 98312 | tf_op jit(solution)/shard_map/ppermute | solution.py:18
  66.9 0.0 collective-permute-done.9
  67.0 7.0 %collective-permute-done.10 = f32[4,16,1,128]{3,2,1,0:T(1,128)S(1)} collective-permute-done((f32[4,16,1,128]{3,2,1,0:T(1,128)S(1)}, f32[4,16,1,128]{3,2,1,0:T(1,128)S(1)}, u32[]{:S(2)}, u32[]{:S(2)}) %collective-permute-start.10) | collective-permute-done | bytes 32800 | tf_op jit(solution)/shard_map/ppermute | solution.py:17
  74.0 3.3 %collective-permute-done.11 = f32[4,16,1,128]{3,2,1,0:T(1,128)S(1)} collective-permute-done((f32[4,16,1,128]{3,2,1,0:T(1,128)S(1)}, f32[4,16,1,128]{3,2,1,0:T(1,128)S(1)}, u32[]{:S(2)}, u32[]{:S(2)}) %collective-permute-start.11) | collective-permute-done | bytes 32800 | tf_op jit(solution)/shard_map/ppermute | solution.py:18
  77.3 0.0 collective-permute-done.6
  77.3 0.0 collective-permute-done.7
  77.3 7.6 %fusion.16 = f32[4,16,128,128]{3,2,1,0:T(8,128)S(1)} fusion(f32[4,16,128,128]{3,2,1,0:T(8,128)S(1)} %copy-done, f32[4,16,128,128]{3,2,1,0:T(8,128)S(1)} %copy-done.2, f32[4,16,128,128]{3,2,1,0:T(8,128)S(1)} %copy-done.1, f32[4,16,1,128]{3,2,1,0:T(1,128)S(1)} %collective-permute-done.11, f32[6,1,128,128]{3,2,1,0:T(8,128)S(1)} %pad.43, ...), kind=kLoop, calls=%fused_computation.35 | loop fusion | flops 35651584 | bytes 19726336 | tf_op jit(solution)/shard_map/add | solution.py:64
  85.0 0.2 fusion.40
  85.2 0.1 collective-permute-start.12
  85.3 1.7 %collective-permute-start.13 = (f32[1,16,128,128]{3,2,1,0:T(8,128)S(1)}, f32[1,16,128,128]{3,2,1,0:T(8,128)S(1)}, u32[]{:S(2)}, u32[]{:S(2)}) collective-permute-start(f32[1,16,128,128]{3,2,1,0:T(8,128)S(1)} %get-tuple-element.10), channel_id=1, source_target_pairs={{16,0},{32,16},{48,32},{0,48},{17,1},{33,17},{49,33},{1,49},{18,2}... | collective-permute-start | bytes 3145736 | tf_op jit(solution)/shard_map/ppermute | solution.py:18
  87.0 1.3 collective-permute-start.14
  88.3 0.8 collective-permute-start.15
  89.2 0.8 collective-permute-start.16
  90.0 6.2 %collective-permute-done.14 = f32[4,1,128,128]{3,2,1,0:T(8,128)S(1)} collective-permute-done((f32[4,1,128,128]{3,2,1,0:T(8,128)S(1)}, f32[4,1,128,128]{3,2,1,0:T(8,128)S(1)}, u32[]{:S(2)}, u32[]{:S(2)}) %collective-permute-start.14) | collective-permute-done | bytes 262176 | tf_op jit(solution)/shard_map/ppermute | solution.py:17
  96.1 5.3 %collective-permute-start.17 = (f32[4,16,1,128]{3,2,1,0:T(1,128)S(1)}, f32[4,16,1,128]{3,2,1,0:T(1,128)S(1)}, u32[]{:S(2)}, u32[]{:S(2)}) collective-permute-start(f32[4,16,1,128]{3,2,1,0:T(1,128)S(1)} %get-tuple-element.6), channel_id=1, source_target_pairs={{1,0},{2,1},{3,2},{0,3},{5,4},{6,5},{7,6},{4,7},{9,8},{10,9},{11,1... | collective-permute-start | bytes 98312 | tf_op jit(solution)/shard_map/ppermute | solution.py:18
  101.5 0.0 collective-permute-done.15
  101.5 10.3 %collective-permute-done.16 = f32[4,16,1,128]{3,2,1,0:T(1,128)S(1)} collective-permute-done((f32[4,16,1,128]{3,2,1,0:T(1,128)S(1)}, f32[4,16,1,128]{3,2,1,0:T(1,128)S(1)}, u32[]{:S(2)}, u32[]{:S(2)}) %collective-permute-start.16) | collective-permute-done | bytes 32800 | tf_op jit(solution)/shard_map/ppermute | solution.py:17
  111.8 0.3 collective-permute-done.17
  112.1 0.0 collective-permute-done.12
  112.1 0.0 collective-permute-done.13
  112.1 10.4 %add_reduce_fusion = (f32[4,16,128]{2,1,0:T(8,128)S(1)}, f32[4,16,128]{2,1,0:T(8,128)S(1)}, f32[4,16,128,128]{3,2,1,0:T(8,128)}) fusion(f32[4,16,128,128]{3,2,1,0:T(8,128)S(1)} %copy-done, f32[4,16,128,128]{3,2,1,0:T(8,128)S(1)} %fusion.16, f32[4,16,128,128]{3,2,1,0:T(8,128)S(1)} %copy-done.1, f32[4,16,1,128]{3,2,1,0:T(1,128)S(1)} %collective-permute-done.17, ...), kind=kLoop, calls=%fused_computation.83 | loop fusion | flops 39829504 | bytes 19791872 | tf_op jit(solution)/shard_map/reduce_sum | solution.py:75
  122.5 0.1 broadcast_in_dim.3
  122.6 24.8 %all_to_all.6 = f32[4,1,16384]{2,1,0:T(1,128)S(1)} all-to-all(f32[4,1,16384]{2,1,0:T(1,128)S(1)} %broadcast_in_dim.3), channel_id=1, replica_groups=mesh['trial'=4,'south'=4,'east'=4,'down'=4] {'down'}, dimensions={0} | all-to-all | bytes 524288 | tf_op jit(solution)/shard_map/all_to_all | solution.py:31
  147.4 0.2 reduce_sum.29
  147.6 5.2 %subtract_multiply_fusion = f32[4,16,128,128]{3,2,1,0:T(8,128)} fusion(f32[4,16,128,128]{3,2,1,0:T(8,128)} %get-tuple-element.4, f32[4,16,128]{2,1,0:T(8,128)S(1)} %bitcast.7, f32[4,16,128]{2,1,0:T(8,128)S(1)} %bitcast.6), kind=kLoop, calls=%fused_computation.81 | loop fusion | flops 2097152 | bytes 8454144 | tf_op jit(solution)/shard_map/mul | solution.py:81
  (14 shorter events, 0.4 us)
Async XLA Ops:
  0.6 3.7 %copy-start.3 = (f32[4,16,128,128]{3,2,1,0:T(8,128)S(1)}, f32[4,16,128,128]{3,2,1,0:T(8,128)}, u32[]{:S(2)}) copy-start(f32[4,16,128,128]{3,2,1,0:T(8,128)} %param.3) | copy-start | bytes 12582916
  2.5 25.5 %collective-permute-start = (f32[1,16,128,128]{3,2,1,0:T(8,128)S(1)}, f32[1,16,128,128]{3,2,1,0:T(8,128)S(1)}, u32[]{:S(2)}, u32[]{:S(2)}) collective-permute-start(f32[1,16,128,128]{3,2,1,0:T(8,128)S(1)} %get-tuple-element.22), channel_id=1, source_target_pairs={{0,16},{16,32},{32,48},{48,0},{1,17},{17,33},{33,49},{49,1},{2,18}... | collective-permute-start | bytes 3145736 | tf_op jit(solution)/shard_map/ppermute | solution.py:17
  2.6 28.9 %collective-permute-start.1 = (f32[1,16,128,128]{3,2,1,0:T(8,128)S(1)}, f32[1,16,128,128]{3,2,1,0:T(8,128)S(1)}, u32[]{:S(2)}, u32[]{:S(2)}) collective-permute-start(f32[1,16,128,128]{3,2,1,0:T(8,128)S(1)} %get-tuple-element.21), channel_id=1, source_target_pairs={{16,0},{32,16},{48,32},{0,48},{17,1},{33,17},{49,33},{1,49},{18,2}... | collective-permute-start | bytes 3145736 | tf_op jit(solution)/shard_map/ppermute | solution.py:18
  4.4 7.3 %collective-permute-start.2 = (f32[4,1,128,128]{3,2,1,0:T(8,128)S(1)}, f32[4,1,128,128]{3,2,1,0:T(8,128)S(1)}, u32[]{:S(2)}, u32[]{:S(2)}) collective-permute-start(f32[4,1,128,128]{3,2,1,0:T(8,128)S(1)} %get-tuple-element.19), channel_id=1, source_target_pairs={{0,4},{4,8},{8,12},{12,0},{1,5},{5,9},{9,13},{13,1},{2,6},{6,10},{... | collective-permute-start | bytes 786440 | tf_op jit(solution)/shard_map/ppermute | solution.py:17
  5.6 14.2 %collective-permute-start.3 = (f32[4,1,128,128]{3,2,1,0:T(8,128)S(1)}, f32[4,1,128,128]{3,2,1,0:T(8,128)S(1)}, u32[]{:S(2)}, u32[]{:S(2)}) collective-permute-start(f32[4,1,128,128]{3,2,1,0:T(8,128)S(1)} %get-tuple-element.20), channel_id=1, source_target_pairs={{4,0},{8,4},{12,8},{0,12},{5,1},{9,5},{13,9},{1,13},{6,2},{10,6},{... | collective-permute-start | bytes 786440 | tf_op jit(solution)/shard_map/ppermute | solution.py:18
  6.5 26.0 %collective-permute-start.4 = (f32[4,16,1,128]{3,2,1,0:T(1,128)S(1)}, f32[4,16,1,128]{3,2,1,0:T(1,128)S(1)}, u32[]{:S(2)}, u32[]{:S(2)}) collective-permute-start(f32[4,16,1,128]{3,2,1,0:T(1,128)S(1)} %get-tuple-element.17), channel_id=1, source_target_pairs={{0,1},{1,2},{2,3},{3,0},{4,5},{5,6},{6,7},{7,4},{8,9},{9,10},{10,1... | collective-permute-start | bytes 98312 | tf_op jit(solution)/shard_map/ppermute | solution.py:17
  11.6 20.9 %collective-permute-start.5 = (f32[4,16,1,128]{3,2,1,0:T(1,128)S(1)}, f32[4,16,1,128]{3,2,1,0:T(1,128)S(1)}, u32[]{:S(2)}, u32[]{:S(2)}) collective-permute-start(f32[4,16,1,128]{3,2,1,0:T(1,128)S(1)} %get-tuple-element.18), channel_id=1, source_target_pairs={{1,0},{2,1},{3,2},{0,3},{5,4},{6,5},{7,6},{4,7},{9,8},{10,9},{11,1... | collective-permute-start | bytes 98312 | tf_op jit(solution)/shard_map/ppermute | solution.py:18
  29.0 4.1 %copy-start = (f32[4,16,128,128]{3,2,1,0:T(8,128)S(1)}, f32[4,16,128,128]{3,2,1,0:T(8,128)}, u32[]{:S(2)}) copy-start(f32[4,16,128,128]{3,2,1,0:T(8,128)} %param.5) | copy-start | bytes 12582916
  29.0 5.4 %copy-start.1 = (f32[4,16,128,128]{3,2,1,0:T(8,128)S(1)}, f32[4,16,128,128]{3,2,1,0:T(8,128)}, u32[]{:S(2)}) copy-start(f32[4,16,128,128]{3,2,1,0:T(8,128)} %param.4) | copy-start | bytes 12582916
  48.3 3.7 %copy-start.2 = (f32[4,16,128,128]{3,2,1,0:T(8,128)S(1)}, f32[4,16,128,128]{3,2,1,0:T(8,128)}, u32[]{:S(2)}) copy-start(f32[4,16,128,128]{3,2,1,0:T(8,128)} %fusion.27) | copy-start | bytes 12582916
  50.2 27.1 %collective-permute-start.6 = (f32[1,16,128,128]{3,2,1,0:T(8,128)S(1)}, f32[1,16,128,128]{3,2,1,0:T(8,128)S(1)}, u32[]{:S(2)}, u32[]{:S(2)}) collective-permute-start(f32[1,16,128,128]{3,2,1,0:T(8,128)S(1)} %get-tuple-element.13), channel_id=1, source_target_pairs={{0,16},{16,32},{32,48},{48,0},{1,17},{17,33},{33,49},{49,1},{2,18}... | collective-permute-start | bytes 3145736 | tf_op jit(solution)/shard_map/ppermute | solution.py:17
  50.3 27.0 %collective-permute-start.7 = (f32[1,16,128,128]{3,2,1,0:T(8,128)S(1)}, f32[1,16,128,128]{3,2,1,0:T(8,128)S(1)}, u32[]{:S(2)}, u32[]{:S(2)}) collective-permute-start(f32[1,16,128,128]{3,2,1,0:T(8,128)S(1)} %get-tuple-element.14), channel_id=1, source_target_pairs={{16,0},{32,16},{48,32},{0,48},{17,1},{33,17},{49,33},{1,49},{18,2}... | collective-permute-start | bytes 3145736 | tf_op jit(solution)/shard_map/ppermute | solution.py:18
  52.0 7.1 %collective-permute-start.8 = (f32[4,1,128,128]{3,2,1,0:T(8,128)S(1)}, f32[4,1,128,128]{3,2,1,0:T(8,128)S(1)}, u32[]{:S(2)}, u32[]{:S(2)}) collective-permute-start(f32[4,1,128,128]{3,2,1,0:T(8,128)S(1)} %get-tuple-element.15), channel_id=1, source_target_pairs={{0,4},{4,8},{8,12},{12,0},{1,5},{5,9},{9,13},{13,1},{2,6},{6,10},{... | collective-permute-start | bytes 786440 | tf_op jit(solution)/shard_map/ppermute | solution.py:17
  53.3 13.6 %collective-permute-start.9 = (f32[4,1,128,128]{3,2,1,0:T(8,128)S(1)}, f32[4,1,128,128]{3,2,1,0:T(8,128)S(1)}, u32[]{:S(2)}, u32[]{:S(2)}) collective-permute-start(f32[4,1,128,128]{3,2,1,0:T(8,128)S(1)} %get-tuple-element.16), channel_id=1, source_target_pairs={{4,0},{8,4},{12,8},{0,12},{5,1},{9,5},{13,9},{1,13},{6,2},{10,6},{... | collective-permute-start | bytes 786440 | tf_op jit(solution)/shard_map/ppermute | solution.py:18
  54.2 19.8 %collective-permute-start.10 = (f32[4,16,1,128]{3,2,1,0:T(1,128)S(1)}, f32[4,16,1,128]{3,2,1,0:T(1,128)S(1)}, u32[]{:S(2)}, u32[]{:S(2)}) collective-permute-start(f32[4,16,1,128]{3,2,1,0:T(1,128)S(1)} %get-tuple-element.11), channel_id=1, source_target_pairs={{0,1},{1,2},{2,3},{3,0},{4,5},{5,6},{6,7},{7,4},{8,9},{9,10},{10,1... | collective-permute-start | bytes 98312 | tf_op jit(solution)/shard_map/ppermute | solution.py:17
  59.2 18.1 %collective-permute-start.11 = (f32[4,16,1,128]{3,2,1,0:T(1,128)S(1)}, f32[4,16,1,128]{3,2,1,0:T(1,128)S(1)}, u32[]{:S(2)}, u32[]{:S(2)}) collective-permute-start(f32[4,16,1,128]{3,2,1,0:T(1,128)S(1)} %get-tuple-element.12), channel_id=1, source_target_pairs={{1,0},{2,1},{3,2},{0,3},{5,4},{6,5},{7,6},{4,7},{9,8},{10,9},{11,1... | collective-permute-start | bytes 98312 | tf_op jit(solution)/shard_map/ppermute | solution.py:18
  85.2 26.9 %collective-permute-start.12 = (f32[1,16,128,128]{3,2,1,0:T(8,128)S(1)}, f32[1,16,128,128]{3,2,1,0:T(8,128)S(1)}, u32[]{:S(2)}, u32[]{:S(2)}) collective-permute-start(f32[1,16,128,128]{3,2,1,0:T(8,128)S(1)} %get-tuple-element.9), channel_id=1, source_target_pairs={{0,16},{16,32},{32,48},{48,0},{1,17},{17,33},{33,49},{49,1},{2,18}... | collective-permute-start | bytes 3145736 | tf_op jit(solution)/shard_map/ppermute | solution.py:17
  85.3 26.8 %collective-permute-start.13 = (f32[1,16,128,128]{3,2,1,0:T(8,128)S(1)}, f32[1,16,128,128]{3,2,1,0:T(8,128)S(1)}, u32[]{:S(2)}, u32[]{:S(2)}) collective-permute-start(f32[1,16,128,128]{3,2,1,0:T(8,128)S(1)} %get-tuple-element.10), channel_id=1, source_target_pairs={{16,0},{32,16},{48,32},{0,48},{17,1},{33,17},{49,33},{1,49},{18,2}... | collective-permute-start | bytes 3145736 | tf_op jit(solution)/shard_map/ppermute | solution.py:18
  87.0 9.1 %collective-permute-start.14 = (f32[4,1,128,128]{3,2,1,0:T(8,128)S(1)}, f32[4,1,128,128]{3,2,1,0:T(8,128)S(1)}, u32[]{:S(2)}, u32[]{:S(2)}) collective-permute-start(f32[4,1,128,128]{3,2,1,0:T(8,128)S(1)} %get-tuple-element.7), channel_id=1, source_target_pairs={{0,4},{4,8},{8,12},{12,0},{1,5},{5,9},{9,13},{13,1},{2,6},{6,10},{... | collective-permute-start | bytes 786440 | tf_op jit(solution)/shard_map/ppermute | solution.py:17
  88.3 13.2 %collective-permute-start.15 = (f32[4,1,128,128]{3,2,1,0:T(8,128)S(1)}, f32[4,1,128,128]{3,2,1,0:T(8,128)S(1)}, u32[]{:S(2)}, u32[]{:S(2)}) collective-permute-start(f32[4,1,128,128]{3,2,1,0:T(8,128)S(1)} %get-tuple-element.8), channel_id=1, source_target_pairs={{4,0},{8,4},{12,8},{0,12},{5,1},{9,5},{13,9},{1,13},{6,2},{10,6},{... | collective-permute-start | bytes 786440 | tf_op jit(solution)/shard_map/ppermute | solution.py:18
  89.2 22.7 %collective-permute-start.16 = (f32[4,16,1,128]{3,2,1,0:T(1,128)S(1)}, f32[4,16,1,128]{3,2,1,0:T(1,128)S(1)}, u32[]{:S(2)}, u32[]{:S(2)}) collective-permute-start(f32[4,16,1,128]{3,2,1,0:T(1,128)S(1)} %get-tuple-element.5), channel_id=1, source_target_pairs={{0,1},{1,2},{2,3},{3,0},{4,5},{5,6},{6,7},{7,4},{8,9},{9,10},{10,1... | collective-permute-start | bytes 98312 | tf_op jit(solution)/shard_map/ppermute | solution.py:17
  96.1 16.0 %collective-permute-start.17 = (f32[4,16,1,128]{3,2,1,0:T(1,128)S(1)}, f32[4,16,1,128]{3,2,1,0:T(1,128)S(1)}, u32[]{:S(2)}, u32[]{:S(2)}) collective-permute-start(f32[4,16,1,128]{3,2,1,0:T(1,128)S(1)} %get-tuple-element.6), channel_id=1, source_target_pairs={{1,0},{2,1},{3,2},{0,3},{5,4},{6,5},{7,6},{4,7},{9,8},{10,9},{11,1... | collective-permute-start | bytes 98312 | tf_op jit(solution)/shard_map/ppermute | solution.py:18
where the time goes:
time: 153 us
  waiting for transfers between devices  40.7 us (27%)
  starting transfers between devices  38.3 us (25%)
  other arithmetic  37.4 us (24%)
  blocking collectives  24.8 us (16%)
  local copies, waits for them, and re-layouts  10.8 us (7%)
    ppermute x9, waiting for transfers between devices, with_halo(): lax.ppermute(last, axis, up)  37.1 us
    ppermute x9, starting transfers between devices, with_halo(): lax.ppermute(leading, axis, [(b, a) for a, b in up])  28.9 us
    all_to_all x1, blocking collectives, copy_for_each(): return lax.all_to_all(copies, axis, split_axis=0, concat_axis=0, tiled=True)  24.8 us
    add x2, other arithmetic, one_step(): return middle + mobility * spread + source  21.6 us
    reduce_sum x1, other arithmetic, body(): jnp.sum(moved, axis=2, keepdims=True)  10.4 us
    ppermute x9, starting transfers between devices, with_halo(): lax.ppermute(last, axis, up)  9.46 us
    unnamed x10, local copies, waits for them, and re-layouts  5.36 us
    mul x1, other arithmetic, body(): standardized = centred * lax.rsqrt(line_variance + 0.0001)  5.23 us
  transfers between devices with their start and end apart: 18, of which 8 were waited for; matrix products, arithmetic and copies ran while one was open for 3% of the time, Pallas kernels for 0%

commit v1 on v0

v1 whole, which is shorter than its diff:
```python
import functools

import jax
import jax.numpy as jnp
from jax import lax
from jax.experimental import pallas as pl
from jax.experimental.pallas import tpu as pltpu
from jax.sharding import PartitionSpec as P

STEPS = 3
VMEM_LIMIT = 16 * 1024 * 1024
PARAMS = pltpu.CompilerParams(vmem_limit_bytes=VMEM_LIMIT)


def f32(*shape):
    return jax.ShapeDtypeStruct(shape, jnp.float32)


def rows_of(refs):
    if len(refs) == 1:
        return [refs[0].at[r] for r in range(refs[0].shape[0])]
    first, middle, last = refs
    return [first] + [middle.at[r] for r in range(middle.shape[0])] + [last]


def partial_kernel(n, *refs):
    tracer = rows_of(refs[:n])
    mobility, source, low_x, high_x = refs[n : n + 4]
    out = rows_of(refs[n + 4 :])
    width, depth, _ = tracer[0].shape
    z = lax.broadcasted_iota(jnp.int32, tracer[0].shape[1:], 0)

    def cell(r, x, before, after):
        here = tracer[r][x]
        spread = before + after
        if r > 0:
            spread += tracer[r - 1][x]
        if r < len(tracer) - 1:
            spread += tracer[r + 1][x]
        spread += jnp.where(z == 0, 0.0, pltpu.roll(here, 1, 0))
        spread += jnp.where(z == depth - 1, 0.0, pltpu.roll(here, depth - 1, 0))
        out[r][x] = here + mobility[r, x] * (spread - 6.0 * here) + source[r, x]

    for r in range(len(tracer)):
        cell(r, 0, low_x[r], tracer[r][1])

        @pl.loop(1, width - 1)
        def _(x, r=r):
            cell(r, x, tracer[r][x - 1], tracer[r][x + 1])

        cell(r, width - 1, tracer[r][width - 2], high_x[r])


def add_lines(row, mobility, low_z, high_z, r, x):
    depth = row.shape[1]
    row[x, 0:1] += mobility[r, x, 0:1] * low_z[r, pl.ds(x, 1)]
    row[x, depth - 1 : depth] += mobility[r, x, depth - 1 : depth] * high_z[r, pl.ds(x, 1)]


def finish_kernel(first_in, middle_in, last_in, mobility, low_y, high_y, low_z, high_z, first, middle, last, *edges):
    first_x, last_x, first_z, last_z = edges
    width, depth, _ = first.shape
    rows = rows_of((first, middle, last))
    top = len(rows) - 1

    @pl.loop(0, width)
    def _(x):
        first[x] = first_in[x] + mobility[0, x] * low_y[x]
        last[x] = last_in[x] + mobility[top, x] * high_y[x]

    for r, row in enumerate(rows):

        @pl.loop(0, width)
        def _(x, r=r, row=row):
            add_lines(row, mobility, low_z, high_z, r, x)
            first_z[r, pl.ds(x, 1)] = row[x, 0:1]
            last_z[r, pl.ds(x, 1)] = row[x, depth - 1 : depth]

        first_x[r] = row[0]
        last_x[r] = row[width - 1]


def last_kernel(first_in, middle_in, last_in, mobility, low_y, high_y, low_z, high_z, tracer, means, spreads):
    rows_in = rows_of((first_in, middle_in, last_in))
    top = len(rows_in) - 1
    width, depth, _ = first_in.shape
    z = lax.broadcasted_iota(jnp.int32, (depth, first_in.shape[2]), 0)

    for r, row in enumerate(rows_in):

        @pl.loop(0, width)
        def _(x, r=r, row=row):
            value = row[x]
            if r == 0:
                value += mobility[r, x] * low_y[x]
            if r == top:
                value += mobility[r, x] * high_y[x]
            lines = jnp.where(z == 0, low_z[r, pl.ds(x, 1)], 0.0)
            lines += jnp.where(z == depth - 1, high_z[r, pl.ds(x, 1)], 0.0)
            value += mobility[r, x] * lines
            tracer[r, x] = value
            mean = jnp.sum(value, axis=0, keepdims=True) * (1.0 / depth)
            off = value - mean
            means[r, pl.ds(x, 1)] = mean
            spreads[r, pl.ds(x, 1)] = jnp.sum(off * off, axis=0, keepdims=True)


def store_kernel(tracer, out, sem):
    copy = pltpu.make_async_copy(tracer, out, sem)
    copy.start()
    copy.wait()


def scale_kernel(tracer, *refs):
    *parts, out, held, sems = refs
    means, spreads = (parts[0::2], parts[1::2])
    count, width, depth, _ = tracer.shape
    copies = []
    for r in range(count):
        mean = sum(part[r] for part in means) * (1.0 / len(means))
        away = sum((part[r] - mean) * (part[r] - mean) for part in means)
        total = sum(part[r] for part in spreads) + depth * away
        scale = lax.rsqrt(total * (1.0 / (depth * len(means))) + 0.0001)
        for x in range(width):
            held[r, x] = (tracer[r, x] - mean[x : x + 1]) * scale[x : x + 1]
        copies.append(pltpu.make_async_copy(held.at[r], out.at[r], sems.at[r]))
        copies[-1].start()
    for copy in copies:
        copy.wait()


def body(tracer, mobility, source):
    count, width, depth, levels = tracer.shape
    row, middle = (f32(width, depth, levels), f32(count - 2, width, depth, levels))
    plane, line = (f32(count, depth, levels), f32(count, width, levels))

    def swap(leading, last, axis):
        peers = lax.axis_size(axis)
        up = [(i, (i + 1) % peers) for i in range(peers)]
        low = lax.ppermute(last, axis, up)
        high = lax.ppermute(leading, axis, [(b, a) for a, b in up])
        return (low, high)

    rows = (tracer,)
    ends = (tracer[0], tracer[-1])
    edges = (tracer[:, 0], tracer[:, -1], tracer[:, :, 0], tracer[:, :, -1])
    for step in range(STEPS):
        along_y = swap(*ends, "south")
        along_x = swap(*edges[:2], "east")
        along_z = swap(*edges[2:], "down")
        partial = pl.pallas_call(
            functools.partial(partial_kernel, len(rows)),
            out_shape=(row, middle, row),
            compiler_params=PARAMS,
            name="partial",
        )(*rows, mobility, source, *along_x)
        inputs = (*partial, mobility, *along_y, *along_z)
        if step < STEPS - 1:
            first, inner, last, *edges = pl.pallas_call(
                finish_kernel,
                out_shape=(row, middle, row, plane, plane, line, line),
                input_output_aliases={1: 1},
                compiler_params=PARAMS,
                name="finish",
            )(*inputs)
            rows = (first, inner, last)
            ends = (first, last)
    end, mean, spread = pl.pallas_call(
        last_kernel,
        out_shape=(f32(count, width, depth, levels), line, line),
        compiler_params=PARAMS,
        name="last",
    )(*inputs)
    peers = lax.axis_size("down")
    sums = jnp.stack([mean, spread])
    parts = [mean, spread]
    for away in range(peers - 1, 0, -1):
        other = lax.ppermute(sums, "down", [(i, i ^ away) for i in range(peers)])
        parts += [other[0], other[1]]
    stored = pl.pallas_call(
        store_kernel,
        out_shape=f32(count, width, depth, levels),
        out_specs=pl.BlockSpec(memory_space=pl.ANY),
        scratch_shapes=[pltpu.SemaphoreType.DMA],
        compiler_params=PARAMS,
        name="store",
    )(end)
    standardized = pl.pallas_call(
        scale_kernel,
        out_shape=f32(count, width, depth, levels),
        out_specs=pl.BlockSpec(memory_space=pl.ANY),
        scratch_shapes=[pltpu.VMEM((count, width, depth, levels), jnp.float32), pltpu.SemaphoreType.DMA((count,))],
        compiler_params=PARAMS,
        name="scale",
    )(end, *parts)
    return (standardized, stored)


def solution(mesh):
    spec = P(("trial", "south"), "east", "down", None)
    return jax.shard_map(body, mesh=mesh, in_specs=(spec,) * 3, out_specs=(spec,) * 2, check_vma=False)
```

time: 153 us -> 115 us (0.75)
  the two profiles are of different devices: /device:TPU:44 before, /device:TPU:16 now
where the time goes in v1:
time: 115 us
  starting transfers between devices  47.5 us (41%)
  waiting for transfers between devices  41.4 us (36%)
  Pallas kernels  16.4 us (14%)
  local copies, waits for them, and re-layouts  8.46 us (7%)
    ppermute x9, waiting for transfers between devices, swap(): low = lax.ppermute(last, axis, up)  32.2 us
    ppermute x9, starting transfers between devices, swap(): low = lax.ppermute(last, axis, up)  25.5 us
    ppermute x9, starting transfers between devices, swap(): high = lax.ppermute(leading, axis, [(b, a) for a, b in up])  11.3 us
    ppermute x3, starting transfers between devices, body(): other = lax.ppermute(sums, 'down', [(i, i ^ away) for i in range(peers)])  10.7 us
    ppermute x3, waiting for transfers between devices, body(): other = lax.ppermute(sums, 'down', [(i, i ^ away) for i in range(peers)])  9.12 us
    pallas_call x3, Pallas kernels, body(): pl.pallas_call(functools.partial(partial_kernel, len(rows)), out_shape=(r...  6.74 us
    unnamed x8, local copies, waits for them, and re-layouts  4.39 us
    pallas_call x1, Pallas kernels, body(): pl.pallas_call(last_kernel, out_shape=(f32(count, width, depth, levels),...  3.37 us
  transfers between devices with their start and end apart: 21, of which 8 were waited for; matrix products, arithmetic and copies ran while one was open for 2% of the time, Pallas kernels for 8%

profile of v1, /device:TPU:16, one launch (start us, length us, event | category | flops | bytes accessed | tf_op | source)
XLA Modules:
  0.0 114.6 jit_solution(11162836624301736518)
XLA Ops:
  0.6 0.0 copy-start
  0.6 1.9 %slice_bitcast_fusion = (f32[16,128,128]{2,1,0:T(8,128)S(1)}, f32[16,128,128]{2,1,0:T(8,128)S(1)}) fusion(f32[4,16,128,128]{3,2,1,0:T(8,128)} %refs_0_.1), kind=kLoop, calls=%fused_computation | loop fusion | bytes 4194304 | tf_op jit(solution)/shard_map/squeeze | solution.py:145
  2.6 0.8 collective-permute-start.3
  3.4 0.0 collective-permute-start.2
  3.4 1.1 slice_bitcast_fusion.2
  4.4 2.8 %collective-permute-start.1 = (f32[4,128,128]{2,1,0:T(8,128)S(1)}, f32[4,128,128]{2,1,0:T(8,128)S(1)}, u32[]{:S(2)}, u32[]{:S(2)}) collective-permute-start(f32[4,128,128]{2,1,0:T(8,128)S(1)} %get-tuple-element.58), channel_id=1, source_target_pairs={{4,0},{8,4},{12,8},{0,12},{5,1},{9,5},{13,9},{1,13},{6,2},{10,6},{... | collective-permute-start | bytes 786440 | tf_op jit(solution)/shard_map/ppermute | solution.py:141
  7.3 0.0 collective-permute-start
  7.3 1.1 fusion
  8.3 7.3 %collective-permute-start.4 = (f32[4,16,128]{2,1,0:T(8,128)S(1)}, f32[4,16,128]{2,1,0:T(8,128)S(1)}, u32[]{:S(2)}, u32[]{:S(2)}) collective-permute-start(f32[4,16,128]{2,1,0:T(8,128)S(1)} %bitcast.35), channel_id=1, source_target_pairs={{0,1},{1,2},{2,3},{3,0},{4,5},{5,6},{6,7},{7,4},{8,9},{9,10},{10,1... | collective-permute-start | bytes 98312 | tf_op jit(solution)/shard_map/ppermute | solution.py:140
  15.7 0.0 collective-permute-done.1.refs_4_
  15.7 0.0 collective-permute-start.5
  15.7 1.6 %collective-permute-done.refs_3_ = f32[4,128,128]{2,1,0:T(8,128)S(1)} collective-permute-done((f32[4,128,128]{2,1,0:T(8,128)S(1)}, f32[4,128,128]{2,1,0:T(8,128)S(1)}, u32[]{:S(2)}, u32[]{:S(2)}) %collective-permute-start) | collective-permute-done | bytes 262176 | tf_op jit(solution)/shard_map/ppermute | solution.py:140
  17.3 0.0 copy-done
  17.3 0.0 copy-start.1
  17.3 2.2 %copy-done.1 = f32[4,16,128,128]{3,2,1,0:T(8,128)S(1)} copy-done((f32[4,16,128,128]{3,2,1,0:T(8,128)S(1)}, f32[4,16,128,128]{3,2,1,0:T(8,128)}, u32[]{:S(2)}) %copy-start.1) | copy-done | bytes 4194328
  19.5 0.0 copy-start.3
  19.5 2.2 %copy-done.3 = f32[4,16,128,128]{3,2,1,0:T(8,128)S(1)} copy-done((f32[4,16,128,128]{3,2,1,0:T(8,128)S(1)}, f32[4,16,128,128]{3,2,1,0:T(8,128)}, u32[]{:S(2)}) %copy-start.3) | copy-done | bytes 4194328
  21.6 2.3 %partial.3 = (f32[16,128,128]{2,1,0:T(8,128)S(1)}, f32[2,16,128,128]{3,2,1,0:T(8,128)S(1)}, f32[16,128,128]{2,1,0:T(8,128)S(1)}) custom-call(f32[4,16,128,128]{3,2,1,0:T(8,128)S(1)} %copy-done.3, f32[4,16,128,128]{3,2,1,0:T(8,128)S(1)} %copy-done, f32[4,16,128,128]{3,2,1,0:T(8,128)S(1)} %copy-done.1, f32[4,128,128]{2,1,0:T(8,128)S(1)} %collective-permute-done.refs_3_, ...), custom_call_target="tpu_custom_call" | custom-call | tf_op jit(solution)/shard_map/partial/pallas_call | solution.py:151
  23.9 6.0 %collective-permute-done.4.low_z = f32[4,16,128]{2,1,0:T(8,128)S(1)} collective-permute-done((f32[4,16,128]{2,1,0:T(8,128)S(1)}, f32[4,16,128]{2,1,0:T(8,128)S(1)}, u32[]{:S(2)}, u32[]{:S(2)}) %collective-permute-start.4) | collective-permute-done | bytes 32800 | tf_op jit(solution)/shard_map/ppermute | solution.py:140
  29.9 0.0 collective-permute-done.5.high_z
  29.9 0.0 collective-permute-done.3.high_y
  29.9 0.0 collective-permute-done.2.low_y
  29.9 0.0 copy-start.2
  29.9 1.1 finish.2
  31.0 0.2 collective-permute-start.9
  31.2 0.4 collective-permute-start.8
  31.6 1.1 collective-permute-start.6
  32.7 2.2 %collective-permute-start.7 = (f32[4,128,128]{2,1,0:T(8,128)S(1)}, f32[4,128,128]{2,1,0:T(8,128)S(1)}, u32[]{:S(2)}, u32[]{:S(2)}) collective-permute-start(f32[4,128,128]{2,1,0:T(8,128)S(1)} %get-tuple-element.35), channel_id=1, source_target_pairs={{4,0},{8,4},{12,8},{0,12},{5,1},{9,5},{13,9},{1,13},{6,2},{10,6},{... | collective-permute-start | bytes 786440 | tf_op jit(solution)/shard_map/ppermute | solution.py:141
  34.8 8.8 %collective-permute-start.10 = (f32[4,16,128]{2,1,0:T(8,128)S(1)}, f32[4,16,128]{2,1,0:T(8,128)S(1)}, u32[]{:S(2)}, u32[]{:S(2)}) collective-permute-start(f32[4,16,128]{2,1,0:T(8,128)S(1)} %get-tuple-element.39), channel_id=1, source_target_pairs={{0,1},{1,2},{2,3},{3,0},{4,5},{5,6},{6,7},{7,4},{8,9},{9,10},{10,1... | collective-permute-start | bytes 98312 | tf_op jit(solution)/shard_map/ppermute | solution.py:140
  43.7 0.0 collective-permute-done.6.refs_5_
  43.7 0.1 collective-permute-start.11
  43.8 0.0 collective-permute-done.7.refs_6_
  43.8 0.0 copy-done.2
  43.8 2.2 %partial.4 = (f32[16,128,128]{2,1,0:T(8,128)S(1)}, f32[2,16,128,128]{3,2,1,0:T(8,128)S(1)}, f32[16,128,128]{2,1,0:T(8,128)S(1)}) custom-call(f32[16,128,128]{2,1,0:T(8,128)S(1)} %get-tuple-element.31.refs_0_, f32[2,16,128,128]{3,2,1,0:T(8,128)S(1)} %get-tuple-element.32.refs_1_, f32[16,128,128]{2,1,0:T(8,128)S(1)} %get-tuple-element.33.refs_2_, ...), custom_call_target="tpu_custom_call" | custom-call | tf_op jit(solution)/shard_map/partial/pallas_call | solution.py:151
  46.1 11.5 %collective-permute-done.10.low_z = f32[4,16,128]{2,1,0:T(8,128)S(1)} collective-permute-done((f32[4,16,128]{2,1,0:T(8,128)S(1)}, f32[4,16,128]{2,1,0:T(8,128)S(1)}, u32[]{:S(2)}, u32[]{:S(2)}) %collective-permute-start.10) | collective-permute-done | bytes 32800 | tf_op jit(solution)/shard_map/ppermute | solution.py:140
  57.5 0.0 collective-permute-done.11.high_z
  57.5 0.0 collective-permute-done.9.high_y
  57.5 0.0 collective-permute-done.8.low_y
  57.5 1.1 finish.3
  58.6 2.9 %collective-permute-start.15 = (f32[16,128,128]{2,1,0:T(8,128)S(1)}, f32[16,128,128]{2,1,0:T(8,128)S(1)}, u32[]{:S(2)}, u32[]{:S(2)}) collective-permute-start(f32[16,128,128]{2,1,0:T(8,128)S(1)} %get-tuple-element.41.refs_0_), channel_id=1, source_target_pairs={{16,0},{32,16},{48,32},{0,48},{17,1},{33,17},{49,33},{1,49},{18,2}... | collective-permute-start | bytes 3145736 | tf_op jit(solution)/shard_map/ppermute | solution.py:141
  61.5 0.0 collective-permute-start.14
  61.5 1.5 %collective-permute-start.12 = (f32[4,128,128]{2,1,0:T(8,128)S(1)}, f32[4,128,128]{2,1,0:T(8,128)S(1)}, u32[]{:S(2)}, u32[]{:S(2)}) collective-permute-start(f32[4,128,128]{2,1,0:T(8,128)S(1)} %get-tuple-element.44), channel_id=1, source_target_pairs={{0,4},{4,8},{8,12},{12,0},{1,5},{5,9},{9,13},{13,1},{2,6},{6,10},{... | collective-permute-start | bytes 786440 | tf_op jit(solution)/shard_map/ppermute | solution.py:140
  63.0 1.7 %collective-permute-start.13 = (f32[4,128,128]{2,1,0:T(8,128)S(1)}, f32[4,128,128]{2,1,0:T(8,128)S(1)}, u32[]{:S(2)}, u32[]{:S(2)}) collective-permute-start(f32[4,128,128]{2,1,0:T(8,128)S(1)} %get-tuple-element.45), channel_id=1, source_target_pairs={{4,0},{8,4},{12,8},{0,12},{5,1},{9,5},{13,9},{1,13},{6,2},{10,6},{... | collective-permute-start | bytes 786440 | tf_op jit(solution)/shard_map/ppermute | solution.py:141
  64.7 6.4 %collective-permute-start.16 = (f32[4,16,128]{2,1,0:T(8,128)S(1)}, f32[4,16,128]{2,1,0:T(8,128)S(1)}, u32[]{:S(2)}, u32[]{:S(2)}) collective-permute-start(f32[4,16,128]{2,1,0:T(8,128)S(1)} %get-tuple-element.49), channel_id=1, source_target_pairs={{0,1},{1,2},{2,3},{3,0},{4,5},{5,6},{6,7},{7,4},{8,9},{9,10},{10,1... | collective-permute-start | bytes 98312 | tf_op jit(solution)/shard_map/ppermute | solution.py:140
  71.1 0.5 collective-permute-done.12.refs_5_
  71.6 0.5 collective-permute-start.17
  72.1 0.0 collective-permute-done.13.refs_6_
  72.2 2.2 %partial.5 = (f32[16,128,128]{2,1,0:T(8,128)S(1)}, f32[2,16,128,128]{3,2,1,0:T(8,128)S(1)}, f32[16,128,128]{2,1,0:T(8,128)S(1)}) custom-call(f32[16,128,128]{2,1,0:T(8,128)S(1)} %get-tuple-element.41.refs_0_, f32[2,16,128,128]{3,2,1,0:T(8,128)S(1)} %get-tuple-element.42.refs_1_, f32[16,128,128]{2,1,0:T(8,128)S(1)} %get-tuple-element.43.refs_2_, ...), custom_call_target="tpu_custom_call" | custom-call | tf_op jit(solution)/shard_map/partial/pallas_call | solution.py:151
  74.4 12.5 %collective-permute-done.16.low_z = f32[4,16,128]{2,1,0:T(8,128)S(1)} collective-permute-done((f32[4,16,128]{2,1,0:T(8,128)S(1)}, f32[4,16,128]{2,1,0:T(8,128)S(1)}, u32[]{:S(2)}, u32[]{:S(2)}) %collective-permute-start.16) | collective-permute-done | bytes 32800 | tf_op jit(solution)/shard_map/ppermute | solution.py:140
  86.9 0.0 collective-permute-done.17.high_z
  86.9 0.0 collective-permute-done.15.high_y
  86.9 0.2 collective-permute-done.14.low_y
  87.1 3.4 %last.1 = (f32[4,16,128,128]{3,2,1,0:T(8,128)S(1)}, f32[4,16,128]{2,1,0:T(8,128)S(1)}, f32[4,16,128]{2,1,0:T(8,128)S(1)}) custom-call(f32[16,128,128]{2,1,0:T(8,128)S(1)} %get-tuple-element.46.first_in, f32[2,16,128,128]{3,2,1,0:T(8,128)S(1)} %get-tuple-element.47.middle_in, f32[16,128,128]{2,1,0:T(8,128)S(1)} %get-tuple-element.48.last_in, ...), custom_call_target="tpu_custom_call" | custom-call | tf_op jit(solution)/shard_map/last/pallas_call | solution.py:168
  90.4 3.5 %collective-permute-start.20 = (f32[2,4,16,128]{3,2,1,0:T(8,128)S(1)}, f32[2,4,16,128]{3,2,1,0:T(8,128)S(1)}, u32[]{:S(2)}, u32[]{:S(2)}) collective-permute-start(f32[2,4,16,128]{3,2,1,0:T(8,128)S(1)} %pad_maximum_fusion), channel_id=1, source_target_pairs={{0,1},{1,0},{2,3},{3,2},{4,5},{5,4},{6,7},{7,6},{8,9},{9,8},{10,11... | collective-permute-start | bytes 196616 | tf_op jit(solution)/shard_map/ppermute | solution.py:178
  93.9 7.2 %collective-permute-start.19 = (f32[2,4,16,128]{3,2,1,0:T(8,128)S(1)}, f32[2,4,16,128]{3,2,1,0:T(8,128)S(1)}, u32[]{:S(2)}, u32[]{:S(2)}) collective-permute-start(f32[2,4,16,128]{3,2,1,0:T(8,128)S(1)} %pad_maximum_fusion), channel_id=1, source_target_pairs={{0,2},{1,3},{2,0},{3,1},{4,6},{5,7},{6,4},{7,5},{8,10},{9,11},{10,... | collective-permute-start | bytes 196616 | tf_op jit(solution)/shard_map/ppermute | solution.py:178
  101.1 0.0 collective-permute-start.18
  101.1 2.0 %store.1 = f32[4,16,128,128]{3,2,1,0:T(8,128)} custom-call(f32[4,16,128,128]{3,2,1,0:T(8,128)S(1)} %get-tuple-element.51.tracer), custom_call_target="tpu_custom_call" | custom-call | tf_op jit(solution)/shard_map/store/pallas_call | solution.py:180
  103.1 0.0 collective-permute-done.20
  103.2 0.7 collective-permute-done.19
  103.9 8.4 %collective-permute-done.18 = f32[2,4,16,128]{3,2,1,0:T(8,128)S(1)} collective-permute-done((f32[2,4,16,128]{3,2,1,0:T(8,128)S(1)}, f32[2,4,16,128]{3,2,1,0:T(8,128)S(1)}, u32[]{:S(2)}, u32[]{:S(2)}) %collective-permute-start.18) | collective-permute-done | bytes 65568 | tf_op jit(solution)/shard_map/ppermute | solution.py:178
  112.3 2.2 %scale.1 = f32[4,16,128,128]{3,2,1,0:T(8,128)} custom-call(f32[4,16,128,128]{3,2,1,0:T(8,128)S(1)} %get-tuple-element.51.tracer, f32[4,16,128]{2,1,0:T(8,128)S(1)} %get-tuple-element.52.refs_0_, f32[4,16,128]{2,1,0:T(8,128)S(1)} %get-tuple-element.53.refs_1_, f32[4,16,128]{2,1,0:T(8,128)S(1)} %get-tuple-element.65.refs_2_, ...), custom_call_target="tpu_custom_call" | custom-call | tf_op jit(solution)/shard_map/scale/pallas_call | solution.py:188
  (4 shorter events, 0.0 us)
Async XLA Ops:
  0.6 16.6 %copy-start = (f32[4,16,128,128]{3,2,1,0:T(8,128)S(1)}, f32[4,16,128,128]{3,2,1,0:T(8,128)}, u32[]{:S(2)}) copy-start(f32[4,16,128,128]{3,2,1,0:T(8,128)} %mobility.5) | copy-start | bytes 12582916
  2.6 27.4 %collective-permute-start.3 = (f32[16,128,128]{2,1,0:T(8,128)S(1)}, f32[16,128,128]{2,1,0:T(8,128)S(1)}, u32[]{:S(2)}, u32[]{:S(2)}) collective-permute-start(f32[16,128,128]{2,1,0:T(8,128)S(1)} %get-tuple-element.56), channel_id=1, source_target_pairs={{16,0},{32,16},{48,32},{0,48},{17,1},{33,17},{49,33},{1,49},{18,2}... | collective-permute-start | bytes 3145736 | tf_op jit(solution)/shard_map/ppermute | solution.py:141
  3.4 26.6 %collective-permute-start.2 = (f32[16,128,128]{2,1,0:T(8,128)S(1)}, f32[16,128,128]{2,1,0:T(8,128)S(1)}, u32[]{:S(2)}, u32[]{:S(2)}) collective-permute-start(f32[16,128,128]{2,1,0:T(8,128)S(1)} %get-tuple-element.57), channel_id=1, source_target_pairs={{0,16},{16,32},{32,48},{48,0},{1,17},{17,33},{33,49},{49,1},{2,18}... | collective-permute-start | bytes 3145736 | tf_op jit(solution)/shard_map/ppermute | solution.py:140
  4.4 11.3 %collective-permute-start.1 = (f32[4,128,128]{2,1,0:T(8,128)S(1)}, f32[4,128,128]{2,1,0:T(8,128)S(1)}, u32[]{:S(2)}, u32[]{:S(2)}) collective-permute-start(f32[4,128,128]{2,1,0:T(8,128)S(1)} %get-tuple-element.58), channel_id=1, source_target_pairs={{4,0},{8,4},{12,8},{0,12},{5,1},{9,5},{13,9},{1,13},{6,2},{10,6},{... | collective-permute-start | bytes 786440 | tf_op jit(solution)/shard_map/ppermute | solution.py:141
  7.3 10.0 %collective-permute-start = (f32[4,128,128]{2,1,0:T(8,128)S(1)}, f32[4,128,128]{2,1,0:T(8,128)S(1)}, u32[]{:S(2)}, u32[]{:S(2)}) collective-permute-start(f32[4,128,128]{2,1,0:T(8,128)S(1)} %get-tuple-element.59), channel_id=1, source_target_pairs={{0,4},{4,8},{8,12},{12,0},{1,5},{5,9},{9,13},{13,1},{2,6},{6,10},{... | collective-permute-start | bytes 786440 | tf_op jit(solution)/shard_map/ppermute | solution.py:140
  8.3 21.6 %collective-permute-start.4 = (f32[4,16,128]{2,1,0:T(8,128)S(1)}, f32[4,16,128]{2,1,0:T(8,128)S(1)}, u32[]{:S(2)}, u32[]{:S(2)}) collective-permute-start(f32[4,16,128]{2,1,0:T(8,128)S(1)} %bitcast.35), channel_id=1, source_target_pairs={{0,1},{1,2},{2,3},{3,0},{4,5},{5,6},{6,7},{7,4},{8,9},{9,10},{10,1... | collective-permute-start | bytes 98312 | tf_op jit(solution)/shard_map/ppermute | solution.py:140
  15.7 14.2 %collective-permute-start.5 = (f32[4,16,128]{2,1,0:T(8,128)S(1)}, f32[4,16,128]{2,1,0:T(8,128)S(1)}, u32[]{:S(2)}, u32[]{:S(2)}) collective-permute-start(f32[4,16,128]{2,1,0:T(8,128)S(1)} %bitcast.34), channel_id=1, source_target_pairs={{1,0},{2,1},{3,2},{0,3},{5,4},{6,5},{7,6},{4,7},{9,8},{10,9},{11,1... | collective-permute-start | bytes 98312 | tf_op jit(solution)/shard_map/ppermute | solution.py:141
  17.3 2.2 %copy-start.1 = (f32[4,16,128,128]{3,2,1,0:T(8,128)S(1)}, f32[4,16,128,128]{3,2,1,0:T(8,128)}, u32[]{:S(2)}) copy-start(f32[4,16,128,128]{3,2,1,0:T(8,128)} %refs_4_.3) | copy-start | bytes 12582916
  19.5 2.2 %copy-start.3 = (f32[4,16,128,128]{3,2,1,0:T(8,128)S(1)}, f32[4,16,128,128]{3,2,1,0:T(8,128)}, u32[]{:S(2)}) copy-start(f32[4,16,128,128]{3,2,1,0:T(8,128)} %refs_0_.1) | copy-start | bytes 12582916
  29.9 13.9 %copy-start.2 = (f32[4,16,128,128]{3,2,1,0:T(8,128)S(1)}, f32[4,16,128,128]{3,2,1,0:T(8,128)}, u32[]{:S(2)}) copy-start(f32[4,16,128,128]{3,2,1,0:T(8,128)} %refs_4_.3) | copy-start | bytes 12582916
  31.0 26.5 %collective-permute-start.9 = (f32[16,128,128]{2,1,0:T(8,128)S(1)}, f32[16,128,128]{2,1,0:T(8,128)S(1)}, u32[]{:S(2)}, u32[]{:S(2)}) collective-permute-start(f32[16,128,128]{2,1,0:T(8,128)S(1)} %get-tuple-element.31.refs_0_), channel_id=1, source_target_pairs={{16,0},{32,16},{48,32},{0,48},{17,1},{33,17},{49,33},{1,49},{18,2}... | collective-permute-start | bytes 3145736 | tf_op jit(solution)/shard_map/ppermute | solution.py:141
  31.2 26.4 %collective-permute-start.8 = (f32[16,128,128]{2,1,0:T(8,128)S(1)}, f32[16,128,128]{2,1,0:T(8,128)S(1)}, u32[]{:S(2)}, u32[]{:S(2)}) collective-permute-start(f32[16,128,128]{2,1,0:T(8,128)S(1)} %get-tuple-element.33.refs_2_), channel_id=1, source_target_pairs={{0,16},{16,32},{32,48},{48,0},{1,17},{17,33},{33,49},{49,1},{2,18}... | collective-permute-start | bytes 3145736 | tf_op jit(solution)/shard_map/ppermute | solution.py:140
  31.6 12.1 %collective-permute-start.6 = (f32[4,128,128]{2,1,0:T(8,128)S(1)}, f32[4,128,128]{2,1,0:T(8,128)S(1)}, u32[]{:S(2)}, u32[]{:S(2)}) collective-permute-start(f32[4,128,128]{2,1,0:T(8,128)S(1)} %get-tuple-element.34), channel_id=1, source_target_pairs={{0,4},{4,8},{8,12},{12,0},{1,5},{5,9},{9,13},{13,1},{2,6},{6,10},{... | collective-permute-start | bytes 786440 | tf_op jit(solution)/shard_map/ppermute | solution.py:140
  32.7 11.1 %collective-permute-start.7 = (f32[4,128,128]{2,1,0:T(8,128)S(1)}, f32[4,128,128]{2,1,0:T(8,128)S(1)}, u32[]{:S(2)}, u32[]{:S(2)}) collective-permute-start(f32[4,128,128]{2,1,0:T(8,128)S(1)} %get-tuple-element.35), channel_id=1, source_target_pairs={{4,0},{8,4},{12,8},{0,12},{5,1},{9,5},{13,9},{1,13},{6,2},{10,6},{... | collective-permute-start | bytes 786440 | tf_op jit(solution)/shard_map/ppermute | solution.py:141
  34.8 22.7 %collective-permute-start.10 = (f32[4,16,128]{2,1,0:T(8,128)S(1)}, f32[4,16,128]{2,1,0:T(8,128)S(1)}, u32[]{:S(2)}, u32[]{:S(2)}) collective-permute-start(f32[4,16,128]{2,1,0:T(8,128)S(1)} %get-tuple-element.39), channel_id=1, source_target_pairs={{0,1},{1,2},{2,3},{3,0},{4,5},{5,6},{6,7},{7,4},{8,9},{9,10},{10,1... | collective-permute-start | bytes 98312 | tf_op jit(solution)/shard_map/ppermute | solution.py:140
  43.7 13.9 %collective-permute-start.11 = (f32[4,16,128]{2,1,0:T(8,128)S(1)}, f32[4,16,128]{2,1,0:T(8,128)S(1)}, u32[]{:S(2)}, u32[]{:S(2)}) collective-permute-start(f32[4,16,128]{2,1,0:T(8,128)S(1)} %get-tuple-element.40), channel_id=1, source_target_pairs={{1,0},{2,1},{3,2},{0,3},{5,4},{6,5},{7,6},{4,7},{9,8},{10,9},{11,1... | collective-permute-start | bytes 98312 | tf_op jit(solution)/shard_map/ppermute | solution.py:141
  58.6 28.3 %collective-permute-start.15 = (f32[16,128,128]{2,1,0:T(8,128)S(1)}, f32[16,128,128]{2,1,0:T(8,128)S(1)}, u32[]{:S(2)}, u32[]{:S(2)}) collective-permute-start(f32[16,128,128]{2,1,0:T(8,128)S(1)} %get-tuple-element.41.refs_0_), channel_id=1, source_target_pairs={{16,0},{32,16},{48,32},{0,48},{17,1},{33,17},{49,33},{1,49},{18,2}... | collective-permute-start | bytes 3145736 | tf_op jit(solution)/shard_map/ppermute | solution.py:141
  61.5 25.6 %collective-permute-start.14 = (f32[16,128,128]{2,1,0:T(8,128)S(1)}, f32[16,128,128]{2,1,0:T(8,128)S(1)}, u32[]{:S(2)}, u32[]{:S(2)}) collective-permute-start(f32[16,128,128]{2,1,0:T(8,128)S(1)} %get-tuple-element.43.refs_2_), channel_id=1, source_target_pairs={{0,16},{16,32},{32,48},{48,0},{1,17},{17,33},{33,49},{49,1},{2,18}... | collective-permute-start | bytes 3145736 | tf_op jit(solution)/shard_map/ppermute | solution.py:140
  61.5 10.1 %collective-permute-start.12 = (f32[4,128,128]{2,1,0:T(8,128)S(1)}, f32[4,128,128]{2,1,0:T(8,128)S(1)}, u32[]{:S(2)}, u32[]{:S(2)}) collective-permute-start(f32[4,128,128]{2,1,0:T(8,128)S(1)} %get-tuple-element.44), channel_id=1, source_target_pairs={{0,4},{4,8},{8,12},{12,0},{1,5},{5,9},{9,13},{13,1},{2,6},{6,10},{... | collective-permute-start | bytes 786440 | tf_op jit(solution)/shard_map/ppermute | solution.py:140
  63.0 9.1 %collective-permute-start.13 = (f32[4,128,128]{2,1,0:T(8,128)S(1)}, f32[4,128,128]{2,1,0:T(8,128)S(1)}, u32[]{:S(2)}, u32[]{:S(2)}) collective-permute-start(f32[4,128,128]{2,1,0:T(8,128)S(1)} %get-tuple-element.45), channel_id=1, source_target_pairs={{4,0},{8,4},{12,8},{0,12},{5,1},{9,5},{13,9},{1,13},{6,2},{10,6},{... | collective-permute-start | bytes 786440 | tf_op jit(solution)/shard_map/ppermute | solution.py:141
  64.7 22.1 %collective-permute-start.16 = (f32[4,16,128]{2,1,0:T(8,128)S(1)}, f32[4,16,128]{2,1,0:T(8,128)S(1)}, u32[]{:S(2)}, u32[]{:S(2)}) collective-permute-start(f32[4,16,128]{2,1,0:T(8,128)S(1)} %get-tuple-element.49), channel_id=1, source_target_pairs={{0,1},{1,2},{2,3},{3,0},{4,5},{5,6},{6,7},{7,4},{8,9},{9,10},{10,1... | collective-permute-start | bytes 98312 | tf_op jit(solution)/shard_map/ppermute | solution.py:140
  71.6 15.3 %collective-permute-start.17 = (f32[4,16,128]{2,1,0:T(8,128)S(1)}, f32[4,16,128]{2,1,0:T(8,128)S(1)}, u32[]{:S(2)}, u32[]{:S(2)}) collective-permute-start(f32[4,16,128]{2,1,0:T(8,128)S(1)} %get-tuple-element.50), channel_id=1, source_target_pairs={{1,0},{2,1},{3,2},{0,3},{5,4},{6,5},{7,6},{4,7},{9,8},{10,9},{11,1... | collective-permute-start | bytes 98312 | tf_op jit(solution)/shard_map/ppermute | solution.py:141
  90.4 12.7 %collective-permute-start.20 = (f32[2,4,16,128]{3,2,1,0:T(8,128)S(1)}, f32[2,4,16,128]{3,2,1,0:T(8,128)S(1)}, u32[]{:S(2)}, u32[]{:S(2)}) collective-permute-start(f32[2,4,16,128]{3,2,1,0:T(8,128)S(1)} %pad_maximum_fusion), channel_id=1, source_target_pairs={{0,1},{1,0},{2,3},{3,2},{4,5},{5,4},{6,7},{7,6},{8,9},{9,8},{10,11... | collective-permute-start | bytes 196616 | tf_op jit(solution)/shard_map/ppermute | solution.py:178
  93.9 9.9 %collective-permute-start.19 = (f32[2,4,16,128]{3,2,1,0:T(8,128)S(1)}, f32[2,4,16,128]{3,2,1,0:T(8,128)S(1)}, u32[]{:S(2)}, u32[]{:S(2)}) collective-permute-start(f32[2,4,16,128]{3,2,1,0:T(8,128)S(1)} %pad_maximum_fusion), channel_id=1, source_target_pairs={{0,2},{1,3},{2,0},{3,1},{4,6},{5,7},{6,4},{7,5},{8,10},{9,11},{10,... | collective-permute-start | bytes 196616 | tf_op jit(solution)/shard_map/ppermute | solution.py:178
  101.1 11.2 %collective-permute-start.18 = (f32[2,4,16,128]{3,2,1,0:T(8,128)S(1)}, f32[2,4,16,128]{3,2,1,0:T(8,128)S(1)}, u32[]{:S(2)}, u32[]{:S(2)}) collective-permute-start(f32[2,4,16,128]{3,2,1,0:T(8,128)S(1)} %pad_maximum_fusion), channel_id=1, source_target_pairs={{0,3},{1,2},{2,1},{3,0},{4,7},{5,6},{6,5},{7,4},{8,11},{9,10},{10,... | collective-permute-start | bytes 196616 | tf_op jit(solution)/shard_map/ppermute | solution.py:178

commit v2 on v0

v2 whole, which is shorter than its diff:
```python
import functools

import jax
import jax.numpy as jnp
from jax import lax
from jax.experimental import pallas as pl
from jax.experimental.pallas import tpu as pltpu
from jax.sharding import PartitionSpec as P


STEPS = 3
RIM = 16


def f32(*shape):
    return jax.ShapeDtypeStruct(shape, jnp.float32)


def plane_of(pieces, x):
    if len(pieces) == 1:
        return pieces[0][x]
    inner, outer = pieces
    rim = outer.shape[1] // 2
    return jnp.concatenate([outer[x, :rim], inner[x], outer[x, rim:]], axis=0)


def rows_of(refs):
    if len(refs) == 1:
        return [(refs[0].at[r],) for r in range(refs[0].shape[0])]
    half = len(refs) // 2
    middle = refs[half]
    return [refs[:half]] + [(middle.at[r],) for r in range(middle.shape[0])] + [refs[half + 1 :]]


def line_stats(value):
    mean = jnp.sum(value, axis=0, keepdims=True) * (1.0 / value.shape[0])
    off = value - mean
    return mean, jnp.sum(off * off, axis=0, keepdims=True)


def partial_kernel(n, with_stats, *refs):
    tracer = rows_of(refs[:n])
    mobility, source, low_x, high_x, first, middle, last, *stats = refs[n:]
    top, width, depth, levels = (mobility.shape[0] - 1, *mobility.shape[1:])
    out = [first] + [middle.at[r] for r in range(top - 1)] + [last]
    z = lax.broadcasted_iota(jnp.int32, (depth, levels), 0)

    def cell(r, x, before, after):
        here = plane_of(tracer[r], x)
        spread = before + after
        if r > 0:
            spread += plane_of(tracer[r - 1], x)
        if r < top:
            spread += plane_of(tracer[r + 1], x)
        spread += jnp.where(z == 0, 0.0, pltpu.roll(here, 1, 0))
        spread += jnp.where(z == depth - 1, 0.0, pltpu.roll(here, depth - 1, 0))
        value = here + mobility[r, x] * (spread - 6.0 * here) + source[r, x]
        out[r][x] = value
        if with_stats and 0 < r < top:
            mean, squares = line_stats(value)
            stats[0][0, r - 1, pl.ds(x, 1)] = mean
            stats[0][1, r - 1, pl.ds(x, 1)] = squares

    for r in range(top + 1):
        cell(r, 0, low_x[r], plane_of(tracer[r], 1))

        @pl.loop(1, width - 1)
        def _(x, r=r):
            cell(r, x, plane_of(tracer[r], x - 1), plane_of(tracer[r], x + 1))

        cell(r, width - 1, plane_of(tracer[r], width - 2), high_x[r])


def is_even():
    return lax.rem(lax.axis_index("down"), 2) == 0


def add_lines(row, mobility, far, near, r, x):
    end, depth = (row.shape[1] - 1, mobility.shape[2])
    low_z, high_z = sides_of(far, near, r, x)
    row[x, 0:1] += mobility[r, x, 0:1] * low_z
    row[x, end : end + 1] += mobility[r, x, depth - 1 : depth] * high_z


def sides_of(far, near, r, x):
    across, beside = (far[r, pl.ds(x, 1)], near[r, pl.ds(x, 1)])
    even = is_even()
    return jnp.where(even, across, beside), jnp.where(even, beside, across)


def inner_kernel(first_in, last_in, mobility, low_y, high_y, first, last):
    top = mobility.shape[0] - 1
    rim = (mobility.shape[2] - first.shape[1]) // 2
    inside = slice(rim, mobility.shape[2] - rim)

    @pl.loop(0, first.shape[0])
    def _(x):
        first[x] = first_in[x, inside] + mobility[0, x, inside] * low_y[x]
        last[x] = last_in[x, inside] + mobility[top, x, inside] * high_y[x]


def add_outer(row_in, row, mobility, beside, r, x):
    rim, depth = (row.shape[1] // 2, mobility.shape[2])
    row[x, :rim] = row_in[x, :rim] + mobility[r, x, :rim] * beside[x, :rim]
    row[x, rim:] = row_in[x, depth - rim :] + mobility[r, x, depth - rim :] * beside[x, rim:]


def outer_kernel(first_in, last_in, mobility, low_y, high_y, far, near, first, last):
    top = mobility.shape[0] - 1

    @pl.loop(0, first.shape[0])
    def _(x):
        add_outer(first_in, first, mobility, low_y, 0, x)
        add_outer(last_in, last, mobility, high_y, top, x)
        add_lines(first, mobility, far, near, 0, x)
        add_lines(last, mobility, far, near, top, x)


def take_edges(rows, first_x, last_x, far, near):
    width = far.shape[1]
    even = is_even()
    for r, row in enumerate(rows):
        outer = row[-1]
        end = outer.shape[1] - 1

        @pl.loop(0, width)
        def _(x, r=r, outer=outer, end=end):
            leading, trailing = (outer[x, 0:1], outer[x, end : end + 1])
            far[r, pl.ds(x, 1)] = jnp.where(even, leading, trailing)
            near[r, pl.ds(x, 1)] = jnp.where(even, trailing, leading)

        first_x[r] = plane_of(row, 0)
        last_x[r] = plane_of(row, width - 1)


def edges_kernel(middle_in, *refs):
    ends, (mobility, far, near, middle), edges = (refs[:4], refs[4:8], refs[8:])

    @pl.loop(0, mobility.shape[1])
    def _(x):
        for r in range(1, mobility.shape[0] - 1):
            add_lines(middle.at[r - 1], mobility, far, near, r, x)

    take_edges(rows_of((*ends[:2], middle, *ends[2:])), *edges)


def take_inner_kernel(tracer, first, last):
    rim = (tracer.shape[2] - first.shape[1]) // 2
    inside = slice(rim, tracer.shape[2] - rim)

    @pl.loop(0, first.shape[0])
    def _(x):
        first[x] = tracer[0, x, inside]
        last[x] = tracer[tracer.shape[0] - 1, x, inside]


def take_outer_kernel(tracer, first, last, *edges):
    rim, depth = (first.shape[1] // 2, tracer.shape[2])

    @pl.loop(0, first.shape[0])
    def _(x):
        for r, row in ((0, first), (tracer.shape[0] - 1, last)):
            row[x, :rim] = tracer[r, x, :rim]
            row[x, rim:] = tracer[r, x, depth - rim :]

    take_edges(rows_of((tracer,)), *edges)


def last_kernel(first_in, middle_in, last_in, middle_stats, mobility, *refs):
    low_inner, high_inner, low_outer, high_outer, far, near, first, middle, last, stats = refs
    top = mobility.shape[0] - 1
    width, depth, _ = first_in.shape

    @pl.loop(0, width)
    def _(x):
        low_y, high_y = ((low_inner, low_outer), (high_inner, high_outer))
        for r, row_in, row, beside in ((0, first_in, first, low_y), (top, last_in, last, high_y)):
            row[x] = row_in[x] + mobility[r, x] * plane_of(beside, x)
            add_lines(row, mobility, far, near, r, x)
            stats[0, r, pl.ds(x, 1)], stats[1, r, pl.ds(x, 1)] = line_stats(row[x])
        for r in range(1, top):
            row = middle.at[r - 1]
            mean = middle_stats[0, r - 1, pl.ds(x, 1)]
            more = squares = 0.0
            for z, line in zip((0, depth - 1), sides_of(far, near, r, x)):
                old = row[x, z : z + 1]
                added = mobility[r, x, z : z + 1] * line
                row[x, z : z + 1] = old + added
                more += added
                squares += added * (2.0 * (old - mean) + added)
            shift = more * (1.0 / depth)
            stats[0, r, pl.ds(x, 1)] = mean + shift
            stats[1, r, pl.ds(x, 1)] = middle_stats[1, r - 1, pl.ds(x, 1)] + (squares - more * shift)


def store_kernel(first, middle, last, out, sems):
    top = out.shape[0] - 1
    copies = [
        pltpu.make_async_copy(first, out.at[0], sems.at[0]),
        pltpu.make_async_copy(middle, out.at[1:top], sems.at[1]),
        pltpu.make_async_copy(last, out.at[top], sems.at[2]),
    ]
    for copy in copies:
        copy.start()
    for copy in copies:
        copy.wait()


def merged(mine, other, count):
    away = mine[0] - other[0]
    return 0.5 * (mine[0] + other[0]), mine[1] + other[1] + (0.5 * count) * (away * away)


def scale_kernel(count, first, middle, last, mine, other, out, held, sems):
    copies = []
    rows = [first] + [middle.at[r] for r in range(middle.shape[0])] + [last]
    for r, row in enumerate(rows):
        mean, squares = merged((mine[0, r], mine[1, r]), (other[0, r], other[1, r]), count)
        scale = lax.rsqrt(squares * (1.0 / (2 * count)) + 0.0001)
        for x in range(row.shape[0]):
            held[r, x] = (row[x] - mean[x : x + 1]) * scale[x : x + 1]
        copies.append(pltpu.make_async_copy(held.at[r], out.at[r], sems.at[r]))
        copies[-1].start()
    for copy in copies:
        copy.wait()


def kernel_call(kernel, *out_shape, vmem_mib=16, **options):
    params = pltpu.CompilerParams(vmem_limit_bytes=vmem_mib * 1024 * 1024)
    return pl.pallas_call(kernel, out_shape=out_shape, compiler_params=params, **options)


def body(tracer, mobility, source):
    count, width, depth, levels = tracer.shape
    row, middle = (f32(width, depth, levels), f32(count - 2, width, depth, levels))
    inner, outer = (f32(width, depth - 2 * RIM, levels), f32(width, 2 * RIM, levels))
    edge_shapes = (f32(count, depth, levels),) * 2 + (f32(count, width, levels),) * 2

    peers = lax.axis_size("down")
    near = [(i, i ^ 1) for i in range(peers)]
    far = [(i, (i + (1 if i % 2 else -1)) % peers) for i in range(peers)]

    def swap(leading, last, axis):
        peers = lax.axis_size(axis)
        up = [(i, (i + 1) % peers) for i in range(peers)]
        low = lax.ppermute(last, axis, up)
        high = lax.ppermute(leading, axis, [(b, a) for a, b in up])
        return (low, high)

    def call(kernel, *out_shape, **options):
        return kernel_call(kernel, *out_shape, **options)

    inners = call(take_inner_kernel, inner, inner)(tracer)
    inners_y = swap(*inners, "south")
    first, last, *edges = call(take_outer_kernel, outer, outer, *edge_shapes)(tracer)
    pieces = (tracer,)
    outers = (first, last)
    for step in range(STEPS):
        final = step == STEPS - 1
        along_x = swap(*edges[:2], "east")
        along_z = (lax.ppermute(edges[2], "down", far), lax.ppermute(edges[3], "down", near))
        outers_y = swap(*outers, "south")
        stats = (f32(2, count - 2, width, levels),) if final else ()
        first, inside, last, *stats = call(
            functools.partial(partial_kernel, len(pieces), final), row, middle, row, *stats
        )(*pieces, mobility, source, *along_x)
        if not final:
            inners = call(inner_kernel, inner, inner)(first, last, mobility, *inners_y)
            inners_y_next = swap(*inners, "south")
            outers = call(outer_kernel, outer, outer)(first, last, mobility, *outers_y, *along_z)
            inside, *edges = call(
                edges_kernel, middle, *edge_shapes, input_output_aliases={0: 0}
            )(inside, inners[0], outers[0], inners[1], outers[1], mobility, *along_z)
            pieces = (inners[0], outers[0], inside, inners[1], outers[1])
            inners_y = inners_y_next
    *rows, mine = kernel_call(
        last_kernel, row, middle, row, f32(2, count, width, levels), input_output_aliases={1: 1}
    )(first, inside, last, *stats, mobility, *inners_y, *outers_y, *along_z)
    (stored,) = kernel_call(
        store_kernel,
        f32(count, width, depth, levels),
        out_specs=(pl.BlockSpec(memory_space=pl.ANY),),
        scratch_shapes=[pltpu.SemaphoreType.DMA((3,))],
    )(*rows)
    members = depth
    other = lax.ppermute(mine, "down", near)
    mine = jnp.stack(merged(mine, other, members))
    members *= 2
    other = lax.ppermute(mine, "down", [(i, (i + 2) % peers) for i in range(peers)])
    (standardized,) = kernel_call(
        functools.partial(scale_kernel, members),
        f32(count, width, depth, levels),
        out_specs=(pl.BlockSpec(memory_space=pl.ANY),),
        scratch_shapes=[pltpu.VMEM((count, width, depth, levels), jnp.float32), pltpu.SemaphoreType.DMA((count,))],
    )(*rows, mine, other)
    return (standardized, stored)


def solution(mesh):
    spec = P(("trial", "south"), "east", "down", None)
    return jax.shard_map(body, mesh=mesh, in_specs=(spec,) * 3, out_specs=(spec,) * 2, check_vma=False)
```

time: 153 us -> 130 us (0.85)
  the two profiles are of different devices: /device:TPU:44 before, /device:TPU:32 now
where the time goes in v2:
time: 130 us
  waiting for transfers between devices  56.9 us (44%)
  starting transfers between devices  53.6 us (41%)
  Pallas kernels  16.4 us (13%)
  local copies, waits for them, and re-layouts  2.19 us (2%)
    ppermute x3, waiting for transfers between devices, body(): lax.ppermute(edges[3], 'down', near)  24.3 us
    ppermute x3, starting transfers between devices, body(): lax.ppermute(edges[2], 'down', far)  23.5 us
    ppermute x9, waiting for transfers between devices, swap(): low = lax.ppermute(last, axis, up)  20.7 us
    ppermute x9, starting transfers between devices, swap(): high = lax.ppermute(leading, axis, [(b, a) for a, b in up])  13.5 us
    pallas_call x3, Pallas kernels, body(): call(functools.partial(partial_kernel, len(pieces), final), row, middle,...  7.76 us
    ppermute x3, starting transfers between devices, body(): lax.ppermute(edges[3], 'down', near)  6.26 us
    ppermute x9, starting transfers between devices, swap(): low = lax.ppermute(last, axis, up)  6.22 us
    ppermute x1, waiting for transfers between devices, body(): other = lax.ppermute(mine, 'down', near)  4.35 us
  transfers between devices with their start and end apart: 26, of which 12 were waited for; matrix products, arithmetic and copies ran while one was open for 0% of the time, Pallas kernels for 10%

profile of v2, /device:TPU:32, one launch (start us, length us, event | category | flops | bytes accessed | tf_op | source)
XLA Modules:
  0.0 130.1 jit_solution(8336654278307422869)
XLA Ops:
  0.6 2.2 %copy-done.2 = f32[4,16,128,128]{3,2,1,0:T(8,128)S(1)} copy-done((f32[4,16,128,128]{3,2,1,0:T(8,128)S(1)}, f32[4,16,128,128]{3,2,1,0:T(8,128)}, u32[]{:S(2)}) %copy-start.2) | copy-done | bytes 4194328
  2.8 0.1 shard_map.52
  3.0 0.1 collective-permute-start.2
  3.0 0.0 copy-start
  3.1 1.7 %collective-permute-start.3 = (f32[16,96,128]{2,1,0:T(8,128)S(1)}, f32[16,96,128]{2,1,0:T(8,128)S(1)}, u32[]{:S(2)}, u32[]{:S(2)}) collective-permute-start(f32[16,96,128]{2,1,0:T(8,128)S(1)} %get-tuple-element.47), channel_id=1, source_target_pairs={{16,0},{32,16},{48,32},{0,48},{17,1},{33,17},{49,33},{1,49},{18,2}... | collective-permute-start | bytes 2359304 | tf_op jit(solution)/shard_map/ppermute | solution.py:247
  4.8 0.5 shard_map.50
  5.3 1.6 %collective-permute-start = (f32[4,128,128]{2,1,0:T(8,128)S(1)}, f32[4,128,128]{2,1,0:T(8,128)S(1)}, u32[]{:S(2)}, u32[]{:S(2)}) collective-permute-start(f32[4,128,128]{2,1,0:T(8,128)S(1)} %get-tuple-element.42), channel_id=1, source_target_pairs={{0,4},{4,8},{8,12},{12,0},{1,5},{5,9},{9,13},{13,1},{2,6},{6,10},{... | collective-permute-start | bytes 786440 | tf_op jit(solution)/shard_map/ppermute | solution.py:246
  6.9 1.7 %collective-permute-start.1 = (f32[4,128,128]{2,1,0:T(8,128)S(1)}, f32[4,128,128]{2,1,0:T(8,128)S(1)}, u32[]{:S(2)}, u32[]{:S(2)}) collective-permute-start(f32[4,128,128]{2,1,0:T(8,128)S(1)} %get-tuple-element.43), channel_id=1, source_target_pairs={{4,0},{8,4},{12,8},{0,12},{5,1},{9,5},{13,9},{1,13},{6,2},{10,6},{... | collective-permute-start | bytes 786440 | tf_op jit(solution)/shard_map/ppermute | solution.py:247
  8.6 6.1 %collective-permute-done.refs_3_ = f32[4,128,128]{2,1,0:T(8,128)S(1)} collective-permute-done((f32[4,128,128]{2,1,0:T(8,128)S(1)}, f32[4,128,128]{2,1,0:T(8,128)S(1)}, u32[]{:S(2)}, u32[]{:S(2)}) %collective-permute-start) | collective-permute-done | bytes 262176 | tf_op jit(solution)/shard_map/ppermute | solution.py:246
  14.8 0.0 collective-permute-done.1.refs_4_
  14.8 2.3 %shard_map.51 = (f32[16,128,128]{2,1,0:T(8,128)S(1)}, f32[2,16,128,128]{3,2,1,0:T(8,128)S(1)}, f32[16,128,128]{2,1,0:T(8,128)S(1)}) custom-call(f32[4,16,128,128]{3,2,1,0:T(8,128)S(1)} %copy-done.2, f32[4,16,128,128]{3,2,1,0:T(8,128)S(1)} %copy-done, f32[4,16,128,128]{3,2,1,0:T(8,128)S(1)} %copy-done.1, f32[4,128,128]{2,1,0:T(8,128)S(1)} %collective-permute-done.refs_3_, ...), custom_call_target="tpu_custom_call" | custom-call | tf_op jit(solution)/shard_map/pallas_call | solution.py:264
  17.1 3.9 %collective-permute-done.2.low_y = f32[16,96,128]{2,1,0:T(8,128)S(1)} collective-permute-done((f32[16,96,128]{2,1,0:T(8,128)S(1)}, f32[16,96,128]{2,1,0:T(8,128)S(1)}, u32[]{:S(2)}, u32[]{:S(2)}) %collective-permute-start.2) | collective-permute-done | bytes 786464 | tf_op jit(solution)/shard_map/ppermute | solution.py:246
  21.0 1.0 collective-permute-done.3.high_y
  22.0 0.3 shard_map.53
  22.2 2.0 %collective-permute-start.11 = (f32[16,96,128]{2,1,0:T(8,128)S(1)}, f32[16,96,128]{2,1,0:T(8,128)S(1)}, u32[]{:S(2)}, u32[]{:S(2)}) collective-permute-start(f32[16,96,128]{2,1,0:T(8,128)S(1)} %get-tuple-element.48.refs_0_), channel_id=1, source_target_pairs={{16,0},{32,16},{48,32},{0,48},{17,1},{33,17},{49,33},{1,49},{18,2}... | collective-permute-start | bytes 2359304 | tf_op jit(solution)/shard_map/ppermute | solution.py:247
  24.2 0.0 collective-permute-start.10
  24.2 0.6 collective-permute-start.4
  24.8 1.2 collective-permute-start.5
  26.0 8.6 %collective-permute-start.6 = (f32[4,16,128]{2,1,0:T(8,128)S(1)}, f32[4,16,128]{2,1,0:T(8,128)S(1)}, u32[]{:S(2)}, u32[]{:S(2)}) collective-permute-start(f32[4,16,128]{2,1,0:T(8,128)S(1)} %get-tuple-element.51), channel_id=1, source_target_pairs={{0,3},{1,2},{2,1},{3,0},{4,7},{5,6},{6,5},{7,4},{8,11},{9,10},{10,... | collective-permute-start | bytes 98312 | tf_op jit(solution)/shard_map/ppermute | solution.py:261
  34.6 2.0 %collective-permute-done.6.far.refs_5_ = f32[4,16,128]{2,1,0:T(8,128)S(1)} collective-permute-done((f32[4,16,128]{2,1,0:T(8,128)S(1)}, f32[4,16,128]{2,1,0:T(8,128)S(1)}, u32[]{:S(2)}, u32[]{:S(2)}) %collective-permute-start.6) | collective-permute-done | bytes 32800 | tf_op jit(solution)/shard_map/ppermute | solution.py:261
  36.6 2.6 %collective-permute-start.7 = (f32[4,16,128]{2,1,0:T(8,128)S(1)}, f32[4,16,128]{2,1,0:T(8,128)S(1)}, u32[]{:S(2)}, u32[]{:S(2)}) collective-permute-start(f32[4,16,128]{2,1,0:T(8,128)S(1)} %get-tuple-element.52), channel_id=1, source_target_pairs={{0,1},{1,0},{2,3},{3,2},{4,5},{5,4},{6,7},{7,6},{8,9},{9,8},{10,11... | collective-permute-start | bytes 98312 | tf_op jit(solution)/shard_map/ppermute | solution.py:261
  39.2 13.1 %collective-permute-done.7.near.refs_6_ = f32[4,16,128]{2,1,0:T(8,128)S(1)} collective-permute-done((f32[4,16,128]{2,1,0:T(8,128)S(1)}, f32[4,16,128]{2,1,0:T(8,128)S(1)}, u32[]{:S(2)}, u32[]{:S(2)}) %collective-permute-start.7) | collective-permute-done | bytes 32800 | tf_op jit(solution)/shard_map/ppermute | solution.py:261
  52.4 0.0 collective-permute-done.4.low_y
  52.4 0.0 collective-permute-done.5.high_y
  52.4 0.3 shard_map.54
  52.6 0.7 shard_map.55
  53.4 1.6 %collective-permute-start.8 = (f32[4,128,128]{2,1,0:T(8,128)S(1)}, f32[4,128,128]{2,1,0:T(8,128)S(1)}, u32[]{:S(2)}, u32[]{:S(2)}) collective-permute-start(f32[4,128,128]{2,1,0:T(8,128)S(1)} %get-tuple-element.58), channel_id=1, source_target_pairs={{0,4},{4,8},{8,12},{12,0},{1,5},{5,9},{9,13},{13,1},{2,6},{6,10},{... | collective-permute-start | bytes 786440 | tf_op jit(solution)/shard_map/ppermute | solution.py:246
  54.9 1.7 %collective-permute-start.9 = (f32[4,128,128]{2,1,0:T(8,128)S(1)}, f32[4,128,128]{2,1,0:T(8,128)S(1)}, u32[]{:S(2)}, u32[]{:S(2)}) collective-permute-start(f32[4,128,128]{2,1,0:T(8,128)S(1)} %get-tuple-element.59), channel_id=1, source_target_pairs={{4,0},{8,4},{12,8},{0,12},{5,1},{9,5},{13,9},{1,13},{6,2},{10,6},{... | collective-permute-start | bytes 786440 | tf_op jit(solution)/shard_map/ppermute | solution.py:247
  56.7 0.0 collective-permute-start.13
  56.7 6.3 %collective-permute-done.8.refs_7_ = f32[4,128,128]{2,1,0:T(8,128)S(1)} collective-permute-done((f32[4,128,128]{2,1,0:T(8,128)S(1)}, f32[4,128,128]{2,1,0:T(8,128)S(1)}, u32[]{:S(2)}, u32[]{:S(2)}) %collective-permute-start.8) | collective-permute-done | bytes 262176 | tf_op jit(solution)/shard_map/ppermute | solution.py:246
  63.0 0.0 collective-permute-start.12
  63.0 0.0 collective-permute-done.9.refs_8_
  63.0 2.2 %shard_map.56 = (f32[16,128,128]{2,1,0:T(8,128)S(1)}, f32[2,16,128,128]{3,2,1,0:T(8,128)S(1)}, f32[16,128,128]{2,1,0:T(8,128)S(1)}) custom-call(f32[16,96,128]{2,1,0:T(8,128)S(1)} %get-tuple-element.48.refs_0_, f32[16,32,128]{2,1,0:T(8,128)S(1)} %get-tuple-element.53.refs_1_, f32[2,16,128,128]{3,2,1,0:T(8,128)S(1)} %get-tuple-element.57.refs_2_, ...), custom_call_target="tpu_custom_call" | custom-call | tf_op jit(solution)/shard_map/pallas_call | solution.py:264
  65.2 0.0 collective-permute-done.11.high_y
  65.2 0.0 collective-permute-done.10.low_y
  65.3 0.3 shard_map.57
  65.5 1.8 %collective-permute-start.19 = (f32[16,96,128]{2,1,0:T(8,128)S(1)}, f32[16,96,128]{2,1,0:T(8,128)S(1)}, u32[]{:S(2)}, u32[]{:S(2)}) collective-permute-start(f32[16,96,128]{2,1,0:T(8,128)S(1)} %get-tuple-element.62.refs_0_), channel_id=1, source_target_pairs={{16,0},{32,16},{48,32},{0,48},{17,1},{33,17},{49,33},{1,49},{18,2}... | collective-permute-start | bytes 2359304 | tf_op jit(solution)/shard_map/ppermute | solution.py:247
  67.4 0.0 collective-permute-start.18
  67.4 6.3 %collective-permute-start.14 = (f32[4,16,128]{2,1,0:T(8,128)S(1)}, f32[4,16,128]{2,1,0:T(8,128)S(1)}, u32[]{:S(2)}, u32[]{:S(2)}) collective-permute-start(f32[4,16,128]{2,1,0:T(8,128)S(1)} %get-tuple-element.63), channel_id=1, source_target_pairs={{0,3},{1,2},{2,1},{3,0},{4,7},{5,6},{6,5},{7,4},{8,11},{9,10},{10,... | collective-permute-start | bytes 98312 | tf_op jit(solution)/shard_map/ppermute | solution.py:261
  73.6 3.0 %collective-permute-start.15 = (f32[4,16,128]{2,1,0:T(8,128)S(1)}, f32[4,16,128]{2,1,0:T(8,128)S(1)}, u32[]{:S(2)}, u32[]{:S(2)}) collective-permute-start(f32[4,16,128]{2,1,0:T(8,128)S(1)} %get-tuple-element.64), channel_id=1, source_target_pairs={{0,1},{1,0},{2,3},{3,2},{4,5},{5,4},{6,7},{7,6},{8,9},{9,8},{10,11... | collective-permute-start | bytes 98312 | tf_op jit(solution)/shard_map/ppermute | solution.py:261
  76.6 0.0 collective-permute-done.12.low_y
  76.6 1.0 collective-permute-done.14.far.refs_5_
  77.6 9.7 %collective-permute-done.15.near.refs_6_ = f32[4,16,128]{2,1,0:T(8,128)S(1)} collective-permute-done((f32[4,16,128]{2,1,0:T(8,128)S(1)}, f32[4,16,128]{2,1,0:T(8,128)S(1)}, u32[]{:S(2)}, u32[]{:S(2)}) %collective-permute-start.15) | collective-permute-done | bytes 32800 | tf_op jit(solution)/shard_map/ppermute | solution.py:261
  87.3 0.3 shard_map.58
  87.5 0.3 collective-permute-start.21
  87.9 0.7 shard_map.59
  88.6 0.4 collective-permute-start.16
  88.9 3.0 %collective-permute-start.17 = (f32[4,128,128]{2,1,0:T(8,128)S(1)}, f32[4,128,128]{2,1,0:T(8,128)S(1)}, u32[]{:S(2)}, u32[]{:S(2)}) collective-permute-start(f32[4,128,128]{2,1,0:T(8,128)S(1)} %get-tuple-element.71), channel_id=1, source_target_pairs={{4,0},{8,4},{12,8},{0,12},{5,1},{9,5},{13,9},{1,13},{6,2},{10,6},{... | collective-permute-start | bytes 786440 | tf_op jit(solution)/shard_map/ppermute | solution.py:247
  91.9 0.0 collective-permute-done.21.refs_3_
  91.9 2.1 %collective-permute-start.20 = (f32[16,32,128]{2,1,0:T(8,128)S(1)}, f32[16,32,128]{2,1,0:T(8,128)S(1)}, u32[]{:S(2)}, u32[]{:S(2)}) collective-permute-start(f32[16,32,128]{2,1,0:T(8,128)S(1)} %get-tuple-element.68.refs_3_.refs_4_), channel_id=1, source_target_pairs={{0,16},{16,32},{32,48},{48,0},{1,17},{17,33},{33,49},{49,1},{2,18}... | collective-permute-start | bytes 786440 | tf_op jit(solution)/shard_map/ppermute | solution.py:246
  94.0 4.4 %collective-permute-done.16.refs_7_ = f32[4,128,128]{2,1,0:T(8,128)S(1)} collective-permute-done((f32[4,128,128]{2,1,0:T(8,128)S(1)}, f32[4,128,128]{2,1,0:T(8,128)S(1)}, u32[]{:S(2)}, u32[]{:S(2)}) %collective-permute-start.16) | collective-permute-done | bytes 262176 | tf_op jit(solution)/shard_map/ppermute | solution.py:246
  98.3 8.6 %collective-permute-start.22 = (f32[4,16,128]{2,1,0:T(8,128)S(1)}, f32[4,16,128]{2,1,0:T(8,128)S(1)}, u32[]{:S(2)}, u32[]{:S(2)}) collective-permute-start(f32[4,16,128]{2,1,0:T(8,128)S(1)} %get-tuple-element.76), channel_id=1, source_target_pairs={{0,3},{1,2},{2,1},{3,0},{4,7},{5,6},{6,5},{7,4},{8,11},{9,10},{10,... | collective-permute-start | bytes 98312 | tf_op jit(solution)/shard_map/ppermute | solution.py:261
  106.9 0.7 collective-permute-start.23
  107.6 3.2 %shard_map.60 = (f32[16,128,128]{2,1,0:T(8,128)S(1)}, f32[2,16,128,128]{3,2,1,0:T(8,128)S(1)}, f32[16,128,128]{2,1,0:T(8,128)S(1)}, f32[2,2,16,128]{3,2,1,0:T(8,128)S(1)}) custom-call(f32[16,96,128]{2,1,0:T(8,128)S(1)} %get-tuple-element.62.refs_0_, f32[16,32,128]{2,1,0:T(8,128)S(1)} %get-tuple-element.65.refs_1_, ...), custom_call_target="tpu_custom_call" | custom-call | tf_op jit(solution)/shard_map/pallas_call | solution.py:264
  110.8 1.5 %collective-permute-done.23.refs_5_ = f32[4,16,128]{2,1,0:T(8,128)S(1)} collective-permute-done((f32[4,16,128]{2,1,0:T(8,128)S(1)}, f32[4,16,128]{2,1,0:T(8,128)S(1)}, u32[]{:S(2)}, u32[]{:S(2)}) %collective-permute-start.23) | collective-permute-done | bytes 32800 | tf_op jit(solution)/shard_map/ppermute | solution.py:261
  112.3 0.0 collective-permute-done.19.refs_1_
  112.3 0.0 collective-permute-done.18.refs_0_
  112.3 1.3 %shard_map.61 = (f32[16,128,128]{2,1,0:T(8,128)S(1)}, f32[2,16,128,128]{3,2,1,0:T(8,128)S(1)}, f32[16,128,128]{2,1,0:T(8,128)S(1)}, f32[2,4,16,128]{3,2,1,0:T(8,128)S(1)}) custom-call(f32[16,128,128]{2,1,0:T(8,128)S(1)} %get-tuple-element.72.first_in, f32[2,16,128,128]{3,2,1,0:T(8,128)S(1)} %get-tuple-element.73.middle_in, ...), custom_call_target="tpu_custom_call", output_to_operand_aliasing={{1}: (1, {})} | custom-call | tf_op jit(solution)/shard_map/pallas_call | solution.py:276
  113.7 1.5 %collective-permute-start.24 = (f32[2,4,16,128]{3,2,1,0:T(8,128)S(1)}, f32[2,4,16,128]{3,2,1,0:T(8,128)S(1)}, u32[]{:S(2)}, u32[]{:S(2)}) collective-permute-start(f32[2,4,16,128]{3,2,1,0:T(8,128)S(1)} %get-tuple-element.81), channel_id=1, source_target_pairs={{0,1},{1,0},{2,3},{3,2},{4,5},{5,4},{6,7},{7,6},{8,9},{9,8},{10,11... | collective-permute-start | bytes 196616 | tf_op jit(solution)/shard_map/ppermute | solution.py:286
  115.2 4.4 %collective-permute-done.24 = f32[2,4,16,128]{3,2,1,0:T(8,128)S(1)} collective-permute-done((f32[2,4,16,128]{3,2,1,0:T(8,128)S(1)}, f32[2,4,16,128]{3,2,1,0:T(8,128)S(1)}, u32[]{:S(2)}, u32[]{:S(2)}) %collective-permute-start.24) | collective-permute-done | bytes 65568 | tf_op jit(solution)/shard_map/ppermute | solution.py:286
  119.5 2.6 %collective-permute-start.25 = (f32[2,4,16,128]{3,2,1,0:T(8,128)S(1)}, f32[2,4,16,128]{3,2,1,0:T(8,128)S(1)}, u32[]{:S(2)}, u32[]{:S(2)}) collective-permute-start(f32[2,4,16,128]{3,2,1,0:T(8,128)S(1)} %pad_maximum_fusion.mine), channel_id=1, source_target_pairs={{0,2},{1,3},{2,0},{3,1},{4,6},{5,7},{6,4},{7,5},{8,10},{9,11},{10,... | collective-permute-start | bytes 196616 | tf_op jit(solution)/shard_map/ppermute | solution.py:289
  122.2 2.0 %shard_map.63 = f32[4,16,128,128]{3,2,1,0:T(8,128)} custom-call(f32[16,128,128]{2,1,0:T(8,128)S(1)} %get-tuple-element.78.first, f32[2,16,128,128]{3,2,1,0:T(8,128)S(1)} %get-tuple-element.79.middle, f32[16,128,128]{2,1,0:T(8,128)S(1)} %get-tuple-element.80.last), custom_call_target="tpu_custom_call" | custom-call | tf_op jit(solution)/shard_map/pallas_call | solution.py:279
  124.2 3.6 %collective-permute-done.25.other = f32[2,4,16,128]{3,2,1,0:T(8,128)S(1)} collective-permute-done((f32[2,4,16,128]{3,2,1,0:T(8,128)S(1)}, f32[2,4,16,128]{3,2,1,0:T(8,128)S(1)}, u32[]{:S(2)}, u32[]{:S(2)}) %collective-permute-start.25) | collective-permute-done | bytes 65568 | tf_op jit(solution)/shard_map/ppermute | solution.py:289
  127.8 2.1 %shard_map.62 = f32[4,16,128,128]{3,2,1,0:T(8,128)} custom-call(f32[16,128,128]{2,1,0:T(8,128)S(1)} %get-tuple-element.78.first, f32[2,16,128,128]{3,2,1,0:T(8,128)S(1)} %get-tuple-element.79.middle, f32[16,128,128]{2,1,0:T(8,128)S(1)} %get-tuple-element.80.last, f32[2,4,16,128]{3,2,1,0:T(8,128)S(1)} %pad_maximum_fusion.mine, ...), custom_call_target="tpu_custom_call" | custom-call | tf_op jit(solution)/shard_map/pallas_call | solution.py:290
  (10 shorter events, 0.0 us)
Async XLA Ops:
  0.6 2.2 %copy-start.2 = (f32[4,16,128,128]{3,2,1,0:T(8,128)S(1)}, f32[4,16,128,128]{3,2,1,0:T(8,128)}, u32[]{:S(2)}) copy-start(f32[4,16,128,128]{3,2,1,0:T(8,128)} %tracer.3) | copy-start | bytes 12582916
  2.8 12.0 %copy-start.1 = (f32[4,16,128,128]{3,2,1,0:T(8,128)S(1)}, f32[4,16,128,128]{3,2,1,0:T(8,128)}, u32[]{:S(2)}) copy-start(f32[4,16,128,128]{3,2,1,0:T(8,128)} %refs_6_.3) | copy-start | bytes 12582916
  3.0 18.0 %collective-permute-start.2 = (f32[16,96,128]{2,1,0:T(8,128)S(1)}, f32[16,96,128]{2,1,0:T(8,128)S(1)}, u32[]{:S(2)}, u32[]{:S(2)}) collective-permute-start(f32[16,96,128]{2,1,0:T(8,128)S(1)} %get-tuple-element.46), channel_id=1, source_target_pairs={{0,16},{16,32},{32,48},{48,0},{1,17},{17,33},{33,49},{49,1},{2,18}... | collective-permute-start | bytes 2359304 | tf_op jit(solution)/shard_map/ppermute | solution.py:246
  3.0 11.7 %copy-start = (f32[4,16,128,128]{3,2,1,0:T(8,128)S(1)}, f32[4,16,128,128]{3,2,1,0:T(8,128)}, u32[]{:S(2)}) copy-start(f32[4,16,128,128]{3,2,1,0:T(8,128)} %mobility.9) | copy-start | bytes 12582916
  3.1 18.9 %collective-permute-start.3 = (f32[16,96,128]{2,1,0:T(8,128)S(1)}, f32[16,96,128]{2,1,0:T(8,128)S(1)}, u32[]{:S(2)}, u32[]{:S(2)}) collective-permute-start(f32[16,96,128]{2,1,0:T(8,128)S(1)} %get-tuple-element.47), channel_id=1, source_target_pairs={{16,0},{32,16},{48,32},{0,48},{17,1},{33,17},{49,33},{1,49},{18,2}... | collective-permute-start | bytes 2359304 | tf_op jit(solution)/shard_map/ppermute | solution.py:247
  5.3 9.5 %collective-permute-start = (f32[4,128,128]{2,1,0:T(8,128)S(1)}, f32[4,128,128]{2,1,0:T(8,128)S(1)}, u32[]{:S(2)}, u32[]{:S(2)}) collective-permute-start(f32[4,128,128]{2,1,0:T(8,128)S(1)} %get-tuple-element.42), channel_id=1, source_target_pairs={{0,4},{4,8},{8,12},{12,0},{1,5},{5,9},{9,13},{13,1},{2,6},{6,10},{... | collective-permute-start | bytes 786440 | tf_op jit(solution)/shard_map/ppermute | solution.py:246
  6.9 7.9 %collective-permute-start.1 = (f32[4,128,128]{2,1,0:T(8,128)S(1)}, f32[4,128,128]{2,1,0:T(8,128)S(1)}, u32[]{:S(2)}, u32[]{:S(2)}) collective-permute-start(f32[4,128,128]{2,1,0:T(8,128)S(1)} %get-tuple-element.43), channel_id=1, source_target_pairs={{4,0},{8,4},{12,8},{0,12},{5,1},{9,5},{13,9},{1,13},{6,2},{10,6},{... | collective-permute-start | bytes 786440 | tf_op jit(solution)/shard_map/ppermute | solution.py:247
  22.2 43.0 %collective-permute-start.11 = (f32[16,96,128]{2,1,0:T(8,128)S(1)}, f32[16,96,128]{2,1,0:T(8,128)S(1)}, u32[]{:S(2)}, u32[]{:S(2)}) collective-permute-start(f32[16,96,128]{2,1,0:T(8,128)S(1)} %get-tuple-element.48.refs_0_), channel_id=1, source_target_pairs={{16,0},{32,16},{48,32},{0,48},{17,1},{33,17},{49,33},{1,49},{18,2}... | collective-permute-start | bytes 2359304 | tf_op jit(solution)/shard_map/ppermute | solution.py:247
  24.2 41.0 %collective-permute-start.10 = (f32[16,96,128]{2,1,0:T(8,128)S(1)}, f32[16,96,128]{2,1,0:T(8,128)S(1)}, u32[]{:S(2)}, u32[]{:S(2)}) collective-permute-start(f32[16,96,128]{2,1,0:T(8,128)S(1)} %get-tuple-element.55.refs_2_.refs_3_), channel_id=1, source_target_pairs={{0,16},{16,32},{32,48},{48,0},{1,17},{17,33},{33,49},{49,1},{2,18}... | collective-permute-start | bytes 2359304 | tf_op jit(solution)/shard_map/ppermute | solution.py:246
  24.2 28.1 %collective-permute-start.4 = (f32[16,32,128]{2,1,0:T(8,128)S(1)}, f32[16,32,128]{2,1,0:T(8,128)S(1)}, u32[]{:S(2)}, u32[]{:S(2)}) collective-permute-start(f32[16,32,128]{2,1,0:T(8,128)S(1)} %get-tuple-element.49), channel_id=1, source_target_pairs={{0,16},{16,32},{32,48},{48,0},{1,17},{17,33},{33,49},{49,1},{2,18}... | collective-permute-start | bytes 786440 | tf_op jit(solution)/shard_map/ppermute | solution.py:246
  24.8 27.6 %collective-permute-start.5 = (f32[16,32,128]{2,1,0:T(8,128)S(1)}, f32[16,32,128]{2,1,0:T(8,128)S(1)}, u32[]{:S(2)}, u32[]{:S(2)}) collective-permute-start(f32[16,32,128]{2,1,0:T(8,128)S(1)} %get-tuple-element.50), channel_id=1, source_target_pairs={{16,0},{32,16},{48,32},{0,48},{17,1},{33,17},{49,33},{1,49},{18,2}... | collective-permute-start | bytes 786440 | tf_op jit(solution)/shard_map/ppermute | solution.py:247
  26.0 10.6 %collective-permute-start.6 = (f32[4,16,128]{2,1,0:T(8,128)S(1)}, f32[4,16,128]{2,1,0:T(8,128)S(1)}, u32[]{:S(2)}, u32[]{:S(2)}) collective-permute-start(f32[4,16,128]{2,1,0:T(8,128)S(1)} %get-tuple-element.51), channel_id=1, source_target_pairs={{0,3},{1,2},{2,1},{3,0},{4,7},{5,6},{6,5},{7,4},{8,11},{9,10},{10,... | collective-permute-start | bytes 98312 | tf_op jit(solution)/shard_map/ppermute | solution.py:261
  36.6 15.8 %collective-permute-start.7 = (f32[4,16,128]{2,1,0:T(8,128)S(1)}, f32[4,16,128]{2,1,0:T(8,128)S(1)}, u32[]{:S(2)}, u32[]{:S(2)}) collective-permute-start(f32[4,16,128]{2,1,0:T(8,128)S(1)} %get-tuple-element.52), channel_id=1, source_target_pairs={{0,1},{1,0},{2,3},{3,2},{4,5},{5,4},{6,7},{7,6},{8,9},{9,8},{10,11... | collective-permute-start | bytes 98312 | tf_op jit(solution)/shard_map/ppermute | solution.py:261
  53.4 9.6 %collective-permute-start.8 = (f32[4,128,128]{2,1,0:T(8,128)S(1)}, f32[4,128,128]{2,1,0:T(8,128)S(1)}, u32[]{:S(2)}, u32[]{:S(2)}) collective-permute-start(f32[4,128,128]{2,1,0:T(8,128)S(1)} %get-tuple-element.58), channel_id=1, source_target_pairs={{0,4},{4,8},{8,12},{12,0},{1,5},{5,9},{9,13},{13,1},{2,6},{6,10},{... | collective-permute-start | bytes 786440 | tf_op jit(solution)/shard_map/ppermute | solution.py:246
  54.9 8.1 %collective-permute-start.9 = (f32[4,128,128]{2,1,0:T(8,128)S(1)}, f32[4,128,128]{2,1,0:T(8,128)S(1)}, u32[]{:S(2)}, u32[]{:S(2)}) collective-permute-start(f32[4,128,128]{2,1,0:T(8,128)S(1)} %get-tuple-element.59), channel_id=1, source_target_pairs={{4,0},{8,4},{12,8},{0,12},{5,1},{9,5},{13,9},{1,13},{6,2},{10,6},{... | collective-permute-start | bytes 786440 | tf_op jit(solution)/shard_map/ppermute | solution.py:247
  56.7 17.0 %collective-permute-start.13 = (f32[16,32,128]{2,1,0:T(8,128)S(1)}, f32[16,32,128]{2,1,0:T(8,128)S(1)}, u32[]{:S(2)}, u32[]{:S(2)}) collective-permute-start(f32[16,32,128]{2,1,0:T(8,128)S(1)} %get-tuple-element.53.refs_1_), channel_id=1, source_target_pairs={{16,0},{32,16},{48,32},{0,48},{17,1},{33,17},{49,33},{1,49},{18,2}... | collective-permute-start | bytes 786440 | tf_op jit(solution)/shard_map/ppermute | solution.py:247
  63.0 13.7 %collective-permute-start.12 = (f32[16,32,128]{2,1,0:T(8,128)S(1)}, f32[16,32,128]{2,1,0:T(8,128)S(1)}, u32[]{:S(2)}, u32[]{:S(2)}) collective-permute-start(f32[16,32,128]{2,1,0:T(8,128)S(1)} %get-tuple-element.56.refs_3_.refs_4_), channel_id=1, source_target_pairs={{0,16},{16,32},{32,48},{48,0},{1,17},{17,33},{33,49},{49,1},{2,18}... | collective-permute-start | bytes 786440 | tf_op jit(solution)/shard_map/ppermute | solution.py:246
  65.5 46.8 %collective-permute-start.19 = (f32[16,96,128]{2,1,0:T(8,128)S(1)}, f32[16,96,128]{2,1,0:T(8,128)S(1)}, u32[]{:S(2)}, u32[]{:S(2)}) collective-permute-start(f32[16,96,128]{2,1,0:T(8,128)S(1)} %get-tuple-element.62.refs_0_), channel_id=1, source_target_pairs={{16,0},{32,16},{48,32},{0,48},{17,1},{33,17},{49,33},{1,49},{18,2}... | collective-permute-start | bytes 2359304 | tf_op jit(solution)/shard_map/ppermute | solution.py:247
  67.4 45.0 %collective-permute-start.18 = (f32[16,96,128]{2,1,0:T(8,128)S(1)}, f32[16,96,128]{2,1,0:T(8,128)S(1)}, u32[]{:S(2)}, u32[]{:S(2)}) collective-permute-start(f32[16,96,128]{2,1,0:T(8,128)S(1)} %get-tuple-element.67.refs_2_.refs_3_), channel_id=1, source_target_pairs={{0,16},{16,32},{32,48},{48,0},{1,17},{17,33},{33,49},{49,1},{2,18}... | collective-permute-start | bytes 2359304 | tf_op jit(solution)/shard_map/ppermute | solution.py:246
  67.4 10.2 %collective-permute-start.14 = (f32[4,16,128]{2,1,0:T(8,128)S(1)}, f32[4,16,128]{2,1,0:T(8,128)S(1)}, u32[]{:S(2)}, u32[]{:S(2)}) collective-permute-start(f32[4,16,128]{2,1,0:T(8,128)S(1)} %get-tuple-element.63), channel_id=1, source_target_pairs={{0,3},{1,2},{2,1},{3,0},{4,7},{5,6},{6,5},{7,4},{8,11},{9,10},{10,... | collective-permute-start | bytes 98312 | tf_op jit(solution)/shard_map/ppermute | solution.py:261
  73.6 13.6 %collective-permute-start.15 = (f32[4,16,128]{2,1,0:T(8,128)S(1)}, f32[4,16,128]{2,1,0:T(8,128)S(1)}, u32[]{:S(2)}, u32[]{:S(2)}) collective-permute-start(f32[4,16,128]{2,1,0:T(8,128)S(1)} %get-tuple-element.64), channel_id=1, source_target_pairs={{0,1},{1,0},{2,3},{3,2},{4,5},{5,4},{6,7},{7,6},{8,9},{9,8},{10,11... | collective-permute-start | bytes 98312 | tf_op jit(solution)/shard_map/ppermute | solution.py:261
  87.5 4.4 %collective-permute-start.21 = (f32[16,32,128]{2,1,0:T(8,128)S(1)}, f32[16,32,128]{2,1,0:T(8,128)S(1)}, u32[]{:S(2)}, u32[]{:S(2)}) collective-permute-start(f32[16,32,128]{2,1,0:T(8,128)S(1)} %get-tuple-element.65.refs_1_), channel_id=1, source_target_pairs={{16,0},{32,16},{48,32},{0,48},{17,1},{33,17},{49,33},{1,49},{18,2}... | collective-permute-start | bytes 786440 | tf_op jit(solution)/shard_map/ppermute | solution.py:247
  88.6 9.7 %collective-permute-start.16 = (f32[4,128,128]{2,1,0:T(8,128)S(1)}, f32[4,128,128]{2,1,0:T(8,128)S(1)}, u32[]{:S(2)}, u32[]{:S(2)}) collective-permute-start(f32[4,128,128]{2,1,0:T(8,128)S(1)} %get-tuple-element.70), channel_id=1, source_target_pairs={{0,4},{4,8},{8,12},{12,0},{1,5},{5,9},{9,13},{13,1},{2,6},{6,10},{... | collective-permute-start | bytes 786440 | tf_op jit(solution)/shard_map/ppermute | solution.py:246
  88.9 18.0 %collective-permute-start.17 = (f32[4,128,128]{2,1,0:T(8,128)S(1)}, f32[4,128,128]{2,1,0:T(8,128)S(1)}, u32[]{:S(2)}, u32[]{:S(2)}) collective-permute-start(f32[4,128,128]{2,1,0:T(8,128)S(1)} %get-tuple-element.71), channel_id=1, source_target_pairs={{4,0},{8,4},{12,8},{0,12},{5,1},{9,5},{13,9},{1,13},{6,2},{10,6},{... | collective-permute-start | bytes 786440 | tf_op jit(solution)/shard_map/ppermute | solution.py:247
  91.9 18.9 %collective-permute-start.20 = (f32[16,32,128]{2,1,0:T(8,128)S(1)}, f32[16,32,128]{2,1,0:T(8,128)S(1)}, u32[]{:S(2)}, u32[]{:S(2)}) collective-permute-start(f32[16,32,128]{2,1,0:T(8,128)S(1)} %get-tuple-element.68.refs_3_.refs_4_), channel_id=1, source_target_pairs={{0,16},{16,32},{32,48},{48,0},{1,17},{17,33},{33,49},{49,1},{2,18}... | collective-permute-start | bytes 786440 | tf_op jit(solution)/shard_map/ppermute | solution.py:246
  98.3 12.5 %collective-permute-start.22 = (f32[4,16,128]{2,1,0:T(8,128)S(1)}, f32[4,16,128]{2,1,0:T(8,128)S(1)}, u32[]{:S(2)}, u32[]{:S(2)}) collective-permute-start(f32[4,16,128]{2,1,0:T(8,128)S(1)} %get-tuple-element.76), channel_id=1, source_target_pairs={{0,3},{1,2},{2,1},{3,0},{4,7},{5,6},{6,5},{7,4},{8,11},{9,10},{10,... | collective-permute-start | bytes 98312 | tf_op jit(solution)/shard_map/ppermute | solution.py:261
  106.9 5.4 %collective-permute-start.23 = (f32[4,16,128]{2,1,0:T(8,128)S(1)}, f32[4,16,128]{2,1,0:T(8,128)S(1)}, u32[]{:S(2)}, u32[]{:S(2)}) collective-permute-start(f32[4,16,128]{2,1,0:T(8,128)S(1)} %get-tuple-element.77), channel_id=1, source_target_pairs={{0,1},{1,0},{2,3},{3,2},{4,5},{5,4},{6,7},{7,6},{8,9},{9,8},{10,11... | collective-permute-start | bytes 98312 | tf_op jit(solution)/shard_map/ppermute | solution.py:261
  113.7 5.9 %collective-permute-start.24 = (f32[2,4,16,128]{3,2,1,0:T(8,128)S(1)}, f32[2,4,16,128]{3,2,1,0:T(8,128)S(1)}, u32[]{:S(2)}, u32[]{:S(2)}) collective-permute-start(f32[2,4,16,128]{3,2,1,0:T(8,128)S(1)} %get-tuple-element.81), channel_id=1, source_target_pairs={{0,1},{1,0},{2,3},{3,2},{4,5},{5,4},{6,7},{7,6},{8,9},{9,8},{10,11... | collective-permute-start | bytes 196616 | tf_op jit(solution)/shard_map/ppermute | solution.py:286
  119.5 8.3 %collective-permute-start.25 = (f32[2,4,16,128]{3,2,1,0:T(8,128)S(1)}, f32[2,4,16,128]{3,2,1,0:T(8,128)S(1)}, u32[]{:S(2)}, u32[]{:S(2)}) collective-permute-start(f32[2,4,16,128]{3,2,1,0:T(8,128)S(1)} %pad_maximum_fusion.mine), channel_id=1, source_target_pairs={{0,2},{1,3},{2,0},{3,1},{4,6},{5,7},{6,4},{7,5},{8,10},{9,11},{10,... | collective-permute-start | bytes 196616 | tf_op jit(solution)/shard_map/ppermute | solution.py:289

commit v3 on v2

--- a/solution.py
+++ b/solution.py
@@ -88,15 +88,19 @@
     return jnp.where(even, across, beside), jnp.where(even, beside, across)
 
 
-def inner_kernel(first_in, last_in, mobility, low_y, high_y, first, last):
+def inner_kernel(first_in, last_in, mobility, low_y, high_y, first, last, *stats):
     top = mobility.shape[0] - 1
     rim = (mobility.shape[2] - first.shape[1]) // 2
     inside = slice(rim, mobility.shape[2] - rim)
 
     @pl.loop(0, first.shape[0])
     def _(x):
-        first[x] = first_in[x, inside] + mobility[0, x, inside] * low_y[x]
-        last[x] = last_in[x, inside] + mobility[top, x, inside] * high_y[x]
+        ends = ((0, first_in, first, low_y), (top, last_in, last, high_y))
+        for i, (r, row_in, row, beside) in enumerate(ends):
+            value = row_in[x, inside] + mobility[r, x, inside] * beside[x]
+            row[x] = value
+            for part in stats:
+                part[0, i, pl.ds(x, 1)], part[1, i, pl.ds(x, 1)] = line_stats(value)
 
 
 def add_outer(row_in, row, mobility, beside, r, x):
@@ -144,16 +148,6 @@
     take_edges(rows_of((*ends[:2], middle, *ends[2:])), *edges)
 
 
-def take_inner_kernel(tracer, first, last):
-    rim = (tracer.shape[2] - first.shape[1]) // 2
-    inside = slice(rim, tracer.shape[2] - rim)
-
-    @pl.loop(0, first.shape[0])
-    def _(x):
-        first[x] = tracer[0, x, inside]
-        last[x] = tracer[tracer.shape[0] - 1, x, inside]
-
-
 def take_outer_kernel(tracer, first, last, *edges):
     rim, depth = (first.shape[1] // 2, tracer.shape[2])
 
@@ -166,21 +160,19 @@
     take_edges(rows_of((tracer,)), *edges)
 
 
-def last_kernel(first_in, middle_in, last_in, middle_stats, mobility, *refs):
-    low_inner, high_inner, low_outer, high_outer, far, near, first, middle, last, stats = refs
-    top = mobility.shape[0] - 1
-    width, depth, _ = first_in.shape
+def joined(one, other, count, other_count):
+    away, share = (other[0] - one[0], other_count / (count + other_count))
+    return one[0] + share * away, one[1] + other[1] + (count * share) * (away * away)
+
+
+def middle_kernel(middle_in, stats_in, mobility, far, near, middle, stats):
+    width, depth = mobility.shape[1:3]
 
     @pl.loop(0, width)
     def _(x):
-        low_y, high_y = ((low_inner, low_outer), (high_inner, high_outer))
-        for r, row_in, row, beside in ((0, first_in, first, low_y), (top, last_in, last, high_y)):
-            row[x] = row_in[x] + mobility[r, x] * plane_of(beside, x)
-            add_lines(row, mobility, far, near, r, x)
-            stats[0, r, pl.ds(x, 1)], stats[1, r, pl.ds(x, 1)] = line_stats(row[x])
-        for r in range(1, top):
+        for r in range(1, mobility.shape[0] - 1):
             row = middle.at[r - 1]
-            mean = middle_stats[0, r - 1, pl.ds(x, 1)]
+            mean = stats_in[0, r - 1, pl.ds(x, 1)]
             more = squares = 0.0
             for z, line in zip((0, depth - 1), sides_of(far, near, r, x)):
                 old = row[x, z : z + 1]
@@ -189,38 +181,56 @@
                 more += added
                 squares += added * (2.0 * (old - mean) + added)
             shift = more * (1.0 / depth)
-            stats[0, r, pl.ds(x, 1)] = mean + shift
-            stats[1, r, pl.ds(x, 1)] = middle_stats[1, r - 1, pl.ds(x, 1)] + (squares - more * shift)
-
-
-def store_kernel(first, middle, last, out, sems):
-    top = out.shape[0] - 1
-    copies = [
-        pltpu.make_async_copy(first, out.at[0], sems.at[0]),
-        pltpu.make_async_copy(middle, out.at[1:top], sems.at[1]),
-        pltpu.make_async_copy(last, out.at[top], sems.at[2]),
-    ]
+            stats[0, r - 1, pl.ds(x, 1)] = mean + shift
+            stats[1, r - 1, pl.ds(x, 1)] = stats_in[1, r - 1, pl.ds(x, 1)] + (squares - more * shift)
+
+
+def last_kernel(first_in, last_in, inner_stats, mobility, *refs):
+    low_outer, high_outer, far, near, first, last, stats = refs
+    top = mobility.shape[0] - 1
+    width, depth, _ = first_in.shape
+    count = first.shape[1]
+
+    @pl.loop(0, width, unroll=8)
+    def _(x):
+        ends = ((0, first_in, first, low_outer), (top, last_in, last, high_outer))
+        for i, (r, row_in, row, beside) in enumerate(ends):
+            add_outer(row_in, row, mobility, beside, r, x)
+            add_lines(row, mobility, far, near, r, x)
+            inner = (inner_stats[0, i, pl.ds(x, 1)], inner_stats[1, i, pl.ds(x, 1)])
+            stats[0, i, pl.ds(x, 1)], stats[1, i, pl.ds(x, 1)] = joined(
+                inner, line_stats(row[x]), depth - count, count
+            )
+
+
+def store_kernel(first_inner, first_outer, middle, last_inner, last_outer, out, sems):
+    top, depth, rim = (out.shape[0] - 1, out.shape[2], first_outer.shape[1] // 2)
+    pairs = [(middle, out.at[pl.ds(1, top - 1)])]
+    for r, inner, outer in ((0, first_inner, first_outer), (top, last_inner, last_outer)):
+        pairs.append((inner, out.at[r, :, pl.ds(rim, depth - 2 * rim)]))
+        pairs.append((outer.at[:, pl.ds(0, rim)], out.at[r, :, pl.ds(0, rim)]))
+        pairs.append((outer.at[:, pl.ds(rim, rim)], out.at[r, :, pl.ds(depth - rim, rim)]))
+    copies = [pltpu.make_async_copy(*pair, sems.at[i]) for i, pair in enumerate(pairs)]
     for copy in copies:
         copy.start()
     for copy in copies:
         copy.wait()
 
 
-def merged(mine, other, count):
-    away = mine[0] - other[0]
-    return 0.5 * (mine[0] + other[0]), mine[1] + other[1] + (0.5 * count) * (away * away)
-
-
-def scale_kernel(count, first, middle, last, mine, other, out, held, sems):
+def scale_kernel(count, *refs):
+    *rows, mine, other, out, held, sems = refs
+    width = held.shape[1]
+    share = width * held.shape[0] // sems.shape[0]
     copies = []
-    rows = [first] + [middle.at[r] for r in range(middle.shape[0])] + [last]
-    for r, row in enumerate(rows):
-        mean, squares = merged((mine[0, r], mine[1, r]), (other[0, r], other[1, r]), count)
+    for r, row in enumerate(rows_of(rows)):
+        mean, squares = joined((mine[0, r], mine[1, r]), (other[0, r], other[1, r]), count, count)
         scale = lax.rsqrt(squares * (1.0 / (2 * count)) + 0.0001)
-        for x in range(row.shape[0]):
-            held[r, x] = (row[x] - mean[x : x + 1]) * scale[x : x + 1]
-        copies.append(pltpu.make_async_copy(held.at[r], out.at[r], sems.at[r]))
-        copies[-1].start()
+        for x in range(width):
+            held[r, x] = (plane_of(row, x) - mean[x : x + 1]) * scale[x : x + 1]
+            if (x + 1) % share == 0:
+                planes = pl.ds(x + 1 - share, share)
+                copies.append(pltpu.make_async_copy(held.at[r, planes], out.at[r, planes], sems.at[len(copies)]))
+                copies[-1].start()
     for copy in copies:
         copy.wait()
 
@@ -250,7 +260,7 @@
     def call(kernel, *out_shape, **options):
         return kernel_call(kernel, *out_shape, **options)
 
-    inners = call(take_inner_kernel, inner, inner)(tracer)
+    inners = (tracer[0, :, RIM : depth - RIM], tracer[-1, :, RIM : depth - RIM])
     inners_y = swap(*inners, "south")
     first, last, *edges = call(take_outer_kernel, outer, outer, *edge_shapes)(tracer)
     pieces = (tracer,)
@@ -264,8 +274,12 @@
         first, inside, last, *stats = call(
             functools.partial(partial_kernel, len(pieces), final), row, middle, row, *stats
         )(*pieces, mobility, source, *along_x)
+        end_stats = (f32(2, 2, width, levels),) if final else ()
+        *inners, end_stats = (
+            *call(inner_kernel, inner, inner, *end_stats)(first, last, mobility, *inners_y),
+            *(() if final else (None,)),
+        )
         if not final:
-            inners = call(inner_kernel, inner, inner)(first, last, mobility, *inners_y)
             inners_y_next = swap(*inners, "south")
             outers = call(outer_kernel, outer, outer)(first, last, mobility, *outers_y, *along_z)
             inside, *edges = call(
@@ -273,25 +287,30 @@
             )(inside, inners[0], outers[0], inners[1], outers[1], mobility, *along_z)
             pieces = (inners[0], outers[0], inside, inners[1], outers[1])
             inners_y = inners_y_next
-    *rows, mine = kernel_call(
-        last_kernel, row, middle, row, f32(2, count, width, levels), input_output_aliases={1: 1}
-    )(first, inside, last, *stats, mobility, *inners_y, *outers_y, *along_z)
-    (stored,) = kernel_call(
+    inside, middle_stats = call(
+        middle_kernel, middle, f32(2, count - 2, width, levels), input_output_aliases={0: 0}
+    )(inside, *stats, mobility, *along_z)
+    *outers, mine = call(last_kernel, outer, outer, f32(2, 2, width, levels))(
+        first, last, end_stats, mobility, *outers_y, *along_z
+    )
+    mine = jnp.concatenate([mine[:, :1], middle_stats, mine[:, 1:]], axis=1)
+    rows = (inners[0], outers[0], inside, inners[1], outers[1])
+    (stored,) = call(
         store_kernel,
         f32(count, width, depth, levels),
         out_specs=(pl.BlockSpec(memory_space=pl.ANY),),
-        scratch_shapes=[pltpu.SemaphoreType.DMA((3,))],
+        scratch_shapes=[pltpu.SemaphoreType.DMA((7,))],
     )(*rows)
     members = depth
     other = lax.ppermute(mine, "down", near)
-    mine = jnp.stack(merged(mine, other, members))
+    mine = jnp.stack(joined(mine, other, members, members))
     members *= 2
     other = lax.ppermute(mine, "down", [(i, (i + 2) % peers) for i in range(peers)])
-    (standardized,) = kernel_call(
+    (standardized,) = call(
         functools.partial(scale_kernel, members),
         f32(count, width, depth, levels),
         out_specs=(pl.BlockSpec(memory_space=pl.ANY),),
-        scratch_shapes=[pltpu.VMEM((count, width, depth, levels), jnp.float32), pltpu.SemaphoreType.DMA((count,))],
+        scratch_shapes=[pltpu.VMEM((count, width, depth, levels), jnp.float32), pltpu.SemaphoreType.DMA((2 * count,))],
     )(*rows, mine, other)
     return (standardized, stored)
 

time: 130 us -> 131 us (level)
  waiting for transfers between devices: 56.9 us -> 52.6 us
  local copies, waits for them, and re-layouts: 2.19 us -> 6.02 us
    ppermute x9, waiting for transfers between devices: 20.7 us -> 14.3 us  [swap(): low = lax.ppermute(last, axis, up)]
    ppermute x1, starting transfers between devices: 2.63 us -> 6.03 us  [body(): lax.ppermute(mine, 'down', [(i, (i + 2) % peers) for i in range(peers)])]
    ppermute x1, waiting for transfers between devices: 3.59 us -> 0.89 us  [body(): lax.ppermute(mine, 'down', [(i, (i + 2) % peers) for i in range(peers)])]
    ppermute x3, waiting for transfers between devices: 24.3 us -> 26.8 us  [body(): lax.ppermute(edges[3], 'down', near)]
    ppermute x3, waiting for transfers between devices: 2.96 us -> 5.16 us  [body(): lax.ppermute(edges[2], 'down', far)]
    unnamed x6 -> x8, local copies, waits for them, and re-layouts: 2.19 us -> 4.39 us
    ppermute x3, starting transfers between devices: 6.26 us -> 8.33 us  [body(): lax.ppermute(edges[3], 'down', near)]
    ppermute x9, starting transfers between devices: 6.22 us -> 4.57 us  [swap(): low = lax.ppermute(last, axis, up)]
where the time goes in v3:
time: 131 us
  starting transfers between devices  54.7 us (42%)
  waiting for transfers between devices  52.6 us (40%)
  Pallas kernels  16.4 us (13%)
  local copies, waits for them, and re-layouts  6.02 us (5%)
    ppermute x3, waiting for transfers between devices, body(): lax.ppermute(edges[3], 'down', near)  26.8 us
    ppermute x3, starting transfers between devices, body(): lax.ppermute(edges[2], 'down', far)  22.9 us
    ppermute x9, waiting for transfers between devices, swap(): low = lax.ppermute(last, axis, up)  14.3 us
    ppermute x9, starting transfers between devices, swap(): high = lax.ppermute(leading, axis, [(b, a) for a, b in up])  11.9 us
    ppermute x3, starting transfers between devices, body(): lax.ppermute(edges[3], 'down', near)  8.33 us
    pallas_call x3, Pallas kernels, body(): call(functools.partial(partial_kernel, len(pieces), final), row, middle,...  7.76 us
    ppermute x1, starting transfers between devices, body(): lax.ppermute(mine, 'down', [(i, (i + 2) % peers) for i in range(peers)])  6.03 us
    ppermute x3, waiting for transfers between devices, body(): lax.ppermute(edges[2], 'down', far)  5.16 us
  transfers between devices with their start and end apart: 26, of which 12 were waited for; matrix products, arithmetic and copies ran while one was open for 0% of the time, Pallas kernels for 10%

profile of v3, /device:TPU:32, one launch (start us, length us, event | category | flops | bytes accessed | tf_op | source)
XLA Modules:
  0.0 130.7 jit_solution(10634739373092940931)
XLA Ops:
  0.6 1.6 %slice_bitcast_fusion = (f32[16,96,128]{2,1,0:T(8,128)S(1)}, f32[16,96,128]{2,1,0:T(8,128)S(1)}) fusion(f32[4,16,128,128]{3,2,1,0:T(8,128)} %refs_0_.1), kind=kLoop, calls=%fused_computation | loop fusion | bytes 3145728 | tf_op jit(solution)/shard_map/squeeze | solution.py:263
  2.3 1.1 collective-permute-start.3
  3.4 0.0 collective-permute-start.2
  3.4 2.2 %copy-done.3 = f32[4,16,128,128]{3,2,1,0:T(8,128)S(1)} copy-done((f32[4,16,128,128]{3,2,1,0:T(8,128)S(1)}, f32[4,16,128,128]{3,2,1,0:T(8,128)}, u32[]{:S(2)}) %copy-start.3) | copy-done | bytes 4194328
  5.6 0.5 shard_map.50
  6.1 1.6 %collective-permute-start = (f32[4,128,128]{2,1,0:T(8,128)S(1)}, f32[4,128,128]{2,1,0:T(8,128)S(1)}, u32[]{:S(2)}, u32[]{:S(2)}) collective-permute-start(f32[4,128,128]{2,1,0:T(8,128)S(1)} %get-tuple-element.44), channel_id=1, source_target_pairs={{0,4},{4,8},{8,12},{12,0},{1,5},{5,9},{9,13},{13,1},{2,6},{6,10},{... | collective-permute-start | bytes 786440 | tf_op jit(solution)/shard_map/ppermute | solution.py:256
  7.7 1.7 %collective-permute-start.1 = (f32[4,128,128]{2,1,0:T(8,128)S(1)}, f32[4,128,128]{2,1,0:T(8,128)S(1)}, u32[]{:S(2)}, u32[]{:S(2)}) collective-permute-start(f32[4,128,128]{2,1,0:T(8,128)S(1)} %get-tuple-element.45), channel_id=1, source_target_pairs={{4,0},{8,4},{12,8},{0,12},{5,1},{9,5},{13,9},{1,13},{6,2},{10,6},{... | collective-permute-start | bytes 786440 | tf_op jit(solution)/shard_map/ppermute | solution.py:257
  9.4 6.9 %collective-permute-done.refs_3_ = f32[4,128,128]{2,1,0:T(8,128)S(1)} collective-permute-done((f32[4,128,128]{2,1,0:T(8,128)S(1)}, f32[4,128,128]{2,1,0:T(8,128)S(1)}, u32[]{:S(2)}, u32[]{:S(2)}) %collective-permute-start) | collective-permute-done | bytes 262176 | tf_op jit(solution)/shard_map/ppermute | solution.py:256
  16.4 2.2 %copy-done.1 = f32[4,16,128,128]{3,2,1,0:T(8,128)S(1)} copy-done((f32[4,16,128,128]{3,2,1,0:T(8,128)S(1)}, f32[4,16,128,128]{3,2,1,0:T(8,128)}, u32[]{:S(2)}) %copy-start.1) | copy-done | bytes 4194328
  18.6 2.3 %shard_map.51 = (f32[16,128,128]{2,1,0:T(8,128)S(1)}, f32[2,16,128,128]{3,2,1,0:T(8,128)S(1)}, f32[16,128,128]{2,1,0:T(8,128)S(1)}) custom-call(f32[4,16,128,128]{3,2,1,0:T(8,128)S(1)} %copy-done.3, f32[4,16,128,128]{3,2,1,0:T(8,128)S(1)} %copy-done, f32[4,16,128,128]{3,2,1,0:T(8,128)S(1)} %copy-done.1, f32[4,128,128]{2,1,0:T(8,128)S(1)} %collective-permute-done.refs_3_, ...), custom_call_target="tpu_custom_call" | custom-call | tf_op jit(solution)/shard_map/pallas_call | solution.py:274
  20.8 0.4 collective-permute-done.3.high_y
  21.2 1.1 collective-permute-done.2.low_y
  22.3 0.3 shard_map.52
  22.6 1.2 collective-permute-start.11
  23.8 0.6 collective-permute-start.4
  24.3 1.2 collective-permute-start.5
  25.6 8.5 %collective-permute-start.6 = (f32[4,16,128]{2,1,0:T(8,128)S(1)}, f32[4,16,128]{2,1,0:T(8,128)S(1)}, u32[]{:S(2)}, u32[]{:S(2)}) collective-permute-start(f32[4,16,128]{2,1,0:T(8,128)S(1)} %get-tuple-element.51), channel_id=1, source_target_pairs={{0,3},{1,2},{2,1},{3,0},{4,7},{5,6},{6,5},{7,4},{8,11},{9,10},{10,... | collective-permute-start | bytes 98312 | tf_op jit(solution)/shard_map/ppermute | solution.py:271
  34.1 2.0 %collective-permute-done.6.far.refs_5_ = f32[4,16,128]{2,1,0:T(8,128)S(1)} collective-permute-done((f32[4,16,128]{2,1,0:T(8,128)S(1)}, f32[4,16,128]{2,1,0:T(8,128)S(1)}, u32[]{:S(2)}, u32[]{:S(2)}) %collective-permute-start.6) | collective-permute-done | bytes 32800 | tf_op jit(solution)/shard_map/ppermute | solution.py:271
  36.1 2.6 %collective-permute-start.7 = (f32[4,16,128]{2,1,0:T(8,128)S(1)}, f32[4,16,128]{2,1,0:T(8,128)S(1)}, u32[]{:S(2)}, u32[]{:S(2)}) collective-permute-start(f32[4,16,128]{2,1,0:T(8,128)S(1)} %get-tuple-element.52), channel_id=1, source_target_pairs={{0,1},{1,0},{2,3},{3,2},{4,5},{5,4},{6,7},{7,6},{8,9},{9,8},{10,11... | collective-permute-start | bytes 98312 | tf_op jit(solution)/shard_map/ppermute | solution.py:271
  38.7 13.3 %collective-permute-done.7.near.refs_6_ = f32[4,16,128]{2,1,0:T(8,128)S(1)} collective-permute-done((f32[4,16,128]{2,1,0:T(8,128)S(1)}, f32[4,16,128]{2,1,0:T(8,128)S(1)}, u32[]{:S(2)}, u32[]{:S(2)}) %collective-permute-start.7) | collective-permute-done | bytes 32800 | tf_op jit(solution)/shard_map/ppermute | solution.py:271
  52.0 0.0 collective-permute-done.4.low_y
  52.0 0.0 collective-permute-done.5.high_y
  52.0 0.3 shard_map.53
  52.2 0.0 copy-start.2
  52.3 0.7 shard_map.54
  53.0 1.6 %collective-permute-start.8 = (f32[4,128,128]{2,1,0:T(8,128)S(1)}, f32[4,128,128]{2,1,0:T(8,128)S(1)}, u32[]{:S(2)}, u32[]{:S(2)}) collective-permute-start(f32[4,128,128]{2,1,0:T(8,128)S(1)} %get-tuple-element.58), channel_id=1, source_target_pairs={{0,4},{4,8},{8,12},{12,0},{1,5},{5,9},{9,13},{13,1},{2,6},{6,10},{... | collective-permute-start | bytes 786440 | tf_op jit(solution)/shard_map/ppermute | solution.py:256
  54.5 1.7 %collective-permute-start.9 = (f32[4,128,128]{2,1,0:T(8,128)S(1)}, f32[4,128,128]{2,1,0:T(8,128)S(1)}, u32[]{:S(2)}, u32[]{:S(2)}) collective-permute-start(f32[4,128,128]{2,1,0:T(8,128)S(1)} %get-tuple-element.59), channel_id=1, source_target_pairs={{4,0},{8,4},{12,8},{0,12},{5,1},{9,5},{13,9},{1,13},{6,2},{10,6},{... | collective-permute-start | bytes 786440 | tf_op jit(solution)/shard_map/ppermute | solution.py:257
  56.3 0.0 collective-permute-start.13
  56.3 6.3 %collective-permute-done.8.refs_7_ = f32[4,128,128]{2,1,0:T(8,128)S(1)} collective-permute-done((f32[4,128,128]{2,1,0:T(8,128)S(1)}, f32[4,128,128]{2,1,0:T(8,128)S(1)}, u32[]{:S(2)}, u32[]{:S(2)}) %collective-permute-start.8) | collective-permute-done | bytes 262176 | tf_op jit(solution)/shard_map/ppermute | solution.py:256
  62.5 0.0 collective-permute-start.12
  62.5 0.0 collective-permute-done.9.refs_8_
  62.6 2.3 %shard_map.55 = (f32[16,128,128]{2,1,0:T(8,128)S(1)}, f32[2,16,128,128]{3,2,1,0:T(8,128)S(1)}, f32[16,128,128]{2,1,0:T(8,128)S(1)}) custom-call(f32[16,96,128]{2,1,0:T(8,128)S(1)} %get-tuple-element.48.refs_0_, f32[16,32,128]{2,1,0:T(8,128)S(1)} %get-tuple-element.53.refs_1_, f32[2,16,128,128]{3,2,1,0:T(8,128)S(1)} %get-tuple-element.57.refs_2_, ...), custom_call_target="tpu_custom_call" | custom-call | tf_op jit(solution)/shard_map/pallas_call | solution.py:274
  64.8 0.0 collective-permute-done.11.high_y
  64.8 0.0 collective-permute-done.10.low_y
  64.8 0.3 shard_map.56
  65.1 2.0 %collective-permute-start.19 = (f32[16,96,128]{2,1,0:T(8,128)S(1)}, f32[16,96,128]{2,1,0:T(8,128)S(1)}, u32[]{:S(2)}, u32[]{:S(2)}) collective-permute-start(f32[16,96,128]{2,1,0:T(8,128)S(1)} %get-tuple-element.62.refs_0_), channel_id=1, source_target_pairs={{16,0},{32,16},{48,32},{0,48},{17,1},{33,17},{49,33},{1,49},{18,2}... | collective-permute-start | bytes 2359304 | tf_op jit(solution)/shard_map/ppermute | solution.py:257
  67.1 0.0 collective-permute-start.18
  67.1 6.3 %collective-permute-start.14 = (f32[4,16,128]{2,1,0:T(8,128)S(1)}, f32[4,16,128]{2,1,0:T(8,128)S(1)}, u32[]{:S(2)}, u32[]{:S(2)}) collective-permute-start(f32[4,16,128]{2,1,0:T(8,128)S(1)} %get-tuple-element.63), channel_id=1, source_target_pairs={{0,3},{1,2},{2,1},{3,0},{4,7},{5,6},{6,5},{7,4},{8,11},{9,10},{10,... | collective-permute-start | bytes 98312 | tf_op jit(solution)/shard_map/ppermute | solution.py:271
  73.4 0.0 collective-permute-done.13.high_y
  73.4 3.0 %collective-permute-start.15 = (f32[4,16,128]{2,1,0:T(8,128)S(1)}, f32[4,16,128]{2,1,0:T(8,128)S(1)}, u32[]{:S(2)}, u32[]{:S(2)}) collective-permute-start(f32[4,16,128]{2,1,0:T(8,128)S(1)} %get-tuple-element.64), channel_id=1, source_target_pairs={{0,1},{1,0},{2,3},{3,2},{4,5},{5,4},{6,7},{7,6},{8,9},{9,8},{10,11... | collective-permute-start | bytes 98312 | tf_op jit(solution)/shard_map/ppermute | solution.py:271
  76.4 0.0 collective-permute-done.12.low_y
  76.4 1.1 collective-permute-done.14.far.refs_5_
  77.4 9.7 %collective-permute-done.15.near.refs_6_ = f32[4,16,128]{2,1,0:T(8,128)S(1)} collective-permute-done((f32[4,16,128]{2,1,0:T(8,128)S(1)}, f32[4,16,128]{2,1,0:T(8,128)S(1)}, u32[]{:S(2)}, u32[]{:S(2)}) %collective-permute-start.15) | collective-permute-done | bytes 32800 | tf_op jit(solution)/shard_map/ppermute | solution.py:271
  87.1 0.3 shard_map.57
  87.4 0.7 shard_map.58
  88.1 0.4 collective-permute-start.16
  88.4 3.0 %collective-permute-start.17 = (f32[4,128,128]{2,1,0:T(8,128)S(1)}, f32[4,128,128]{2,1,0:T(8,128)S(1)}, u32[]{:S(2)}, u32[]{:S(2)}) collective-permute-start(f32[4,128,128]{2,1,0:T(8,128)S(1)} %get-tuple-element.71), channel_id=1, source_target_pairs={{4,0},{8,4},{12,8},{0,12},{5,1},{9,5},{13,9},{1,13},{6,2},{10,6},{... | collective-permute-start | bytes 786440 | tf_op jit(solution)/shard_map/ppermute | solution.py:257
  91.4 8.1 %collective-permute-start.22 = (f32[4,16,128]{2,1,0:T(8,128)S(1)}, f32[4,16,128]{2,1,0:T(8,128)S(1)}, u32[]{:S(2)}, u32[]{:S(2)}) collective-permute-start(f32[4,16,128]{2,1,0:T(8,128)S(1)} %get-tuple-element.76), channel_id=1, source_target_pairs={{0,3},{1,2},{2,1},{3,0},{4,7},{5,6},{6,5},{7,4},{8,11},{9,10},{10,... | collective-permute-start | bytes 98312 | tf_op jit(solution)/shard_map/ppermute | solution.py:271
  99.5 2.1 %collective-permute-done.22.refs_2_.far = f32[4,16,128]{2,1,0:T(8,128)S(1)} collective-permute-done((f32[4,16,128]{2,1,0:T(8,128)S(1)}, f32[4,16,128]{2,1,0:T(8,128)S(1)}, u32[]{:S(2)}, u32[]{:S(2)}) %collective-permute-start.22) | collective-permute-done | bytes 32800 | tf_op jit(solution)/shard_map/ppermute | solution.py:271
  101.6 0.0 collective-permute-start.21
  101.6 0.0 collective-permute-done.16.refs_7_
  101.6 0.5 collective-permute-start.20
  102.1 2.7 %collective-permute-start.23 = (f32[4,16,128]{2,1,0:T(8,128)S(1)}, f32[4,16,128]{2,1,0:T(8,128)S(1)}, u32[]{:S(2)}, u32[]{:S(2)}) collective-permute-start(f32[4,16,128]{2,1,0:T(8,128)S(1)} %get-tuple-element.77), channel_id=1, source_target_pairs={{0,1},{1,0},{2,3},{3,2},{4,5},{5,4},{6,7},{7,6},{8,9},{9,8},{10,11... | collective-permute-start | bytes 98312 | tf_op jit(solution)/shard_map/ppermute | solution.py:271
  104.9 3.2 %shard_map.59 = (f32[16,128,128]{2,1,0:T(8,128)S(1)}, f32[2,16,128,128]{3,2,1,0:T(8,128)S(1)}, f32[16,128,128]{2,1,0:T(8,128)S(1)}, f32[2,2,16,128]{3,2,1,0:T(8,128)S(1)}) custom-call(f32[16,96,128]{2,1,0:T(8,128)S(1)} %get-tuple-element.62.refs_0_, f32[16,32,128]{2,1,0:T(8,128)S(1)} %get-tuple-element.65.refs_1_, ...), custom_call_target="tpu_custom_call" | custom-call | tf_op jit(solution)/shard_map/pallas_call | solution.py:274
  108.1 3.9 %collective-permute-done.23.refs_3_.near = f32[4,16,128]{2,1,0:T(8,128)S(1)} collective-permute-done((f32[4,16,128]{2,1,0:T(8,128)S(1)}, f32[4,16,128]{2,1,0:T(8,128)S(1)}, u32[]{:S(2)}, u32[]{:S(2)}) %collective-permute-start.23) | collective-permute-done | bytes 32800 | tf_op jit(solution)/shard_map/ppermute | solution.py:271
  112.1 0.3 shard_map.62
  112.4 0.8 shard_map.60
  113.2 0.3 shard_map.61
  113.6 0.9 collective-permute-start.24
  114.5 5.0 %collective-permute-done.24 = f32[2,4,16,128]{3,2,1,0:T(8,128)S(1)} collective-permute-done((f32[2,4,16,128]{3,2,1,0:T(8,128)S(1)}, f32[2,4,16,128]{3,2,1,0:T(8,128)S(1)}, u32[]{:S(2)}, u32[]{:S(2)}) %collective-permute-start.24) | collective-permute-done | bytes 65568 | tf_op jit(solution)/shard_map/ppermute | solution.py:305
  119.5 6.0 %collective-permute-start.25 = (f32[2,4,16,128]{3,2,1,0:T(8,128)S(1)}, f32[2,4,16,128]{3,2,1,0:T(8,128)S(1)}, u32[]{:S(2)}, u32[]{:S(2)}) collective-permute-start(f32[2,4,16,128]{3,2,1,0:T(8,128)S(1)} %pad_maximum_fusion.1.refs_5_), channel_id=1, source_target_pairs={{0,2},{1,3},{2,0},{3,1},{4,6},{5,7},{6,4},{7,5},{8,10},{9,11},{10,... | collective-permute-start | bytes 196616 | tf_op jit(solution)/shard_map/ppermute | solution.py:308
  125.5 2.0 %shard_map.64 = f32[4,16,128,128]{3,2,1,0:T(8,128)} custom-call(f32[16,96,128]{2,1,0:T(8,128)S(1)} %get-tuple-element.74.refs_0_.first_inner, f32[16,32,128]{2,1,0:T(8,128)S(1)} %get-tuple-element.78.refs_1_.first_outer, f32[2,16,128,128]{3,2,1,0:T(8,128)S(1)} %get-tuple-element.81.refs_2_.middle, f32[16,96,128]{2,1,0:T(8,128)S(1)} %get-tuple-element.82.refs_3_.last_inner, ...), custom_call_target="tpu_custom_call" | custom-call | tf_op jit(solution)/shard_map/pallas_call | solution.py:298
  127.6 0.9 collective-permute-done.25.refs_6_
  128.4 2.1 %shard_map.63 = f32[4,16,128,128]{3,2,1,0:T(8,128)} custom-call(f32[16,96,128]{2,1,0:T(8,128)S(1)} %get-tuple-element.74.refs_0_.first_inner, f32[16,32,128]{2,1,0:T(8,128)S(1)} %get-tuple-element.78.refs_1_.first_outer, f32[2,16,128,128]{3,2,1,0:T(8,128)S(1)} %get-tuple-element.81.refs_2_.middle, f32[16,96,128]{2,1,0:T(8,128)S(1)} %get-tuple-element.82.refs_3_.last_inner, ...), custom_call_target="tpu_custom_call" | custom-call | tf_op jit(solution)/shard_map/pallas_call | solution.py:309
  (16 shorter events, 0.1 us)
Async XLA Ops:
  0.6 15.8 %copy-start = (f32[4,16,128,128]{3,2,1,0:T(8,128)S(1)}, f32[4,16,128,128]{3,2,1,0:T(8,128)}, u32[]{:S(2)}) copy-start(f32[4,16,128,128]{3,2,1,0:T(8,128)} %mobility.13) | copy-start | bytes 12582916
  2.3 18.9 %collective-permute-start.3 = (f32[16,96,128]{2,1,0:T(8,128)S(1)}, f32[16,96,128]{2,1,0:T(8,128)S(1)}, u32[]{:S(2)}, u32[]{:S(2)}) collective-permute-start(f32[16,96,128]{2,1,0:T(8,128)S(1)} %get-tuple-element.86), channel_id=1, source_target_pairs={{16,0},{32,16},{48,32},{0,48},{17,1},{33,17},{49,33},{1,49},{18,2}... | collective-permute-start | bytes 2359304 | tf_op jit(solution)/shard_map/ppermute | solution.py:257
  3.4 19.0 %collective-permute-start.2 = (f32[16,96,128]{2,1,0:T(8,128)S(1)}, f32[16,96,128]{2,1,0:T(8,128)S(1)}, u32[]{:S(2)}, u32[]{:S(2)}) collective-permute-start(f32[16,96,128]{2,1,0:T(8,128)S(1)} %get-tuple-element.87), channel_id=1, source_target_pairs={{0,16},{16,32},{32,48},{48,0},{1,17},{17,33},{33,49},{49,1},{2,18}... | collective-permute-start | bytes 2359304 | tf_op jit(solution)/shard_map/ppermute | solution.py:256
  3.4 2.2 %copy-start.3 = (f32[4,16,128,128]{3,2,1,0:T(8,128)S(1)}, f32[4,16,128,128]{3,2,1,0:T(8,128)}, u32[]{:S(2)}) copy-start(f32[4,16,128,128]{3,2,1,0:T(8,128)} %refs_0_.1) | copy-start | bytes 12582916
  6.1 10.3 %collective-permute-start = (f32[4,128,128]{2,1,0:T(8,128)S(1)}, f32[4,128,128]{2,1,0:T(8,128)S(1)}, u32[]{:S(2)}, u32[]{:S(2)}) collective-permute-start(f32[4,128,128]{2,1,0:T(8,128)S(1)} %get-tuple-element.44), channel_id=1, source_target_pairs={{0,4},{4,8},{8,12},{12,0},{1,5},{5,9},{9,13},{13,1},{2,6},{6,10},{... | collective-permute-start | bytes 786440 | tf_op jit(solution)/shard_map/ppermute | solution.py:256
  7.7 8.7 %collective-permute-start.1 = (f32[4,128,128]{2,1,0:T(8,128)S(1)}, f32[4,128,128]{2,1,0:T(8,128)S(1)}, u32[]{:S(2)}, u32[]{:S(2)}) collective-permute-start(f32[4,128,128]{2,1,0:T(8,128)S(1)} %get-tuple-element.45), channel_id=1, source_target_pairs={{4,0},{8,4},{12,8},{0,12},{5,1},{9,5},{13,9},{1,13},{6,2},{10,6},{... | collective-permute-start | bytes 786440 | tf_op jit(solution)/shard_map/ppermute | solution.py:257
  16.4 2.2 %copy-start.1 = (f32[4,16,128,128]{3,2,1,0:T(8,128)S(1)}, f32[4,16,128,128]{3,2,1,0:T(8,128)}, u32[]{:S(2)}) copy-start(f32[4,16,128,128]{3,2,1,0:T(8,128)} %refs_6_.3) | copy-start | bytes 12582916
  22.6 42.2 %collective-permute-start.11 = (f32[16,96,128]{2,1,0:T(8,128)S(1)}, f32[16,96,128]{2,1,0:T(8,128)S(1)}, u32[]{:S(2)}, u32[]{:S(2)}) collective-permute-start(f32[16,96,128]{2,1,0:T(8,128)S(1)} %get-tuple-element.48.refs_0_), channel_id=1, source_target_pairs={{16,0},{32,16},{48,32},{0,48},{17,1},{33,17},{49,33},{1,49},{18,2}... | collective-permute-start | bytes 2359304 | tf_op jit(solution)/shard_map/ppermute | solution.py:257
  23.8 41.0 %collective-permute-start.10 = (f32[16,96,128]{2,1,0:T(8,128)S(1)}, f32[16,96,128]{2,1,0:T(8,128)S(1)}, u32[]{:S(2)}, u32[]{:S(2)}) collective-permute-start(f32[16,96,128]{2,1,0:T(8,128)S(1)} %get-tuple-element.55.refs_2_.refs_3_), channel_id=1, source_target_pairs={{0,16},{16,32},{32,48},{48,0},{1,17},{17,33},{33,49},{49,1},{2,18}... | collective-permute-start | bytes 2359304 | tf_op jit(solution)/shard_map/ppermute | solution.py:256
  23.8 28.2 %collective-permute-start.4 = (f32[16,32,128]{2,1,0:T(8,128)S(1)}, f32[16,32,128]{2,1,0:T(8,128)S(1)}, u32[]{:S(2)}, u32[]{:S(2)}) collective-permute-start(f32[16,32,128]{2,1,0:T(8,128)S(1)} %get-tuple-element.49), channel_id=1, source_target_pairs={{0,16},{16,32},{32,48},{48,0},{1,17},{17,33},{33,49},{49,1},{2,18}... | collective-permute-start | bytes 786440 | tf_op jit(solution)/shard_map/ppermute | solution.py:256
  24.3 27.6 %collective-permute-start.5 = (f32[16,32,128]{2,1,0:T(8,128)S(1)}, f32[16,32,128]{2,1,0:T(8,128)S(1)}, u32[]{:S(2)}, u32[]{:S(2)}) collective-permute-start(f32[16,32,128]{2,1,0:T(8,128)S(1)} %get-tuple-element.50), channel_id=1, source_target_pairs={{16,0},{32,16},{48,32},{0,48},{17,1},{33,17},{49,33},{1,49},{18,2}... | collective-permute-start | bytes 786440 | tf_op jit(solution)/shard_map/ppermute | solution.py:257
  25.6 10.5 %collective-permute-start.6 = (f32[4,16,128]{2,1,0:T(8,128)S(1)}, f32[4,16,128]{2,1,0:T(8,128)S(1)}, u32[]{:S(2)}, u32[]{:S(2)}) collective-permute-start(f32[4,16,128]{2,1,0:T(8,128)S(1)} %get-tuple-element.51), channel_id=1, source_target_pairs={{0,3},{1,2},{2,1},{3,0},{4,7},{5,6},{6,5},{7,4},{8,11},{9,10},{10,... | collective-permute-start | bytes 98312 | tf_op jit(solution)/shard_map/ppermute | solution.py:271
  36.1 15.9 %collective-permute-start.7 = (f32[4,16,128]{2,1,0:T(8,128)S(1)}, f32[4,16,128]{2,1,0:T(8,128)S(1)}, u32[]{:S(2)}, u32[]{:S(2)}) collective-permute-start(f32[4,16,128]{2,1,0:T(8,128)S(1)} %get-tuple-element.52), channel_id=1, source_target_pairs={{0,1},{1,0},{2,3},{3,2},{4,5},{5,4},{6,7},{7,6},{8,9},{9,8},{10,11... | collective-permute-start | bytes 98312 | tf_op jit(solution)/shard_map/ppermute | solution.py:271
  52.2 10.3 %copy-start.2 = (f32[4,16,128,128]{3,2,1,0:T(8,128)S(1)}, f32[4,16,128,128]{3,2,1,0:T(8,128)}, u32[]{:S(2)}) copy-start(f32[4,16,128,128]{3,2,1,0:T(8,128)} %refs_6_.3) | copy-start | bytes 12582916
  53.0 9.6 %collective-permute-start.8 = (f32[4,128,128]{2,1,0:T(8,128)S(1)}, f32[4,128,128]{2,1,0:T(8,128)S(1)}, u32[]{:S(2)}, u32[]{:S(2)}) collective-permute-start(f32[4,128,128]{2,1,0:T(8,128)S(1)} %get-tuple-element.58), channel_id=1, source_target_pairs={{0,4},{4,8},{8,12},{12,0},{1,5},{5,9},{9,13},{13,1},{2,6},{6,10},{... | collective-permute-start | bytes 786440 | tf_op jit(solution)/shard_map/ppermute | solution.py:256
  54.5 8.0 %collective-permute-start.9 = (f32[4,128,128]{2,1,0:T(8,128)S(1)}, f32[4,128,128]{2,1,0:T(8,128)S(1)}, u32[]{:S(2)}, u32[]{:S(2)}) collective-permute-start(f32[4,128,128]{2,1,0:T(8,128)S(1)} %get-tuple-element.59), channel_id=1, source_target_pairs={{4,0},{8,4},{12,8},{0,12},{5,1},{9,5},{13,9},{1,13},{6,2},{10,6},{... | collective-permute-start | bytes 786440 | tf_op jit(solution)/shard_map/ppermute | solution.py:257
  56.3 17.1 %collective-permute-start.13 = (f32[16,32,128]{2,1,0:T(8,128)S(1)}, f32[16,32,128]{2,1,0:T(8,128)S(1)}, u32[]{:S(2)}, u32[]{:S(2)}) collective-permute-start(f32[16,32,128]{2,1,0:T(8,128)S(1)} %get-tuple-element.53.refs_1_), channel_id=1, source_target_pairs={{16,0},{32,16},{48,32},{0,48},{17,1},{33,17},{49,33},{1,49},{18,2}... | collective-permute-start | bytes 786440 | tf_op jit(solution)/shard_map/ppermute | solution.py:257
  62.5 13.8 %collective-permute-start.12 = (f32[16,32,128]{2,1,0:T(8,128)S(1)}, f32[16,32,128]{2,1,0:T(8,128)S(1)}, u32[]{:S(2)}, u32[]{:S(2)}) collective-permute-start(f32[16,32,128]{2,1,0:T(8,128)S(1)} %get-tuple-element.56.refs_3_.refs_4_), channel_id=1, source_target_pairs={{0,16},{16,32},{32,48},{48,0},{1,17},{17,33},{33,49},{49,1},{2,18}... | collective-permute-start | bytes 786440 | tf_op jit(solution)/shard_map/ppermute | solution.py:256
  65.1 47.3 %collective-permute-start.19 = (f32[16,96,128]{2,1,0:T(8,128)S(1)}, f32[16,96,128]{2,1,0:T(8,128)S(1)}, u32[]{:S(2)}, u32[]{:S(2)}) collective-permute-start(f32[16,96,128]{2,1,0:T(8,128)S(1)} %get-tuple-element.62.refs_0_), channel_id=1, source_target_pairs={{16,0},{32,16},{48,32},{0,48},{17,1},{33,17},{49,33},{1,49},{18,2}... | collective-permute-start | bytes 2359304 | tf_op jit(solution)/shard_map/ppermute | solution.py:257
  67.1 45.3 %collective-permute-start.18 = (f32[16,96,128]{2,1,0:T(8,128)S(1)}, f32[16,96,128]{2,1,0:T(8,128)S(1)}, u32[]{:S(2)}, u32[]{:S(2)}) collective-permute-start(f32[16,96,128]{2,1,0:T(8,128)S(1)} %get-tuple-element.67.refs_2_.refs_3_), channel_id=1, source_target_pairs={{0,16},{16,32},{32,48},{48,0},{1,17},{17,33},{33,49},{49,1},{2,18}... | collective-permute-start | bytes 2359304 | tf_op jit(solution)/shard_map/ppermute | solution.py:256
  67.1 10.3 %collective-permute-start.14 = (f32[4,16,128]{2,1,0:T(8,128)S(1)}, f32[4,16,128]{2,1,0:T(8,128)S(1)}, u32[]{:S(2)}, u32[]{:S(2)}) collective-permute-start(f32[4,16,128]{2,1,0:T(8,128)S(1)} %get-tuple-element.63), channel_id=1, source_target_pairs={{0,3},{1,2},{2,1},{3,0},{4,7},{5,6},{6,5},{7,4},{8,11},{9,10},{10,... | collective-permute-start | bytes 98312 | tf_op jit(solution)/shard_map/ppermute | solution.py:271
  73.4 13.7 %collective-permute-start.15 = (f32[4,16,128]{2,1,0:T(8,128)S(1)}, f32[4,16,128]{2,1,0:T(8,128)S(1)}, u32[]{:S(2)}, u32[]{:S(2)}) collective-permute-start(f32[4,16,128]{2,1,0:T(8,128)S(1)} %get-tuple-element.64), channel_id=1, source_target_pairs={{0,1},{1,0},{2,3},{3,2},{4,5},{5,4},{6,7},{7,6},{8,9},{9,8},{10,11... | collective-permute-start | bytes 98312 | tf_op jit(solution)/shard_map/ppermute | solution.py:271
  88.1 13.5 %collective-permute-start.16 = (f32[4,128,128]{2,1,0:T(8,128)S(1)}, f32[4,128,128]{2,1,0:T(8,128)S(1)}, u32[]{:S(2)}, u32[]{:S(2)}) collective-permute-start(f32[4,128,128]{2,1,0:T(8,128)S(1)} %get-tuple-element.70), channel_id=1, source_target_pairs={{0,4},{4,8},{8,12},{12,0},{1,5},{5,9},{9,13},{13,1},{2,6},{6,10},{... | collective-permute-start | bytes 786440 | tf_op jit(solution)/shard_map/ppermute | solution.py:256
  88.4 13.7 %collective-permute-start.17 = (f32[4,128,128]{2,1,0:T(8,128)S(1)}, f32[4,128,128]{2,1,0:T(8,128)S(1)}, u32[]{:S(2)}, u32[]{:S(2)}) collective-permute-start(f32[4,128,128]{2,1,0:T(8,128)S(1)} %get-tuple-element.71), channel_id=1, source_target_pairs={{4,0},{8,4},{12,8},{0,12},{5,1},{9,5},{13,9},{1,13},{6,2},{10,6},{... | collective-permute-start | bytes 786440 | tf_op jit(solution)/shard_map/ppermute | solution.py:257
  91.4 10.2 %collective-permute-start.22 = (f32[4,16,128]{2,1,0:T(8,128)S(1)}, f32[4,16,128]{2,1,0:T(8,128)S(1)}, u32[]{:S(2)}, u32[]{:S(2)}) collective-permute-start(f32[4,16,128]{2,1,0:T(8,128)S(1)} %get-tuple-element.76), channel_id=1, source_target_pairs={{0,3},{1,2},{2,1},{3,0},{4,7},{5,6},{6,5},{7,4},{8,11},{9,10},{10,... | collective-permute-start | bytes 98312 | tf_op jit(solution)/shard_map/ppermute | solution.py:271
  101.6 11.6 %collective-permute-start.21 = (f32[16,32,128]{2,1,0:T(8,128)S(1)}, f32[16,32,128]{2,1,0:T(8,128)S(1)}, u32[]{:S(2)}, u32[]{:S(2)}) collective-permute-start(f32[16,32,128]{2,1,0:T(8,128)S(1)} %get-tuple-element.65.refs_1_), channel_id=1, source_target_pairs={{16,0},{32,16},{48,32},{0,48},{17,1},{33,17},{49,33},{1,49},{18,2}... | collective-permute-start | bytes 786440 | tf_op jit(solution)/shard_map/ppermute | solution.py:257
  101.6 11.6 %collective-permute-start.20 = (f32[16,32,128]{2,1,0:T(8,128)S(1)}, f32[16,32,128]{2,1,0:T(8,128)S(1)}, u32[]{:S(2)}, u32[]{:S(2)}) collective-permute-start(f32[16,32,128]{2,1,0:T(8,128)S(1)} %get-tuple-element.68.refs_3_.refs_4_), channel_id=1, source_target_pairs={{0,16},{16,32},{32,48},{48,0},{1,17},{17,33},{33,49},{49,1},{2,18}... | collective-permute-start | bytes 786440 | tf_op jit(solution)/shard_map/ppermute | solution.py:256
  102.1 9.9 %collective-permute-start.23 = (f32[4,16,128]{2,1,0:T(8,128)S(1)}, f32[4,16,128]{2,1,0:T(8,128)S(1)}, u32[]{:S(2)}, u32[]{:S(2)}) collective-permute-start(f32[4,16,128]{2,1,0:T(8,128)S(1)} %get-tuple-element.77), channel_id=1, source_target_pairs={{0,1},{1,0},{2,3},{3,2},{4,5},{5,4},{6,7},{7,6},{8,9},{9,8},{10,11... | collective-permute-start | bytes 98312 | tf_op jit(solution)/shard_map/ppermute | solution.py:271
  113.6 5.9 %collective-permute-start.24 = (f32[2,4,16,128]{3,2,1,0:T(8,128)S(1)}, f32[2,4,16,128]{3,2,1,0:T(8,128)S(1)}, u32[]{:S(2)}, u32[]{:S(2)}) collective-permute-start(f32[2,4,16,128]{3,2,1,0:T(8,128)S(1)} %pad_maximum_fusion), channel_id=1, source_target_pairs={{0,1},{1,0},{2,3},{3,2},{4,5},{5,4},{6,7},{7,6},{8,9},{9,8},{10,11... | collective-permute-start | bytes 196616 | tf_op jit(solution)/shard_map/ppermute | solution.py:305
  119.5 9.0 %collective-permute-start.25 = (f32[2,4,16,128]{3,2,1,0:T(8,128)S(1)}, f32[2,4,16,128]{3,2,1,0:T(8,128)S(1)}, u32[]{:S(2)}, u32[]{:S(2)}) collective-permute-start(f32[2,4,16,128]{3,2,1,0:T(8,128)S(1)} %pad_maximum_fusion.1.refs_5_), channel_id=1, source_target_pairs={{0,2},{1,3},{2,0},{3,1},{4,6},{5,7},{6,4},{7,5},{8,10},{9,11},{10,... | collective-permute-start | bytes 196616 | tf_op jit(solution)/shard_map/ppermute | solution.py:308

commit v4 on v3

--- a/solution.py
+++ b/solution.py
@@ -250,11 +250,14 @@
     near = [(i, i ^ 1) for i in range(peers)]
     far = [(i, (i + (1 if i % 2 else -1)) % peers) for i in range(peers)]
 
+    def sent(value, axis, pairs):
+        return lax.ppermute(value, axis, pairs)
+
     def swap(leading, last, axis):
         peers = lax.axis_size(axis)
         up = [(i, (i + 1) % peers) for i in range(peers)]
-        low = lax.ppermute(last, axis, up)
-        high = lax.ppermute(leading, axis, [(b, a) for a, b in up])
+        low = sent(last, axis, up)
+        high = sent(leading, axis, [(b, a) for a, b in up])
         return (low, high)
 
     def call(kernel, *out_shape, **options):
@@ -268,7 +271,7 @@
     for step in range(STEPS):
         final = step == STEPS - 1
         along_x = swap(*edges[:2], "east")
-        along_z = (lax.ppermute(edges[2], "down", far), lax.ppermute(edges[3], "down", near))
+        along_z = (sent(edges[2], "down", far), sent(edges[3], "down", near))
         outers_y = swap(*outers, "south")
         stats = (f32(2, count - 2, width, levels),) if final else ()
         first, inside, last, *stats = call(
@@ -293,7 +296,6 @@
     *outers, mine = call(last_kernel, outer, outer, f32(2, 2, width, levels))(
         first, last, end_stats, mobility, *outers_y, *along_z
     )
-    mine = jnp.concatenate([mine[:, :1], middle_stats, mine[:, 1:]], axis=1)
     rows = (inners[0], outers[0], inside, inners[1], outers[1])
     (stored,) = call(
         store_kernel,
@@ -302,10 +304,13 @@
         scratch_shapes=[pltpu.SemaphoreType.DMA((7,))],
     )(*rows)
     members = depth
-    other = lax.ppermute(mine, "down", near)
-    mine = jnp.stack(joined(mine, other, members, members))
+    pairs = (middle_stats, mine)
+    middle_stats, mine = (
+        jnp.stack(joined(stats, sent(stats, "down", near), members, members)) for stats in pairs
+    )
+    mine = jnp.concatenate([mine[:, :1], middle_stats, mine[:, 1:]], axis=1)
     members *= 2
-    other = lax.ppermute(mine, "down", [(i, (i + 2) % peers) for i in range(peers)])
+    other = sent(mine, "down", [(i, (i + 2) % peers) for i in range(peers)])
     (standardized,) = call(
         functools.partial(scale_kernel, members),
         f32(count, width, depth, levels),

time: 131 us -> 132 us (level)
  the two profiles are of different devices: /device:TPU:32 before, /device:TPU:64 now
where the time goes in v4:
time: 132 us; the launch traced here: 131 us
  waiting for transfers between devices  54.4 us (41%)
  starting transfers between devices  53.6 us (41%)
  Pallas kernels  16.4 us (12%)
  local copies, waits for them, and re-layouts  6.02 us (5%)
    ppermute x27, waiting for transfers between devices, sent(): return lax.ppermute(value, axis, pairs)  54.4 us
    ppermute x27, starting transfers between devices, sent(): return lax.ppermute(value, axis, pairs)  53.6 us
    pallas_call x3, Pallas kernels, body(): call(functools.partial(partial_kernel, len(pieces), final), row, middle,...  7.76 us
    unnamed x8, local copies, waits for them, and re-layouts  4.39 us
  transfers between devices with their start and end apart: 27, of which 13 were waited for; matrix products, arithmetic and copies ran while one was open for 0% of the time, Pallas kernels for 11%

profile of v4, /device:TPU:64, one launch (start us, length us, event | category | flops | bytes accessed | tf_op | source)
XLA Modules:
  0.0 131.4 jit_solution(3278487962733848976)
XLA Ops:
  0.6 1.6 %slice_bitcast_fusion = (f32[16,96,128]{2,1,0:T(8,128)S(1)}, f32[16,96,128]{2,1,0:T(8,128)S(1)}) fusion(f32[4,16,128,128]{3,2,1,0:T(8,128)} %refs_0_.1), kind=kLoop, calls=%fused_computation | loop fusion | bytes 3145728 | tf_op jit(solution)/shard_map/squeeze | solution.py:266
  2.3 1.1 collective-permute-start.3
  3.4 0.0 collective-permute-start.2
  3.4 2.2 %copy-done.3 = f32[4,16,128,128]{3,2,1,0:T(8,128)S(1)} copy-done((f32[4,16,128,128]{3,2,1,0:T(8,128)S(1)}, f32[4,16,128,128]{3,2,1,0:T(8,128)}, u32[]{:S(2)}) %copy-start.3) | copy-done | bytes 4194328
  5.6 0.5 shard_map.50
  6.1 1.6 %collective-permute-start = (f32[4,128,128]{2,1,0:T(8,128)S(1)}, f32[4,128,128]{2,1,0:T(8,128)S(1)}, u32[]{:S(2)}, u32[]{:S(2)}) collective-permute-start(f32[4,128,128]{2,1,0:T(8,128)S(1)} %get-tuple-element.44), channel_id=1, source_target_pairs={{0,4},{4,8},{8,12},{12,0},{1,5},{5,9},{9,13},{13,1},{2,6},{6,10},{... | collective-permute-start | bytes 786440 | tf_op jit(solution)/shard_map/ppermute | solution.py:254
  7.7 1.7 %collective-permute-start.1 = (f32[4,128,128]{2,1,0:T(8,128)S(1)}, f32[4,128,128]{2,1,0:T(8,128)S(1)}, u32[]{:S(2)}, u32[]{:S(2)}) collective-permute-start(f32[4,128,128]{2,1,0:T(8,128)S(1)} %get-tuple-element.45), channel_id=1, source_target_pairs={{4,0},{8,4},{12,8},{0,12},{5,1},{9,5},{13,9},{1,13},{6,2},{10,6},{... | collective-permute-start | bytes 786440 | tf_op jit(solution)/shard_map/ppermute | solution.py:254
  9.4 6.9 %collective-permute-done.refs_3_ = f32[4,128,128]{2,1,0:T(8,128)S(1)} collective-permute-done((f32[4,128,128]{2,1,0:T(8,128)S(1)}, f32[4,128,128]{2,1,0:T(8,128)S(1)}, u32[]{:S(2)}, u32[]{:S(2)}) %collective-permute-start) | collective-permute-done | bytes 262176 | tf_op jit(solution)/shard_map/ppermute | solution.py:254
  16.4 0.0 collective-permute-done.1.refs_4_
  16.4 2.2 %copy-done.1 = f32[4,16,128,128]{3,2,1,0:T(8,128)S(1)} copy-done((f32[4,16,128,128]{3,2,1,0:T(8,128)S(1)}, f32[4,16,128,128]{3,2,1,0:T(8,128)}, u32[]{:S(2)}) %copy-start.1) | copy-done | bytes 4194328
  18.6 2.3 %shard_map.51 = (f32[16,128,128]{2,1,0:T(8,128)S(1)}, f32[2,16,128,128]{3,2,1,0:T(8,128)S(1)}, f32[16,128,128]{2,1,0:T(8,128)S(1)}) custom-call(f32[4,16,128,128]{3,2,1,0:T(8,128)S(1)} %copy-done.3, f32[4,16,128,128]{3,2,1,0:T(8,128)S(1)} %copy-done, f32[4,16,128,128]{3,2,1,0:T(8,128)S(1)} %copy-done.1, f32[4,128,128]{2,1,0:T(8,128)S(1)} %collective-permute-done.refs_3_, ...), custom_call_target="tpu_custom_call" | custom-call | tf_op jit(solution)/shard_map/pallas_call | solution.py:277
  20.8 0.4 collective-permute-done.3.high_y
  21.2 1.1 collective-permute-done.2.low_y
  22.3 0.3 shard_map.52
  22.6 1.2 collective-permute-start.11
  23.8 0.0 collective-permute-start.10
  23.8 0.6 collective-permute-start.4
  24.3 1.2 collective-permute-start.5
  25.6 7.6 %collective-permute-start.6 = (f32[4,16,128]{2,1,0:T(8,128)S(1)}, f32[4,16,128]{2,1,0:T(8,128)S(1)}, u32[]{:S(2)}, u32[]{:S(2)}) collective-permute-start(f32[4,16,128]{2,1,0:T(8,128)S(1)} %get-tuple-element.51), channel_id=1, source_target_pairs={{0,3},{1,2},{2,1},{3,0},{4,7},{5,6},{6,5},{7,4},{8,11},{9,10},{10,... | collective-permute-start | bytes 98312 | tf_op jit(solution)/shard_map/ppermute | solution.py:254
  33.2 2.9 %collective-permute-done.6.far.refs_5_ = f32[4,16,128]{2,1,0:T(8,128)S(1)} collective-permute-done((f32[4,16,128]{2,1,0:T(8,128)S(1)}, f32[4,16,128]{2,1,0:T(8,128)S(1)}, u32[]{:S(2)}, u32[]{:S(2)}) %collective-permute-start.6) | collective-permute-done | bytes 32800 | tf_op jit(solution)/shard_map/ppermute | solution.py:254
  36.1 2.6 %collective-permute-start.7 = (f32[4,16,128]{2,1,0:T(8,128)S(1)}, f32[4,16,128]{2,1,0:T(8,128)S(1)}, u32[]{:S(2)}, u32[]{:S(2)}) collective-permute-start(f32[4,16,128]{2,1,0:T(8,128)S(1)} %get-tuple-element.52), channel_id=1, source_target_pairs={{0,1},{1,0},{2,3},{3,2},{4,5},{5,4},{6,7},{7,6},{8,9},{9,8},{10,11... | collective-permute-start | bytes 98312 | tf_op jit(solution)/shard_map/ppermute | solution.py:254
  38.7 13.3 %collective-permute-done.7.near.refs_6_ = f32[4,16,128]{2,1,0:T(8,128)S(1)} collective-permute-done((f32[4,16,128]{2,1,0:T(8,128)S(1)}, f32[4,16,128]{2,1,0:T(8,128)S(1)}, u32[]{:S(2)}, u32[]{:S(2)}) %collective-permute-start.7) | collective-permute-done | bytes 32800 | tf_op jit(solution)/shard_map/ppermute | solution.py:254
  52.0 0.0 collective-permute-done.4.low_y
  52.0 0.0 collective-permute-done.5.high_y
  52.0 0.3 shard_map.53
  52.2 0.0 copy-start.2
  52.3 0.7 shard_map.54
  53.0 1.6 %collective-permute-start.8 = (f32[4,128,128]{2,1,0:T(8,128)S(1)}, f32[4,128,128]{2,1,0:T(8,128)S(1)}, u32[]{:S(2)}, u32[]{:S(2)}) collective-permute-start(f32[4,128,128]{2,1,0:T(8,128)S(1)} %get-tuple-element.58), channel_id=1, source_target_pairs={{0,4},{4,8},{8,12},{12,0},{1,5},{5,9},{9,13},{13,1},{2,6},{6,10},{... | collective-permute-start | bytes 786440 | tf_op jit(solution)/shard_map/ppermute | solution.py:254
  54.5 1.7 %collective-permute-start.9 = (f32[4,128,128]{2,1,0:T(8,128)S(1)}, f32[4,128,128]{2,1,0:T(8,128)S(1)}, u32[]{:S(2)}, u32[]{:S(2)}) collective-permute-start(f32[4,128,128]{2,1,0:T(8,128)S(1)} %get-tuple-element.59), channel_id=1, source_target_pairs={{4,0},{8,4},{12,8},{0,12},{5,1},{9,5},{13,9},{1,13},{6,2},{10,6},{... | collective-permute-start | bytes 786440 | tf_op jit(solution)/shard_map/ppermute | solution.py:254
  56.3 0.0 collective-permute-start.13
  56.3 6.3 %collective-permute-done.8.refs_7_ = f32[4,128,128]{2,1,0:T(8,128)S(1)} collective-permute-done((f32[4,128,128]{2,1,0:T(8,128)S(1)}, f32[4,128,128]{2,1,0:T(8,128)S(1)}, u32[]{:S(2)}, u32[]{:S(2)}) %collective-permute-start.8) | collective-permute-done | bytes 262176 | tf_op jit(solution)/shard_map/ppermute | solution.py:254
  62.5 0.0 collective-permute-start.12
  62.6 2.3 %shard_map.55 = (f32[16,128,128]{2,1,0:T(8,128)S(1)}, f32[2,16,128,128]{3,2,1,0:T(8,128)S(1)}, f32[16,128,128]{2,1,0:T(8,128)S(1)}) custom-call(f32[16,96,128]{2,1,0:T(8,128)S(1)} %get-tuple-element.48.refs_0_, f32[16,32,128]{2,1,0:T(8,128)S(1)} %get-tuple-element.53.refs_1_, f32[2,16,128,128]{3,2,1,0:T(8,128)S(1)} %get-tuple-element.57.refs_2_, ...), custom_call_target="tpu_custom_call" | custom-call | tf_op jit(solution)/shard_map/pallas_call | solution.py:277
  64.8 0.3 shard_map.56
  65.1 2.0 %collective-permute-start.19 = (f32[16,96,128]{2,1,0:T(8,128)S(1)}, f32[16,96,128]{2,1,0:T(8,128)S(1)}, u32[]{:S(2)}, u32[]{:S(2)}) collective-permute-start(f32[16,96,128]{2,1,0:T(8,128)S(1)} %get-tuple-element.62.refs_0_), channel_id=1, source_target_pairs={{16,0},{32,16},{48,32},{0,48},{17,1},{33,17},{49,33},{1,49},{18,2}... | collective-permute-start | bytes 2359304 | tf_op jit(solution)/shard_map/ppermute | solution.py:254
  67.1 5.4 %collective-permute-start.14 = (f32[4,16,128]{2,1,0:T(8,128)S(1)}, f32[4,16,128]{2,1,0:T(8,128)S(1)}, u32[]{:S(2)}, u32[]{:S(2)}) collective-permute-start(f32[4,16,128]{2,1,0:T(8,128)S(1)} %get-tuple-element.63), channel_id=1, source_target_pairs={{0,3},{1,2},{2,1},{3,0},{4,7},{5,6},{6,5},{7,4},{8,11},{9,10},{10,... | collective-permute-start | bytes 98312 | tf_op jit(solution)/shard_map/ppermute | solution.py:254
  72.5 0.0 collective-permute-done.13.high_y
  72.5 3.0 %collective-permute-start.15 = (f32[4,16,128]{2,1,0:T(8,128)S(1)}, f32[4,16,128]{2,1,0:T(8,128)S(1)}, u32[]{:S(2)}, u32[]{:S(2)}) collective-permute-start(f32[4,16,128]{2,1,0:T(8,128)S(1)} %get-tuple-element.64), channel_id=1, source_target_pairs={{0,1},{1,0},{2,3},{3,2},{4,5},{5,4},{6,7},{7,6},{8,9},{9,8},{10,11... | collective-permute-start | bytes 98312 | tf_op jit(solution)/shard_map/ppermute | solution.py:254
  75.5 0.0 collective-permute-done.12.low_y
  75.5 2.0 %collective-permute-done.14.far.refs_5_ = f32[4,16,128]{2,1,0:T(8,128)S(1)} collective-permute-done((f32[4,16,128]{2,1,0:T(8,128)S(1)}, f32[4,16,128]{2,1,0:T(8,128)S(1)}, u32[]{:S(2)}, u32[]{:S(2)}) %collective-permute-start.14) | collective-permute-done | bytes 32800 | tf_op jit(solution)/shard_map/ppermute | solution.py:254
  77.4 9.7 %collective-permute-done.15.near.refs_6_ = f32[4,16,128]{2,1,0:T(8,128)S(1)} collective-permute-done((f32[4,16,128]{2,1,0:T(8,128)S(1)}, f32[4,16,128]{2,1,0:T(8,128)S(1)}, u32[]{:S(2)}, u32[]{:S(2)}) %collective-permute-start.15) | collective-permute-done | bytes 32800 | tf_op jit(solution)/shard_map/ppermute | solution.py:254
  87.1 0.3 shard_map.57
  87.4 0.7 shard_map.58
  88.1 0.4 collective-permute-start.16
  88.4 3.0 %collective-permute-start.17 = (f32[4,128,128]{2,1,0:T(8,128)S(1)}, f32[4,128,128]{2,1,0:T(8,128)S(1)}, u32[]{:S(2)}, u32[]{:S(2)}) collective-permute-start(f32[4,128,128]{2,1,0:T(8,128)S(1)} %get-tuple-element.71), channel_id=1, source_target_pairs={{4,0},{8,4},{12,8},{0,12},{5,1},{9,5},{13,9},{1,13},{6,2},{10,6},{... | collective-permute-start | bytes 786440 | tf_op jit(solution)/shard_map/ppermute | solution.py:254
  91.4 7.2 %collective-permute-start.22 = (f32[4,16,128]{2,1,0:T(8,128)S(1)}, f32[4,16,128]{2,1,0:T(8,128)S(1)}, u32[]{:S(2)}, u32[]{:S(2)}) collective-permute-start(f32[4,16,128]{2,1,0:T(8,128)S(1)} %get-tuple-element.76), channel_id=1, source_target_pairs={{0,3},{1,2},{2,1},{3,0},{4,7},{5,6},{6,5},{7,4},{8,11},{9,10},{10,... | collective-permute-start | bytes 98312 | tf_op jit(solution)/shard_map/ppermute | solution.py:254
  98.6 3.1 %collective-permute-done.22.refs_2_.far = f32[4,16,128]{2,1,0:T(8,128)S(1)} collective-permute-done((f32[4,16,128]{2,1,0:T(8,128)S(1)}, f32[4,16,128]{2,1,0:T(8,128)S(1)}, u32[]{:S(2)}, u32[]{:S(2)}) %collective-permute-start.22) | collective-permute-done | bytes 32800 | tf_op jit(solution)/shard_map/ppermute | solution.py:254
  101.8 0.0 collective-permute-start.21
  101.8 0.5 collective-permute-start.20
  102.3 2.3 %collective-permute-start.23 = (f32[4,16,128]{2,1,0:T(8,128)S(1)}, f32[4,16,128]{2,1,0:T(8,128)S(1)}, u32[]{:S(2)}, u32[]{:S(2)}) collective-permute-start(f32[4,16,128]{2,1,0:T(8,128)S(1)} %get-tuple-element.77), channel_id=1, source_target_pairs={{0,1},{1,0},{2,3},{3,2},{4,5},{5,4},{6,7},{7,6},{8,9},{9,8},{10,11... | collective-permute-start | bytes 98312 | tf_op jit(solution)/shard_map/ppermute | solution.py:254
  104.5 3.2 %shard_map.59 = (f32[16,128,128]{2,1,0:T(8,128)S(1)}, f32[2,16,128,128]{3,2,1,0:T(8,128)S(1)}, f32[16,128,128]{2,1,0:T(8,128)S(1)}, f32[2,2,16,128]{3,2,1,0:T(8,128)S(1)}) custom-call(f32[16,96,128]{2,1,0:T(8,128)S(1)} %get-tuple-element.62.refs_0_, f32[16,32,128]{2,1,0:T(8,128)S(1)} %get-tuple-element.65.refs_1_, ...), custom_call_target="tpu_custom_call" | custom-call | tf_op jit(solution)/shard_map/pallas_call | solution.py:277
  107.8 3.9 %collective-permute-done.23.refs_3_.near = f32[4,16,128]{2,1,0:T(8,128)S(1)} collective-permute-done((f32[4,16,128]{2,1,0:T(8,128)S(1)}, f32[4,16,128]{2,1,0:T(8,128)S(1)}, u32[]{:S(2)}, u32[]{:S(2)}) %collective-permute-start.23) | collective-permute-done | bytes 32800 | tf_op jit(solution)/shard_map/ppermute | solution.py:254
  111.7 0.3 shard_map.62
  112.0 1.4 %collective-permute-start.25 = (f32[2,2,16,128]{3,2,1,0:T(8,128)S(1)}, f32[2,2,16,128]{3,2,1,0:T(8,128)S(1)}, u32[]{:S(2)}, u32[]{:S(2)}) collective-permute-start(f32[2,2,16,128]{3,2,1,0:T(8,128)S(1)} %get-tuple-element.85), channel_id=1, source_target_pairs={{0,1},{1,0},{2,3},{3,2},{4,5},{5,4},{6,7},{7,6},{8,9},{9,8},{10,11... | collective-permute-start | bytes 98312 | tf_op jit(solution)/shard_map/ppermute | solution.py:254
  113.4 0.8 shard_map.60
  114.2 0.0 collective-permute-done.21.refs_1_
  114.2 0.3 shard_map.61
  114.5 2.4 %collective-permute-start.24 = (f32[2,2,16,128]{3,2,1,0:T(8,128)S(1)}, f32[2,2,16,128]{3,2,1,0:T(8,128)S(1)}, u32[]{:S(2)}, u32[]{:S(2)}) collective-permute-start(f32[2,2,16,128]{3,2,1,0:T(8,128)S(1)} %get-tuple-element.84), channel_id=1, source_target_pairs={{0,1},{1,0},{2,3},{3,2},{4,5},{5,4},{6,7},{7,6},{8,9},{9,8},{10,11... | collective-permute-start | bytes 98312 | tf_op jit(solution)/shard_map/ppermute | solution.py:254
  116.9 0.6 collective-permute-done.25
  117.5 2.5 %collective-permute-done.24 = f32[2,2,16,128]{3,2,1,0:T(8,128)S(1)} collective-permute-done((f32[2,2,16,128]{3,2,1,0:T(8,128)S(1)}, f32[2,2,16,128]{3,2,1,0:T(8,128)S(1)}, u32[]{:S(2)}, u32[]{:S(2)}) %collective-permute-start.24) | collective-permute-done | bytes 32800 | tf_op jit(solution)/shard_map/ppermute | solution.py:254
  120.1 5.3 %collective-permute-start.26 = (f32[2,4,16,128]{3,2,1,0:T(8,128)S(1)}, f32[2,4,16,128]{3,2,1,0:T(8,128)S(1)}, u32[]{:S(2)}, u32[]{:S(2)}) collective-permute-start(f32[2,4,16,128]{3,2,1,0:T(8,128)S(1)} %fusion.refs_5_), channel_id=1, source_target_pairs={{0,2},{1,3},{2,0},{3,1},{4,6},{5,7},{6,4},{7,5},{8,10},{9,11},{10,... | collective-permute-start | bytes 196616 | tf_op jit(solution)/shard_map/ppermute | solution.py:254
  125.4 2.0 %shard_map.64 = f32[4,16,128,128]{3,2,1,0:T(8,128)} custom-call(f32[16,96,128]{2,1,0:T(8,128)S(1)} %get-tuple-element.74.refs_0_.first_inner, f32[16,32,128]{2,1,0:T(8,128)S(1)} %get-tuple-element.78.refs_1_.first_outer, f32[2,16,128,128]{3,2,1,0:T(8,128)S(1)} %get-tuple-element.81.refs_2_.middle, f32[16,96,128]{2,1,0:T(8,128)S(1)} %get-tuple-element.82.refs_3_.last_inner, ...), custom_call_target="tpu_custom_call" | custom-call | tf_op jit(solution)/shard_map/pallas_call | solution.py:300
  127.5 1.7 %collective-permute-done.26.refs_6_ = f32[2,4,16,128]{3,2,1,0:T(8,128)S(1)} collective-permute-done((f32[2,4,16,128]{3,2,1,0:T(8,128)S(1)}, f32[2,4,16,128]{3,2,1,0:T(8,128)S(1)}, u32[]{:S(2)}, u32[]{:S(2)}) %collective-permute-start.26) | collective-permute-done | bytes 65568 | tf_op jit(solution)/shard_map/ppermute | solution.py:254
  129.2 2.1 %shard_map.63 = f32[4,16,128,128]{3,2,1,0:T(8,128)} custom-call(f32[16,96,128]{2,1,0:T(8,128)S(1)} %get-tuple-element.74.refs_0_.first_inner, f32[16,32,128]{2,1,0:T(8,128)S(1)} %get-tuple-element.78.refs_1_.first_outer, f32[2,16,128,128]{3,2,1,0:T(8,128)S(1)} %get-tuple-element.81.refs_2_.middle, f32[16,96,128]{2,1,0:T(8,128)S(1)} %get-tuple-element.82.refs_3_.last_inner, ...), custom_call_target="tpu_custom_call" | custom-call | tf_op jit(solution)/shard_map/pallas_call | solution.py:314
  (18 shorter events, 0.1 us)
Async XLA Ops:
  0.6 15.8 %copy-start = (f32[4,16,128,128]{3,2,1,0:T(8,128)S(1)}, f32[4,16,128,128]{3,2,1,0:T(8,128)}, u32[]{:S(2)}) copy-start(f32[4,16,128,128]{3,2,1,0:T(8,128)} %mobility.13) | copy-start | bytes 12582916
  2.3 18.9 %collective-permute-start.3 = (f32[16,96,128]{2,1,0:T(8,128)S(1)}, f32[16,96,128]{2,1,0:T(8,128)S(1)}, u32[]{:S(2)}, u32[]{:S(2)}) collective-permute-start(f32[16,96,128]{2,1,0:T(8,128)S(1)} %get-tuple-element.86), channel_id=1, source_target_pairs={{16,0},{32,16},{48,32},{0,48},{17,1},{33,17},{49,33},{1,49},{18,2}... | collective-permute-start | bytes 2359304 | tf_op jit(solution)/shard_map/ppermute | solution.py:254
  3.4 19.0 %collective-permute-start.2 = (f32[16,96,128]{2,1,0:T(8,128)S(1)}, f32[16,96,128]{2,1,0:T(8,128)S(1)}, u32[]{:S(2)}, u32[]{:S(2)}) collective-permute-start(f32[16,96,128]{2,1,0:T(8,128)S(1)} %get-tuple-element.87), channel_id=1, source_target_pairs={{0,16},{16,32},{32,48},{48,0},{1,17},{17,33},{33,49},{49,1},{2,18}... | collective-permute-start | bytes 2359304 | tf_op jit(solution)/shard_map/ppermute | solution.py:254
  3.4 2.2 %copy-start.3 = (f32[4,16,128,128]{3,2,1,0:T(8,128)S(1)}, f32[4,16,128,128]{3,2,1,0:T(8,128)}, u32[]{:S(2)}) copy-start(f32[4,16,128,128]{3,2,1,0:T(8,128)} %refs_0_.1) | copy-start | bytes 12582916
  6.1 10.3 %collective-permute-start = (f32[4,128,128]{2,1,0:T(8,128)S(1)}, f32[4,128,128]{2,1,0:T(8,128)S(1)}, u32[]{:S(2)}, u32[]{:S(2)}) collective-permute-start(f32[4,128,128]{2,1,0:T(8,128)S(1)} %get-tuple-element.44), channel_id=1, source_target_pairs={{0,4},{4,8},{8,12},{12,0},{1,5},{5,9},{9,13},{13,1},{2,6},{6,10},{... | collective-permute-start | bytes 786440 | tf_op jit(solution)/shard_map/ppermute | solution.py:254
  7.7 8.7 %collective-permute-start.1 = (f32[4,128,128]{2,1,0:T(8,128)S(1)}, f32[4,128,128]{2,1,0:T(8,128)S(1)}, u32[]{:S(2)}, u32[]{:S(2)}) collective-permute-start(f32[4,128,128]{2,1,0:T(8,128)S(1)} %get-tuple-element.45), channel_id=1, source_target_pairs={{4,0},{8,4},{12,8},{0,12},{5,1},{9,5},{13,9},{1,13},{6,2},{10,6},{... | collective-permute-start | bytes 786440 | tf_op jit(solution)/shard_map/ppermute | solution.py:254
  16.4 2.2 %copy-start.1 = (f32[4,16,128,128]{3,2,1,0:T(8,128)S(1)}, f32[4,16,128,128]{3,2,1,0:T(8,128)}, u32[]{:S(2)}) copy-start(f32[4,16,128,128]{3,2,1,0:T(8,128)} %refs_6_.3) | copy-start | bytes 12582916
  22.6 42.2 %collective-permute-start.11 = (f32[16,96,128]{2,1,0:T(8,128)S(1)}, f32[16,96,128]{2,1,0:T(8,128)S(1)}, u32[]{:S(2)}, u32[]{:S(2)}) collective-permute-start(f32[16,96,128]{2,1,0:T(8,128)S(1)} %get-tuple-element.48.refs_0_), channel_id=1, source_target_pairs={{16,0},{32,16},{48,32},{0,48},{17,1},{33,17},{49,33},{1,49},{18,2}... | collective-permute-start | bytes 2359304 | tf_op jit(solution)/shard_map/ppermute | solution.py:254
  23.8 41.0 %collective-permute-start.10 = (f32[16,96,128]{2,1,0:T(8,128)S(1)}, f32[16,96,128]{2,1,0:T(8,128)S(1)}, u32[]{:S(2)}, u32[]{:S(2)}) collective-permute-start(f32[16,96,128]{2,1,0:T(8,128)S(1)} %get-tuple-element.55.refs_2_.refs_3_), channel_id=1, source_target_pairs={{0,16},{16,32},{32,48},{48,0},{1,17},{17,33},{33,49},{49,1},{2,18}... | collective-permute-start | bytes 2359304 | tf_op jit(solution)/shard_map/ppermute | solution.py:254
  23.8 28.2 %collective-permute-start.4 = (f32[16,32,128]{2,1,0:T(8,128)S(1)}, f32[16,32,128]{2,1,0:T(8,128)S(1)}, u32[]{:S(2)}, u32[]{:S(2)}) collective-permute-start(f32[16,32,128]{2,1,0:T(8,128)S(1)} %get-tuple-element.49), channel_id=1, source_target_pairs={{0,16},{16,32},{32,48},{48,0},{1,17},{17,33},{33,49},{49,1},{2,18}... | collective-permute-start | bytes 786440 | tf_op jit(solution)/shard_map/ppermute | solution.py:254
  24.3 27.6 %collective-permute-start.5 = (f32[16,32,128]{2,1,0:T(8,128)S(1)}, f32[16,32,128]{2,1,0:T(8,128)S(1)}, u32[]{:S(2)}, u32[]{:S(2)}) collective-permute-start(f32[16,32,128]{2,1,0:T(8,128)S(1)} %get-tuple-element.50), channel_id=1, source_target_pairs={{16,0},{32,16},{48,32},{0,48},{17,1},{33,17},{49,33},{1,49},{18,2}... | collective-permute-start | bytes 786440 | tf_op jit(solution)/shard_map/ppermute | solution.py:254
  25.6 10.6 %collective-permute-start.6 = (f32[4,16,128]{2,1,0:T(8,128)S(1)}, f32[4,16,128]{2,1,0:T(8,128)S(1)}, u32[]{:S(2)}, u32[]{:S(2)}) collective-permute-start(f32[4,16,128]{2,1,0:T(8,128)S(1)} %get-tuple-element.51), channel_id=1, source_target_pairs={{0,3},{1,2},{2,1},{3,0},{4,7},{5,6},{6,5},{7,4},{8,11},{9,10},{10,... | collective-permute-start | bytes 98312 | tf_op jit(solution)/shard_map/ppermute | solution.py:254
  36.1 15.8 %collective-permute-start.7 = (f32[4,16,128]{2,1,0:T(8,128)S(1)}, f32[4,16,128]{2,1,0:T(8,128)S(1)}, u32[]{:S(2)}, u32[]{:S(2)}) collective-permute-start(f32[4,16,128]{2,1,0:T(8,128)S(1)} %get-tuple-element.52), channel_id=1, source_target_pairs={{0,1},{1,0},{2,3},{3,2},{4,5},{5,4},{6,7},{7,6},{8,9},{9,8},{10,11... | collective-permute-start | bytes 98312 | tf_op jit(solution)/shard_map/ppermute | solution.py:254
  52.2 10.3 %copy-start.2 = (f32[4,16,128,128]{3,2,1,0:T(8,128)S(1)}, f32[4,16,128,128]{3,2,1,0:T(8,128)}, u32[]{:S(2)}) copy-start(f32[4,16,128,128]{3,2,1,0:T(8,128)} %refs_6_.3) | copy-start | bytes 12582916
  53.0 9.6 %collective-permute-start.8 = (f32[4,128,128]{2,1,0:T(8,128)S(1)}, f32[4,128,128]{2,1,0:T(8,128)S(1)}, u32[]{:S(2)}, u32[]{:S(2)}) collective-permute-start(f32[4,128,128]{2,1,0:T(8,128)S(1)} %get-tuple-element.58), channel_id=1, source_target_pairs={{0,4},{4,8},{8,12},{12,0},{1,5},{5,9},{9,13},{13,1},{2,6},{6,10},{... | collective-permute-start | bytes 786440 | tf_op jit(solution)/shard_map/ppermute | solution.py:254
  54.5 8.0 %collective-permute-start.9 = (f32[4,128,128]{2,1,0:T(8,128)S(1)}, f32[4,128,128]{2,1,0:T(8,128)S(1)}, u32[]{:S(2)}, u32[]{:S(2)}) collective-permute-start(f32[4,128,128]{2,1,0:T(8,128)S(1)} %get-tuple-element.59), channel_id=1, source_target_pairs={{4,0},{8,4},{12,8},{0,12},{5,1},{9,5},{13,9},{1,13},{6,2},{10,6},{... | collective-permute-start | bytes 786440 | tf_op jit(solution)/shard_map/ppermute | solution.py:254
  56.3 16.2 %collective-permute-start.13 = (f32[16,32,128]{2,1,0:T(8,128)S(1)}, f32[16,32,128]{2,1,0:T(8,128)S(1)}, u32[]{:S(2)}, u32[]{:S(2)}) collective-permute-start(f32[16,32,128]{2,1,0:T(8,128)S(1)} %get-tuple-element.53.refs_1_), channel_id=1, source_target_pairs={{16,0},{32,16},{48,32},{0,48},{17,1},{33,17},{49,33},{1,49},{18,2}... | collective-permute-start | bytes 786440 | tf_op jit(solution)/shard_map/ppermute | solution.py:254
  62.5 12.9 %collective-permute-start.12 = (f32[16,32,128]{2,1,0:T(8,128)S(1)}, f32[16,32,128]{2,1,0:T(8,128)S(1)}, u32[]{:S(2)}, u32[]{:S(2)}) collective-permute-start(f32[16,32,128]{2,1,0:T(8,128)S(1)} %get-tuple-element.56.refs_3_.refs_4_), channel_id=1, source_target_pairs={{0,16},{16,32},{32,48},{48,0},{1,17},{17,33},{33,49},{49,1},{2,18}... | collective-permute-start | bytes 786440 | tf_op jit(solution)/shard_map/ppermute | solution.py:254
  65.1 48.3 %collective-permute-start.19 = (f32[16,96,128]{2,1,0:T(8,128)S(1)}, f32[16,96,128]{2,1,0:T(8,128)S(1)}, u32[]{:S(2)}, u32[]{:S(2)}) collective-permute-start(f32[16,96,128]{2,1,0:T(8,128)S(1)} %get-tuple-element.62.refs_0_), channel_id=1, source_target_pairs={{16,0},{32,16},{48,32},{0,48},{17,1},{33,17},{49,33},{1,49},{18,2}... | collective-permute-start | bytes 2359304 | tf_op jit(solution)/shard_map/ppermute | solution.py:254
  67.1 46.3 %collective-permute-start.18 = (f32[16,96,128]{2,1,0:T(8,128)S(1)}, f32[16,96,128]{2,1,0:T(8,128)S(1)}, u32[]{:S(2)}, u32[]{:S(2)}) collective-permute-start(f32[16,96,128]{2,1,0:T(8,128)S(1)} %get-tuple-element.67.refs_2_.refs_3_), channel_id=1, source_target_pairs={{0,16},{16,32},{32,48},{48,0},{1,17},{17,33},{33,49},{49,1},{2,18}... | collective-permute-start | bytes 2359304 | tf_op jit(solution)/shard_map/ppermute | solution.py:254
  67.1 10.3 %collective-permute-start.14 = (f32[4,16,128]{2,1,0:T(8,128)S(1)}, f32[4,16,128]{2,1,0:T(8,128)S(1)}, u32[]{:S(2)}, u32[]{:S(2)}) collective-permute-start(f32[4,16,128]{2,1,0:T(8,128)S(1)} %get-tuple-element.63), channel_id=1, source_target_pairs={{0,3},{1,2},{2,1},{3,0},{4,7},{5,6},{6,5},{7,4},{8,11},{9,10},{10,... | collective-permute-start | bytes 98312 | tf_op jit(solution)/shard_map/ppermute | solution.py:254
  72.5 14.6 %collective-permute-start.15 = (f32[4,16,128]{2,1,0:T(8,128)S(1)}, f32[4,16,128]{2,1,0:T(8,128)S(1)}, u32[]{:S(2)}, u32[]{:S(2)}) collective-permute-start(f32[4,16,128]{2,1,0:T(8,128)S(1)} %get-tuple-element.64), channel_id=1, source_target_pairs={{0,1},{1,0},{2,3},{3,2},{4,5},{5,4},{6,7},{7,6},{8,9},{9,8},{10,11... | collective-permute-start | bytes 98312 | tf_op jit(solution)/shard_map/ppermute | solution.py:254
  88.1 13.7 %collective-permute-start.16 = (f32[4,128,128]{2,1,0:T(8,128)S(1)}, f32[4,128,128]{2,1,0:T(8,128)S(1)}, u32[]{:S(2)}, u32[]{:S(2)}) collective-permute-start(f32[4,128,128]{2,1,0:T(8,128)S(1)} %get-tuple-element.70), channel_id=1, source_target_pairs={{0,4},{4,8},{8,12},{12,0},{1,5},{5,9},{9,13},{13,1},{2,6},{6,10},{... | collective-permute-start | bytes 786440 | tf_op jit(solution)/shard_map/ppermute | solution.py:254
  88.4 13.8 %collective-permute-start.17 = (f32[4,128,128]{2,1,0:T(8,128)S(1)}, f32[4,128,128]{2,1,0:T(8,128)S(1)}, u32[]{:S(2)}, u32[]{:S(2)}) collective-permute-start(f32[4,128,128]{2,1,0:T(8,128)S(1)} %get-tuple-element.71), channel_id=1, source_target_pairs={{4,0},{8,4},{12,8},{0,12},{5,1},{9,5},{13,9},{1,13},{6,2},{10,6},{... | collective-permute-start | bytes 786440 | tf_op jit(solution)/shard_map/ppermute | solution.py:254
  91.4 10.4 %collective-permute-start.22 = (f32[4,16,128]{2,1,0:T(8,128)S(1)}, f32[4,16,128]{2,1,0:T(8,128)S(1)}, u32[]{:S(2)}, u32[]{:S(2)}) collective-permute-start(f32[4,16,128]{2,1,0:T(8,128)S(1)} %get-tuple-element.76), channel_id=1, source_target_pairs={{0,3},{1,2},{2,1},{3,0},{4,7},{5,6},{6,5},{7,4},{8,11},{9,10},{10,... | collective-permute-start | bytes 98312 | tf_op jit(solution)/shard_map/ppermute | solution.py:254
  101.8 12.4 %collective-permute-start.21 = (f32[16,32,128]{2,1,0:T(8,128)S(1)}, f32[16,32,128]{2,1,0:T(8,128)S(1)}, u32[]{:S(2)}, u32[]{:S(2)}) collective-permute-start(f32[16,32,128]{2,1,0:T(8,128)S(1)} %get-tuple-element.65.refs_1_), channel_id=1, source_target_pairs={{16,0},{32,16},{48,32},{0,48},{17,1},{33,17},{49,33},{1,49},{18,2}... | collective-permute-start | bytes 786440 | tf_op jit(solution)/shard_map/ppermute | solution.py:254
  101.8 12.4 %collective-permute-start.20 = (f32[16,32,128]{2,1,0:T(8,128)S(1)}, f32[16,32,128]{2,1,0:T(8,128)S(1)}, u32[]{:S(2)}, u32[]{:S(2)}) collective-permute-start(f32[16,32,128]{2,1,0:T(8,128)S(1)} %get-tuple-element.68.refs_3_.refs_4_), channel_id=1, source_target_pairs={{0,16},{16,32},{32,48},{48,0},{1,17},{17,33},{33,49},{49,1},{2,18}... | collective-permute-start | bytes 786440 | tf_op jit(solution)/shard_map/ppermute | solution.py:254
  102.3 9.4 %collective-permute-start.23 = (f32[4,16,128]{2,1,0:T(8,128)S(1)}, f32[4,16,128]{2,1,0:T(8,128)S(1)}, u32[]{:S(2)}, u32[]{:S(2)}) collective-permute-start(f32[4,16,128]{2,1,0:T(8,128)S(1)} %get-tuple-element.77), channel_id=1, source_target_pairs={{0,1},{1,0},{2,3},{3,2},{4,5},{5,4},{6,7},{7,6},{8,9},{9,8},{10,11... | collective-permute-start | bytes 98312 | tf_op jit(solution)/shard_map/ppermute | solution.py:254
  112.0 5.5 %collective-permute-start.25 = (f32[2,2,16,128]{3,2,1,0:T(8,128)S(1)}, f32[2,2,16,128]{3,2,1,0:T(8,128)S(1)}, u32[]{:S(2)}, u32[]{:S(2)}) collective-permute-start(f32[2,2,16,128]{3,2,1,0:T(8,128)S(1)} %get-tuple-element.85), channel_id=1, source_target_pairs={{0,1},{1,0},{2,3},{3,2},{4,5},{5,4},{6,7},{7,6},{8,9},{9,8},{10,11... | collective-permute-start | bytes 98312 | tf_op jit(solution)/shard_map/ppermute | solution.py:254
  114.5 5.5 %collective-permute-start.24 = (f32[2,2,16,128]{3,2,1,0:T(8,128)S(1)}, f32[2,2,16,128]{3,2,1,0:T(8,128)S(1)}, u32[]{:S(2)}, u32[]{:S(2)}) collective-permute-start(f32[2,2,16,128]{3,2,1,0:T(8,128)S(1)} %get-tuple-element.84), channel_id=1, source_target_pairs={{0,1},{1,0},{2,3},{3,2},{4,5},{5,4},{6,7},{7,6},{8,9},{9,8},{10,11... | collective-permute-start | bytes 98312 | tf_op jit(solution)/shard_map/ppermute | solution.py:254
  120.1 9.1 %collective-permute-start.26 = (f32[2,4,16,128]{3,2,1,0:T(8,128)S(1)}, f32[2,4,16,128]{3,2,1,0:T(8,128)S(1)}, u32[]{:S(2)}, u32[]{:S(2)}) collective-permute-start(f32[2,4,16,128]{3,2,1,0:T(8,128)S(1)} %fusion.refs_5_), channel_id=1, source_target_pairs={{0,2},{1,3},{2,0},{3,1},{4,6},{5,7},{6,4},{7,5},{8,10},{9,11},{10,... | collective-permute-start | bytes 196616 | tf_op jit(solution)/shard_map/ppermute | solution.py:254
